TPU v7x, 1024 devices: a whole 8x8x8 slice. The times are simulated.
1024 devices in a mesh: ab: 32 (over z_lo, x, core), kl: 4 (over z_hi), ij: 8 (over y).
Axes of the slice: x: 8, y: 8, z: 8 (z_hi: 4, z_lo: 2; z = z_hi * 2 + z_lo), core: 2. Of those that a mesh axis runs over, the one named last changes fastest.
Arguments:
- amplitudes: bfloat16 [16384, 8192], P('ab', ('kl', 'ij')), may hold values from -6 to 6
- integrals: bfloat16 [8192, 8192], P(('kl', 'ab'), 'ij'), may hold values from -0.0625 to 0.0625
Outputs:
- ladder: float32 [16384, 8192], P('ab', ('ij', 'kl'))
All inputs are finite; a program needn't handle non-finite values.
Results may differ from a plain program's by a relative error of at most 0.0003.
Values may be sent and summed in bfloat16 or wider, within the bound.
No kernel may reach another device: no remote copies, remote signals or barrier semaphores. Data moves between devices by JAX's collectives and lax.ppermute only.
A program may use at most 32 MiB of HBM per device.

v0:
```python
import jax
import jax.numpy as jnp
from jax import lax
from jax.sharding import PartitionSpec as P

PAIRS = 8128


def laid_out(tiles, dim):
    tiles = jnp.moveaxis(tiles, 0, dim)
    shape = tiles.shape
    return tiles.reshape(*shape[:dim], shape[dim] * shape[dim + 1], *shape[dim + 2 :])


def sent_to_all(shard, axis):
    size = lax.axis_size(axis)
    return lax.all_to_all(
        jnp.broadcast_to(shard[None], (size, *shard.shape)), axis, 0, 0, tiled=True
    )


def gather_directly(shard, axis, dim):
    return laid_out(sent_to_all(shard, axis), dim)


def per_device(amplitudes, integrals):
    kl_index = lax.axis_index("kl")
    ij_index = lax.axis_index("ij")
    blocked = gather_directly(amplitudes, "ij", 1)
    col_count = blocked.shape[1]
    col_ids = kl_index * col_count + jnp.arange(col_count)
    masked = jnp.where((col_ids < PAIRS)[None, :], blocked, jnp.zeros((), jnp.bfloat16))
    partial_terms = jnp.dot(
        masked,
        lax.all_gather(integrals, "ab", axis=0, tiled=True),
        preferred_element_type=jnp.float32,
    )
    owned = lax.psum_scatter(partial_terms, "kl", scatter_dimension=1, tiled=True)
    out_width = owned.shape[1]
    out_ids = ij_index * integrals.shape[1] + kl_index * out_width + jnp.arange(out_width)
    return jnp.where((out_ids < PAIRS)[None, :], owned, jnp.float32(0.0))


def solution(mesh):
    in_specs = (P("ab", ("kl", "ij")), P(("kl", "ab"), "ij"))
    out_specs = P("ab", ("ij", "kl"))
    return jax.shard_map(
        per_device, mesh=mesh, in_specs=in_specs, out_specs=out_specs, check_vma=False
    )
```

profile of v0, /device:TPU:1, one launch (start us, length us, event | category | flops | bytes accessed | tf_op | source)
XLA Modules:
  0.0 166.0 jit_solution(5296900706452763785)
XLA Ops:
  6.5 0.0 all-gather.2.cloned.1.call-start
  6.5 0.7 all-gather.2.cloned.1.call-update
  7.3 2.4 %broadcast_in_dim.34 = bf16[8,512,256]{2,1,0:T(8,128)(2,1)} broadcast(bf16[512,256]{1,0:T(8,128)(2,1)} %param.2), dimensions={1,2} | broadcast | bytes 2359296 | tf_op jit(solution)/shard_map/broadcast_in_dim | solution.py:18
  9.7 8.1 %all-to-all-start = ((bf16[8,512,256]{2,1,0:T(8,128)(2,1)}), bf16[8,512,256]{2,1,0:T(8,128)(2,1)S(1)}, u32[]{:S(2)}, u32[]{:S(2)}) async-start(bf16[8,512,256]{2,1,0:T(8,128)(2,1)} %broadcast_in_dim.34), calls=%async_computation | async-start | bytes 4194304 | tf_op jit(solution)/shard_map/all_to_all | solution.py:17
  17.8 0.0 reduce-scatter.2.cloned.1.call-start
  17.8 44.4 %all-to-all-done = bf16[8,512,256]{2,1,0:T(8,128)(2,1)S(1)} async-done(((bf16[8,512,256]{2,1,0:T(8,128)(2,1)}), bf16[8,512,256]{2,1,0:T(8,128)(2,1)S(1)}, u32[]{:S(2)}, u32[]{:S(2)}) %all-to-all-start) | async-done | bytes 2097184 | tf_op jit(solution)/shard_map/all_to_all | solution.py:17
  62.3 2.4 %copy.3 = bf16[8,512,256]{1,2,0:T(8,128)(2,1)} copy(bf16[8,512,256]{2,1,0:T(8,128)(2,1)S(1)} %all-to-all-done) | data formatting | bytes 4194304 | tf_op jit(solution)/shard_map/all_to_all | solution.py:17
  64.6 1.8 %bitcast_select_fusion = bf16[512,2048]{0,1:T(8,128)(2,1)S(1)} fusion(bf16[8,512,256]{1,2,0:T(8,128)(2,1)} %copy.3, pred[2048]{0:T(1024)(128)(4,1)S(1)} %add_compare_fusion), kind=kLoop, calls=%fused_computation | loop fusion | flops 1048576 | bytes 4196352 | tf_op jit(solution)/shard_map/jit(_where)/select_n | solution.py:32
  66.4 28.1 %all-gather.2.cloned.1.call-done = bf16[2048,1024]{1,0:T(8,128)(2,1)} async-done(((bf16[64,1024]{1,0:T(8,128)(2,1)}), bf16[2048,1024]{1,0:T(8,128)(2,1)}) %all-gather.2.cloned.1.call-update) | async-done | bytes 4194320 | tf_op jit(solution)/shard_map/all_gather | solution.py:35
  94.5 5.9 %fusion = f32[512,1024]{1,0:T(8,128)} fusion(bf16[512,2048]{0,1:T(8,128)(2,1)S(1)} %bitcast_select_fusion, bf16[2048,1024]{1,0:T(8,128)(2,1)} %all-gather.2.cloned.1.call-done), kind=kOutput, calls=%fused_computation.4 | convolution fusion | flops 2147483648 | bytes 8388608 | tf_op jit(solution)/shard_map/dot_general | solution.py:33
  100.3 0.0 reduce-scatter.2.cloned.1.call-update
  100.4 56.9 %reduce-scatter.2.cloned.1.call-done = f32[512,256]{1,0:T(8,128)} async-done(((f32[512,1024]{1,0:T(8,128)}), f32[512,256]{1,0:T(8,128)}) %reduce-scatter.2.cloned.1.call-update) | async-done | bytes 524304 | tf_op jit(solution)/shard_map/reduce_scatter | solution.py:38
  157.3 1.9 %broadcast_select_fusion = f32[512,256]{1,0:T(8,128)} fusion(f32[512,256]{1,0:T(8,128)} %reduce-scatter.2.cloned.1.call-done, pred[256]{0:T(512)(128)(4,1)S(1)} %add_compare_fusion.1), kind=kLoop, calls=%fused_computation.1 | loop fusion | flops 131072 | bytes 1048832 | tf_op jit(solution)/shard_map/jit(_where)/select_n | solution.py:41
  (2 shorter events, 0.0 us)
Async XLA Ops:
  6.5 87.9 %all-gather.2.cloned.1.call-start = ((), (), s32[]{:S(2)}) async-start(), calls=%async_computation.2 | async-start | bytes 4325376 | tf_op jit(solution)/shard_map/all_gather | solution.py:35
  9.7 52.6 %all-to-all-start = ((bf16[8,512,256]{2,1,0:T(8,128)(2,1)}), bf16[8,512,256]{2,1,0:T(8,128)(2,1)S(1)}, u32[]{:S(2)}, u32[]{:S(2)}) async-start(bf16[8,512,256]{2,1,0:T(8,128)(2,1)} %broadcast_in_dim.34), calls=%async_computation | async-start | bytes 4194304 | tf_op jit(solution)/shard_map/all_to_all | solution.py:17
  17.8 139.5 %reduce-scatter.2.cloned.1.call-start = ((), (), s32[]{:S(2)}) async-start(), calls=%async_computation.3 | async-start | bytes 2621440 | tf_op jit(solution)/shard_map/reduce_scatter | solution.py:38
Sparse Core Ops, SparseCore 0:
  10.1 84.3 all-gather.1
  100.5 56.7 reduce-scatter.1
where the time goes:
time: 166 us
  waiting for transfers between devices  130 us (78%)
  between operations  13.4 us (8%)
  starting transfers between devices  8.13 us (5%)
  matrix products  5.85 us (4%)
  local copies, waits for them, and re-layouts  4.77 us (3%)
  other arithmetic  3.66 us (2%)
    reduce_scatter x1, waiting for transfers between devices, per_device(): lax.psum_scatter(partial_terms, 'kl', scatter_dimension=1, tiled=True)  56.9 us
    all_to_all x1, waiting for transfers between devices, sent_to_all(): lax.all_to_all(jnp.broadcast_to(shard[None], (size, *shard.shape)), axis,...  44.4 us
    all_gather x1, waiting for transfers between devices, per_device(): lax.all_gather(integrals, 'ab', axis=0, tiled=True)  28.1 us
    all_to_all x1, starting transfers between devices, sent_to_all(): lax.all_to_all(jnp.broadcast_to(shard[None], (size, *shard.shape)), axis,...  8.09 us
    dot_general x1, matrix products, per_device(): jnp.dot(masked, lax.all_gather(integrals, 'ab', axis=0, tiled=True), pref...  5.85 us
  transfers between devices with their start and end apart: 3, of which 3 were waited for; matrix products, arithmetic and copies ran while one was open for 4% of the time, Pallas kernels for 0%

commit v1 on v0

v1 whole, which is shorter than its diff:
```python
import jax
import jax.numpy as jnp
from jax import lax
from jax.experimental import pallas as pl
from jax.experimental.pallas import tpu as pltpu
from jax.sharding import Mesh
from jax.sharding import PartitionSpec as P

PAIRS = 8128
AXES = ("zl", "x", "c", "kl", "ij")
SCALE = 64.0
HALVES = 2

Y_PARITY = [list(range(p, 8, 2)) for p in range(2)]
X_PARITY = [[zl * 8 + x for zl in range(2) for x in range(p, 8, 2)] for p in range(2)]
Y_HOP = [(c * 8 + y, c * 8 + (y + 1 - 2 * c) % 8) for c in range(2) for y in range(8)]
X_HOP = [(x * 2 + c, (x + 1 - 2 * c) % 8 * 2 + c) for c in range(2) for x in range(8)]
SWAP = [(0, 1), (1, 0)]


def to_all(shard, axes, groups, size):
    return lax.all_to_all(
        jnp.broadcast_to(shard[None], (size, *shard.shape)),
        axes, 0, 0, tiled=True, axis_index_groups=groups,
    )


def product_kernel(a_own, a_oth, v00, v10, v01, v11, out, a_all, v_all):
    px = lax.axis_index("x") % 2
    py = lax.axis_index("ij") % 2
    c = lax.axis_index("c")
    for u, ref in enumerate((a_own, a_oth)):
        for j in range(4):
            start = pl.multiple_of((2 * j + (py + u) % 2) * 256, 256)
            a_all[:, pl.ds(start, 256)] = ref[j]
    for s, t, ref in ((0, 0, v00), (1, 0, v10), (0, 1, v01), (1, 1, v11)):
        offset = ((px + s) % 2) * 128 + ((c + t) % 2) * 64
        for y in range(8):
            start = pl.multiple_of(offset + y * 256, 64)
            v_all[pl.ds(start, 64), :] = ref[y]

    @pl.when(lax.axis_index("kl") == 3)
    def _():
        v_all[pl.ds(1984, 64), :] = jnp.zeros((64, v_all.shape[1]), jnp.bfloat16)

    width = out.shape[2]
    for k in range(4):
        prod = jnp.dot(
            a_all[...], v_all[:, k * width : (k + 1) * width],
            preferred_element_type=jnp.float32,
        )
        out[k] = prod * SCALE


def product(a_own, a_oth, v00, v10, v01, v11):
    n = v00.shape[2]
    return pl.pallas_call(
        product_kernel,
        out_shape=jax.ShapeDtypeStruct((4, 512, n // 4), jnp.float32),
        in_specs=[pl.BlockSpec(memory_space=pltpu.VMEM)] * 6,
        out_specs=pl.BlockSpec(memory_space=pltpu.VMEM),
        scratch_shapes=[
            pltpu.VMEM((512, 2048), jnp.bfloat16),
            pltpu.VMEM((2048, n), jnp.bfloat16),
        ],
        cost_estimate=pl.CostEstimate(
            flops=2 * 512 * 2048 * n, bytes_accessed=4 << 20, transcendentals=0
        ),
    )(a_own, a_oth, v00, v10, v01, v11)


def staged(amplitudes, integrals):
    width = 256 // HALVES
    a_own = to_all(amplitudes, "ij", Y_PARITY, 4)
    a_oth = lax.ppermute(a_own, ("c", "ij"), Y_HOP)
    columns = integrals.reshape(64, 4, HALVES, width)
    owned = []
    for h in range(HALVES):
        part = columns[:, :, h, :].reshape(64, 4 * width)
        v00 = to_all(part, ("zl", "x"), X_PARITY, 8)
        v10 = lax.ppermute(v00, ("x", "c"), X_HOP)
        v01 = lax.ppermute(v00, "c", SWAP)
        v11 = lax.ppermute(v10, "c", SWAP)
        terms = product(a_own, a_oth, v00, v10, v01, v11).astype(jnp.float16)
        got = lax.all_to_all(terms, "kl", 0, 0, tiled=True).astype(jnp.float32)
        owned.append(((got[0] + got[1]) + (got[2] + got[3])) * (1.0 / SCALE))
    owned = jnp.concatenate(owned, axis=1)
    out_ids = lax.axis_index("ij") * 1024 + lax.axis_index("kl") * 256 + jnp.arange(256)
    return jnp.where((out_ids < PAIRS)[None, :], owned, jnp.float32(0.0))


def solution(mesh):
    fine = Mesh(mesh.devices.reshape(2, 8, 2, 4, 8), AXES)
    ab = ("zl", "x", "c")
    return jax.shard_map(
        staged, mesh=fine,
        in_specs=(P(ab, ("kl", "ij")), P(("kl", *ab), "ij")),
        out_specs=P(ab, ("ij", "kl")), check_vma=False,
    )
```

time: 166 us -> 159 us (0.958)
  the two profiles are of different devices: /device:TPU:1 before, /device:TPU:148 now
where the time goes in v1:
time: 159 us; the launch traced here: 158 us
  starting transfers between devices  60.5 us (38%)
  waiting for transfers between devices  52 us (33%)
  blocking collectives  23.1 us (15%)
  Pallas kernels  11.8 us (7%)
  local copies, waits for them, and re-layouts  5.62 us (4%)
  other arithmetic  5.26 us (3%)
    all_to_all x2, starting transfers between devices, staged(): got = lax.all_to_all(terms, 'kl', 0, 0, tiled=True).astype(jnp.float32)  31.6 us
    all_to_all x2, waiting for transfers between devices, to_all(): lax.all_to_all(jnp.broadcast_to(shard[None], (size, *shard.shape)), axes,...  26.4 us
    all_to_all x1, blocking collectives, to_all(): lax.all_to_all(jnp.broadcast_to(shard[None], (size, *shard.shape)), axes,...  23.1 us
    all_to_all x2, waiting for transfers between devices, staged(): got = lax.all_to_all(terms, 'kl', 0, 0, tiled=True).astype(jnp.float32)  17 us
    all_to_all x2, starting transfers between devices, to_all(): lax.all_to_all(jnp.broadcast_to(shard[None], (size, *shard.shape)), axes,...  11.9 us
    pallas_call x2, Pallas kernels, product(): pl.pallas_call(product_kernel, out_shape=jax.ShapeDtypeStruct((4, 512, n...  11.8 us
    ppermute x2, waiting for transfers between devices, staged(): v10 = lax.ppermute(v00, ('x', 'c'), X_HOP)  5.49 us
    ppermute x1, starting transfers between devices, staged(): a_oth = lax.ppermute(a_own, ('c', 'ij'), Y_HOP)  4.64 us
  transfers between devices with their start and end apart: 11, of which 5 were waited for; matrix products, arithmetic and copies ran while one was open for 3% of the time, Pallas kernels for 7%

profile of v1, /device:TPU:148, one launch (start us, length us, event | category | flops | bytes accessed | tf_op | source)
XLA Modules:
  0.0 158.4 jit_solution(3557249119831623447)
XLA Ops:
  0.0 1.0 reshape.21
  1.0 0.7 slice_reduce_fusion.1
  1.8 0.0 copy-start.6
  1.8 23.1 %all_to_all.25.v00 = bf16[8,64,512]{2,1,0:T(8,128)(2,1)S(1)} all-to-all(bf16[8,64,512]{2,1,0:T(8,128)(2,1)S(1)} %broadcast_in_dim.36), channel_id=1, replica_groups={{0,128,256,384,512,640,768,896},{64,192,320,448,576,704,832,960},{1,129..., dimensions={0} | all-to-all | bytes 1048576 | tf_op jit(solution)/shard_map/all_to_all | solution.py:22
  24.9 0.0 copy-done.6
  24.9 0.0 copy-start.3
  24.9 1.1 broadcast_in_dim.34
  26.0 6.6 %all-to-all-start = ((bf16[4,512,256]{2,1,0:T(8,128)(2,1)}), bf16[4,512,256]{2,1,0:T(8,128)(2,1)S(1)}, u32[]{:S(2)}, u32[]{:S(2)}) async-start(bf16[4,512,256]{2,1,0:T(8,128)(2,1)} %broadcast_in_dim.34), calls=%async_computation | async-start | bytes 2097152 | tf_op jit(solution)/shard_map/all_to_all | solution.py:22
  32.7 26.4 %all-to-all-done.a_own = bf16[4,512,256]{2,1,0:T(8,128)(2,1)S(1)} async-done(((bf16[4,512,256]{2,1,0:T(8,128)(2,1)}), bf16[4,512,256]{2,1,0:T(8,128)(2,1)S(1)}, u32[]{:S(2)}, u32[]{:S(2)}) %all-to-all-start) | async-done | bytes 1048608 | tf_op jit(solution)/shard_map/all_to_all | solution.py:22
  59.2 0.0 copy-start
  59.2 0.9 broadcast_in_dim.38
  60.1 5.2 %all-to-all-start.3 = ((bf16[8,64,512]{2,1,0:T(8,128)(2,1)}), bf16[8,64,512]{2,1,0:T(8,128)(2,1)S(1)}, u32[]{:S(2)}, u32[]{:S(2)}) async-start(bf16[8,64,512]{2,1,0:T(8,128)(2,1)} %broadcast_in_dim.38), calls=%async_computation.3 | async-start | bytes 1048576 | tf_op jit(solution)/shard_map/all_to_all | solution.py:22
  65.3 1.9 %collective-permute-start.1 = (bf16[8,64,512]{2,1,0:T(8,128)(2,1)S(1)}, bf16[8,64,512]{2,1,0:T(8,128)(2,1)}, u32[]{:S(2)}, u32[]{:S(2)}) collective-permute-start(bf16[8,64,512]{2,1,0:T(8,128)(2,1)S(1)} %all_to_all.25.v00), channel_id=1, source_target_pairs={{0,64},{64,128},{128,192},{192,256},{256,320},{320,384},{384,448},... | collective-permute-start | bytes 1572872 | tf_op jit(solution)/shard_map/ppermute | solution.py:81
  67.2 4.6 %collective-permute-start = (bf16[4,512,256]{2,1,0:T(8,128)(2,1)S(1)}, bf16[4,512,256]{2,1,0:T(8,128)(2,1)S(1)}, u32[]{:S(2)}, u32[]{:S(2)}) collective-permute-start(bf16[4,512,256]{2,1,0:T(8,128)(2,1)S(1)} %all-to-all-done.a_own), channel_id=1, source_target_pairs={{0,1},{1,2},{2,3},{3,4},{4,5},{5,6},{6,7},{7,0},{32,39},{33,32},{3... | collective-permute-start | bytes 3145736 | tf_op jit(solution)/shard_map/ppermute | solution.py:75
  71.9 0.0 copy-done.3
  71.9 1.9 %collective-permute-start.2 = (bf16[8,64,512]{2,1,0:T(8,128)(2,1)S(1)}, bf16[8,64,512]{2,1,0:T(8,128)(2,1)}, u32[]{:S(2)}, u32[]{:S(2)}) collective-permute-start(bf16[8,64,512]{2,1,0:T(8,128)(2,1)S(1)} %all_to_all.25.v00), channel_id=1, source_target_pairs={{0,32},{32,0},{1,33},{33,1},{2,34},{34,2},{3,35},{35,3},{4,36},{36... | collective-permute-start | bytes 1572872 | tf_op jit(solution)/shard_map/ppermute | solution.py:82
  73.8 5.5 %collective-permute-done.1.v10 = bf16[8,64,512]{2,1,0:T(8,128)(2,1)} collective-permute-done((bf16[8,64,512]{2,1,0:T(8,128)(2,1)S(1)}, bf16[8,64,512]{2,1,0:T(8,128)(2,1)}, u32[]{:S(2)}, u32[]{:S(2)}) %collective-permute-start.1) | collective-permute-done | bytes 524320 | tf_op jit(solution)/shard_map/ppermute | solution.py:81
  79.3 1.9 %collective-permute-start.3 = (bf16[8,64,512]{2,1,0:T(8,128)(2,1)}, bf16[8,64,512]{2,1,0:T(8,128)(2,1)}, u32[]{:S(2)}, u32[]{:S(2)}) collective-permute-start(bf16[8,64,512]{2,1,0:T(8,128)(2,1)} %collective-permute-done.1.v10), channel_id=1, source_target_pairs={{0,32},{32,0},{1,33},{33,1},{2,34},{34,2},{3,35},{35,3},{4,36},{36... | collective-permute-start | bytes 1572872 | tf_op jit(solution)/shard_map/ppermute | solution.py:83
  81.2 0.0 all-to-all-done.3.v00
  81.2 0.0 copy-start.2
  81.2 2.3 %collective-permute-start.4 = (bf16[8,64,512]{2,1,0:T(8,128)(2,1)S(1)}, bf16[8,64,512]{2,1,0:T(8,128)(2,1)}, u32[]{:S(2)}, u32[]{:S(2)}) collective-permute-start(bf16[8,64,512]{2,1,0:T(8,128)(2,1)S(1)} %all-to-all-done.3.v00), channel_id=1, source_target_pairs={{0,64},{64,128},{128,192},{192,256},{256,320},{320,384},{384,448},... | collective-permute-start | bytes 1572872 | tf_op jit(solution)/shard_map/ppermute | solution.py:81
  83.5 0.0 collective-permute-done.2.v01
  83.5 0.0 collective-permute-done.3.v11
  83.5 1.4 collective-permute-done.a_oth
  84.9 0.0 copy-done
  84.9 1.0 copy-done.1
  85.9 5.9 %shard_map.28 = f32[4,512,128]{2,1,0:T(8,128)} custom-call(bf16[4,512,256]{2,1,0:T(8,128)(2,1)} %copy-done, bf16[4,512,256]{2,1,0:T(8,128)(2,1)} %copy-done.1, bf16[8,64,512]{2,1,0:T(8,128)(2,1)} %copy-done.3, bf16[8,64,512]{2,1,0:T(8,128)(2,1)} %collective-permute-done.1.v10, bf16[8,64,512]{2,1,0:T(8,128)(2,1)} %collective-permute-done.2.v01, ...), custom_call_target="tpu_custom_call" | custom-call | flops 1073741824 | bytes 4194304 | tf_op jit(solution)/shard_map/pallas_call | solution.py:57
  91.8 2.1 %convert_element_type.12 = f16[4,512,128]{2,1,0:T(8,128)(2,1)} convert(f32[4,512,128]{2,1,0:T(8,128)} %shard_map.28) | non-fusion elementwise | flops 262144 | bytes 1572864 | tf_op jit(solution)/shard_map/convert_element_type | solution.py:84
  93.9 24.4 %all-to-all-start.2 = ((f16[4,512,128]{2,1,0:T(8,128)(2,1)}), f16[4,512,128]{2,1,0:T(8,128)(2,1)S(1)}, u32[]{:S(2)}, u32[]{:S(2)}) async-start(f16[4,512,128]{2,1,0:T(8,128)(2,1)} %convert_element_type.12), calls=%async_computation.2 | async-start | bytes 1048576 | tf_op jit(solution)/shard_map/all_to_all | solution.py:85
  118.3 0.0 copy-done.2
  118.3 1.9 %collective-permute-start.5 = (bf16[8,64,512]{2,1,0:T(8,128)(2,1)S(1)}, bf16[8,64,512]{2,1,0:T(8,128)(2,1)S(1)}, u32[]{:S(2)}, u32[]{:S(2)}) collective-permute-start(bf16[8,64,512]{2,1,0:T(8,128)(2,1)S(1)} %all-to-all-done.3.v00), channel_id=1, source_target_pairs={{0,32},{32,0},{1,33},{33,1},{2,34},{34,2},{3,35},{35,3},{4,36},{36... | collective-permute-start | bytes 1572872 | tf_op jit(solution)/shard_map/ppermute | solution.py:82
  120.2 0.0 collective-permute-done.4.v10
  120.2 2.4 %collective-permute-start.6 = (bf16[8,64,512]{2,1,0:T(8,128)(2,1)}, bf16[8,64,512]{2,1,0:T(8,128)(2,1)S(1)}, u32[]{:S(2)}, u32[]{:S(2)}) collective-permute-start(bf16[8,64,512]{2,1,0:T(8,128)(2,1)} %collective-permute-done.4.v10), channel_id=1, source_target_pairs={{0,32},{32,0},{1,33},{33,1},{2,34},{34,2},{3,35},{35,3},{4,36},{36... | collective-permute-start | bytes 1572872 | tf_op jit(solution)/shard_map/ppermute | solution.py:83
  122.6 0.0 collective-permute-done.5.v01
  122.6 0.0 copy-start.4
  122.7 1.7 %collective-permute-done.6.v11 = bf16[8,64,512]{2,1,0:T(8,128)(2,1)S(1)} collective-permute-done((bf16[8,64,512]{2,1,0:T(8,128)(2,1)}, bf16[8,64,512]{2,1,0:T(8,128)(2,1)S(1)}, u32[]{:S(2)}, u32[]{:S(2)}) %collective-permute-start.6) | collective-permute-done | bytes 524320 | tf_op jit(solution)/shard_map/ppermute | solution.py:83
  124.4 0.0 copy-done.4
  124.4 0.8 copy-done.5
  125.2 5.9 %shard_map.29 = f32[4,512,128]{2,1,0:T(8,128)} custom-call(bf16[4,512,256]{2,1,0:T(8,128)(2,1)} %copy-done, bf16[4,512,256]{2,1,0:T(8,128)(2,1)} %copy-done.1, bf16[8,64,512]{2,1,0:T(8,128)(2,1)} %copy-done.2, bf16[8,64,512]{2,1,0:T(8,128)(2,1)} %collective-permute-done.4.v10, bf16[8,64,512]{2,1,0:T(8,128)(2,1)} %copy-done.4, bf16[8,64,512]{2,1,0:T(8,128)(2,1)} %copy-done.5), custom_call_target="tpu_custom_call" | custom-call | flops 1073741824 | bytes 4194304 | tf_op jit(solution)/shard_map/pallas_call | solution.py:57
  131.1 2.1 %convert_element_type.14 = f16[4,512,128]{2,1,0:T(8,128)(2,1)} convert(f32[4,512,128]{2,1,0:T(8,128)} %shard_map.29) | non-fusion elementwise | flops 262144 | bytes 1572864 | tf_op jit(solution)/shard_map/convert_element_type | solution.py:84
  133.2 0.0 all-to-all-done.2
  133.2 7.2 %all-to-all-start.4 = ((f16[4,512,128]{2,1,0:T(8,128)(2,1)}), f16[4,512,128]{2,1,0:T(8,128)(2,1)S(1)}, u32[]{:S(2)}, u32[]{:S(2)}) async-start(f16[4,512,128]{2,1,0:T(8,128)(2,1)} %convert_element_type.14), calls=%async_computation.4 | async-start | bytes 1048576 | tf_op jit(solution)/shard_map/all_to_all | solution.py:85
  140.4 0.1 convert_element_type.13
  140.4 0.1 fusion.5
  140.5 17.0 %all-to-all-done.4 = f16[4,512,128]{2,1,0:T(8,128)(2,1)S(1)} async-done(((f16[4,512,128]{2,1,0:T(8,128)(2,1)}), f16[4,512,128]{2,1,0:T(8,128)(2,1)S(1)}, u32[]{:S(2)}, u32[]{:S(2)}) %all-to-all-start.4) | async-done | bytes 524320 | tf_op jit(solution)/shard_map/all_to_all | solution.py:85
  157.5 0.1 convert_element_type.15
  157.6 0.1 fusion.2
  157.6 0.8 maximum_select_fusion
  (6 shorter events, 0.1 us)
Async XLA Ops:
  1.8 23.1 %copy-start.6 = (bf16[512,256]{1,0:T(8,128)(2,1)S(1)}, bf16[512,256]{1,0:T(8,128)(2,1)}, u32[]{:S(2)}) copy-start(bf16[512,256]{1,0:T(8,128)(2,1)} %param.2) | copy-start | bytes 786436
  24.9 46.9 %copy-start.3 = (bf16[8,64,512]{2,1,0:T(8,128)(2,1)}, bf16[8,64,512]{2,1,0:T(8,128)(2,1)S(1)}, u32[]{:S(2)}) copy-start(bf16[8,64,512]{2,1,0:T(8,128)(2,1)S(1)} %all_to_all.25.v00) | copy-start | bytes 1572868
  26.0 33.1 %all-to-all-start = ((bf16[4,512,256]{2,1,0:T(8,128)(2,1)}), bf16[4,512,256]{2,1,0:T(8,128)(2,1)S(1)}, u32[]{:S(2)}, u32[]{:S(2)}) async-start(bf16[4,512,256]{2,1,0:T(8,128)(2,1)} %broadcast_in_dim.34), calls=%async_computation | async-start | bytes 2097152 | tf_op jit(solution)/shard_map/all_to_all | solution.py:22
  59.2 25.7 %copy-start = (bf16[4,512,256]{2,1,0:T(8,128)(2,1)}, bf16[4,512,256]{2,1,0:T(8,128)(2,1)S(1)}, u32[]{:S(2)}) copy-start(bf16[4,512,256]{2,1,0:T(8,128)(2,1)S(1)} %all-to-all-done.a_own) | copy-start | bytes 3145732
  60.1 21.1 %all-to-all-start.3 = ((bf16[8,64,512]{2,1,0:T(8,128)(2,1)}), bf16[8,64,512]{2,1,0:T(8,128)(2,1)S(1)}, u32[]{:S(2)}, u32[]{:S(2)}) async-start(bf16[8,64,512]{2,1,0:T(8,128)(2,1)} %broadcast_in_dim.38), calls=%async_computation.3 | async-start | bytes 1048576 | tf_op jit(solution)/shard_map/all_to_all | solution.py:22
  65.3 14.0 %collective-permute-start.1 = (bf16[8,64,512]{2,1,0:T(8,128)(2,1)S(1)}, bf16[8,64,512]{2,1,0:T(8,128)(2,1)}, u32[]{:S(2)}, u32[]{:S(2)}) collective-permute-start(bf16[8,64,512]{2,1,0:T(8,128)(2,1)S(1)} %all_to_all.25.v00), channel_id=1, source_target_pairs={{0,64},{64,128},{128,192},{192,256},{256,320},{320,384},{384,448},... | collective-permute-start | bytes 1572872 | tf_op jit(solution)/shard_map/ppermute | solution.py:81
  67.2 17.7 %collective-permute-start = (bf16[4,512,256]{2,1,0:T(8,128)(2,1)S(1)}, bf16[4,512,256]{2,1,0:T(8,128)(2,1)S(1)}, u32[]{:S(2)}, u32[]{:S(2)}) collective-permute-start(bf16[4,512,256]{2,1,0:T(8,128)(2,1)S(1)} %all-to-all-done.a_own), channel_id=1, source_target_pairs={{0,1},{1,2},{2,3},{3,4},{4,5},{5,6},{6,7},{7,0},{32,39},{33,32},{3... | collective-permute-start | bytes 3145736 | tf_op jit(solution)/shard_map/ppermute | solution.py:75
  71.9 11.6 %collective-permute-start.2 = (bf16[8,64,512]{2,1,0:T(8,128)(2,1)S(1)}, bf16[8,64,512]{2,1,0:T(8,128)(2,1)}, u32[]{:S(2)}, u32[]{:S(2)}) collective-permute-start(bf16[8,64,512]{2,1,0:T(8,128)(2,1)S(1)} %all_to_all.25.v00), channel_id=1, source_target_pairs={{0,32},{32,0},{1,33},{33,1},{2,34},{34,2},{3,35},{35,3},{4,36},{36... | collective-permute-start | bytes 1572872 | tf_op jit(solution)/shard_map/ppermute | solution.py:82
  79.3 4.2 %collective-permute-start.3 = (bf16[8,64,512]{2,1,0:T(8,128)(2,1)}, bf16[8,64,512]{2,1,0:T(8,128)(2,1)}, u32[]{:S(2)}, u32[]{:S(2)}) collective-permute-start(bf16[8,64,512]{2,1,0:T(8,128)(2,1)} %collective-permute-done.1.v10), channel_id=1, source_target_pairs={{0,32},{32,0},{1,33},{33,1},{2,34},{34,2},{3,35},{35,3},{4,36},{36... | collective-permute-start | bytes 1572872 | tf_op jit(solution)/shard_map/ppermute | solution.py:83
  81.2 37.1 %copy-start.2 = (bf16[8,64,512]{2,1,0:T(8,128)(2,1)}, bf16[8,64,512]{2,1,0:T(8,128)(2,1)S(1)}, u32[]{:S(2)}) copy-start(bf16[8,64,512]{2,1,0:T(8,128)(2,1)S(1)} %all-to-all-done.3.v00) | copy-start | bytes 1572868
  81.2 39.0 %collective-permute-start.4 = (bf16[8,64,512]{2,1,0:T(8,128)(2,1)S(1)}, bf16[8,64,512]{2,1,0:T(8,128)(2,1)}, u32[]{:S(2)}, u32[]{:S(2)}) collective-permute-start(bf16[8,64,512]{2,1,0:T(8,128)(2,1)S(1)} %all-to-all-done.3.v00), channel_id=1, source_target_pairs={{0,64},{64,128},{128,192},{192,256},{256,320},{320,384},{384,448},... | collective-permute-start | bytes 1572872 | tf_op jit(solution)/shard_map/ppermute | solution.py:81
  84.9 1.0 copy-start.1
  93.9 39.3 %all-to-all-start.2 = ((f16[4,512,128]{2,1,0:T(8,128)(2,1)}), f16[4,512,128]{2,1,0:T(8,128)(2,1)S(1)}, u32[]{:S(2)}, u32[]{:S(2)}) async-start(f16[4,512,128]{2,1,0:T(8,128)(2,1)} %convert_element_type.12), calls=%async_computation.2 | async-start | bytes 1048576 | tf_op jit(solution)/shard_map/all_to_all | solution.py:85
  118.3 4.3 %collective-permute-start.5 = (bf16[8,64,512]{2,1,0:T(8,128)(2,1)S(1)}, bf16[8,64,512]{2,1,0:T(8,128)(2,1)S(1)}, u32[]{:S(2)}, u32[]{:S(2)}) collective-permute-start(bf16[8,64,512]{2,1,0:T(8,128)(2,1)S(1)} %all-to-all-done.3.v00), channel_id=1, source_target_pairs={{0,32},{32,0},{1,33},{33,1},{2,34},{34,2},{3,35},{35,3},{4,36},{36... | collective-permute-start | bytes 1572872 | tf_op jit(solution)/shard_map/ppermute | solution.py:82
  120.2 4.1 %collective-permute-start.6 = (bf16[8,64,512]{2,1,0:T(8,128)(2,1)}, bf16[8,64,512]{2,1,0:T(8,128)(2,1)S(1)}, u32[]{:S(2)}, u32[]{:S(2)}) collective-permute-start(bf16[8,64,512]{2,1,0:T(8,128)(2,1)} %collective-permute-done.4.v10), channel_id=1, source_target_pairs={{0,32},{32,0},{1,33},{33,1},{2,34},{34,2},{3,35},{35,3},{4,36},{36... | collective-permute-start | bytes 1572872 | tf_op jit(solution)/shard_map/ppermute | solution.py:83
  122.6 1.7 %copy-start.4 = (bf16[8,64,512]{2,1,0:T(8,128)(2,1)}, bf16[8,64,512]{2,1,0:T(8,128)(2,1)S(1)}, u32[]{:S(2)}) copy-start(bf16[8,64,512]{2,1,0:T(8,128)(2,1)S(1)} %collective-permute-done.5.v01) | copy-start | bytes 1572868
  124.4 0.8 copy-start.5
  133.2 24.3 %all-to-all-start.4 = ((f16[4,512,128]{2,1,0:T(8,128)(2,1)}), f16[4,512,128]{2,1,0:T(8,128)(2,1)S(1)}, u32[]{:S(2)}, u32[]{:S(2)}) async-start(f16[4,512,128]{2,1,0:T(8,128)(2,1)} %convert_element_type.14), calls=%async_computation.4 | async-start | bytes 1048576 | tf_op jit(solution)/shard_map/all_to_all | solution.py:85

commit v2 on v1

v2 whole, which is shorter than its diff:
```python
import jax
import jax.numpy as jnp
from jax import lax
from jax.experimental import pallas as pl
from jax.experimental.pallas import tpu as pltpu
from jax.sharding import Mesh
from jax.sharding import PartitionSpec as P


PAIRS = 8128
AXES = ("zl", "x", "c", "kl", "ij")
SCALE = 64.0

X_PARITY = [[zl * 8 + x for zl in range(2) for x in range(p, 8, 2)] for p in range(2)]
Y_HOP = [(c * 8 + y, c * 8 + (y + 1 - 2 * c) % 8) for c in range(2) for y in range(8)]
X_HOP = [(x * 2 + c, (x + 1 - 2 * c) % 8 * 2 + c) for c in range(2) for x in range(8)]
SWAP = [(0, 1), (1, 0)]


def along_y(shard, step):
    return lax.ppermute(shard, "ij", [(y, (y + step) % 8) for y in range(8)])


def product_kernel(*refs):
    a_refs, v_refs, (out, own, a_all, v_all) = refs[:8], refs[8:12], refs[12:]
    x, y, c = (lax.axis_index(name) for name in ("x", "ij", "c"))
    kl = lax.axis_index("kl")
    near = 2 * c - 1
    places = [0, -2, 2, 4]
    places += [near + place for place in places]
    for place, ref in zip(places, a_refs):
        start = pl.multiple_of((y + place + 16) % 8 * 256, 256)
        a_all[:, pl.ds(start, 256)] = ref[...]
    for s, t, ref in ((0, 0, v_refs[0]), (1, 0, v_refs[1]), (0, 1, v_refs[2]), (1, 1, v_refs[3])):
        offset = (x + s) % 2 * 128 + (c + t) % 2 * 64
        for k in range(8):
            start = pl.multiple_of(offset + k * 256, 64)
            v_all[pl.ds(start, 64), :] = ref[k]

    @pl.when(kl == 3)
    def _():
        v_all[pl.ds(1984, 64), :] = jnp.zeros((64, 1024), jnp.bfloat16)

    for k in range(4):
        out[k] = SCALE * jnp.dot(
            a_all[...], v_all[:, k * 256 : (k + 1) * 256],
            preferred_element_type=jnp.float32,
        )
    own[...] = out[kl]


def product(*pieces):
    return pl.pallas_call(
        product_kernel,
        out_shape=(
            jax.ShapeDtypeStruct((4, 512, 256), jnp.float32),
            jax.ShapeDtypeStruct((512, 256), jnp.float32),
        ),
        in_specs=[pl.BlockSpec(memory_space=pltpu.VMEM)] * 12,
        out_specs=[pl.BlockSpec(memory_space=pltpu.VMEM)] * 2,
        scratch_shapes=[
            pltpu.VMEM((512, 2048), jnp.bfloat16),
            pltpu.VMEM((2048, 1024), jnp.bfloat16),
        ],
        compiler_params=pltpu.CompilerParams(vmem_limit_bytes=24 << 20),
        cost_estimate=pl.CostEstimate(
            flops=2 * 512 * 2048 * 1024, bytes_accessed=8 << 20, transcendentals=0
        ),
    )(*pieces)


def untouched_kernel(given, out):
    del given, out


def untouched(block):
    return pl.pallas_call(
        untouched_kernel,
        out_shape=jax.ShapeDtypeStruct(block.shape, block.dtype),
        in_specs=[pl.BlockSpec(memory_space=pl.ANY)],
        out_specs=pl.BlockSpec(memory_space=pl.ANY),
        input_output_aliases={0: 0},
        compiler_params=pltpu.CompilerParams(vmem_limit_bytes=1 << 20),
        cost_estimate=pl.CostEstimate(flops=1000, bytes_accessed=0, transcendentals=0),
    )(block)


def staged(amplitudes, integrals):
    v00 = lax.all_to_all(
        jnp.broadcast_to(integrals[None], (8, 64, 1024)), ("zl", "x"), 0, 0,
        tiled=True, axis_index_groups=X_PARITY,
    )
    blocks = [amplitudes]
    for step in (2, -2, 4):
        blocks.append(along_y(amplitudes, step))
    for i in range(4):
        blocks.append(lax.ppermute(blocks[i], ("c", "ij"), Y_HOP))
        if i == 0:
            blocks[4] = untouched(blocks[4])
    v10 = lax.ppermute(v00, ("x", "c"), X_HOP)
    v01 = lax.ppermute(v00, "c", SWAP)
    v11 = lax.ppermute(v10, "c", SWAP)
    terms, own = product(*blocks, v00, v10, v01, v11)
    terms = terms.astype(jnp.float16)
    kl = lax.axis_index("kl")
    got = lax.all_to_all(terms, "kl", 0, 0, tiled=True)
    total = own
    for k in range(4):
        total = total + jnp.where(kl == k, 0.0, got[k].astype(jnp.float32))
    out_ids = lax.axis_index("ij") * 1024 + kl * 256 + jnp.arange(256)
    return jnp.where((out_ids < PAIRS)[None, :], total * (1.0 / SCALE), jnp.float32(0.0))


def solution(mesh):
    fine = Mesh(mesh.devices.reshape(2, 8, 2, 4, 8), AXES)
    ab = ("zl", "x", "c")
    return jax.shard_map(
        staged, mesh=fine,
        in_specs=(P(ab, ("kl", "ij")), P(("kl", *ab), "ij")),
        out_specs=P(ab, ("ij", "kl")), check_vma=False,
    )
```

time: 159 us -> 167 us (1.050)
  the two profiles are of different devices: /device:TPU:148 before, /device:TPU:1 now
where the time goes in v2:
time: 167 us; the launch traced here: 165 us
  starting transfers between devices  85.6 us (51%)
  waiting for transfers between devices  39.4 us (24%)
  blocking collectives  33.2 us (20%)
  Pallas kernels  3.06 us (2%)
  other arithmetic  2.19 us (1%)
    all_to_all x1, blocking collectives, staged(): lax.all_to_all(jnp.broadcast_to(integrals[None], (8, 64, 1024)), ('zl', '...  33.2 us
    all_to_all x1, starting transfers between devices, staged(): got = lax.all_to_all(terms, 'kl', 0, 0, tiled=True)  29.6 us
    all_to_all x1, waiting for transfers between devices, staged(): got = lax.all_to_all(terms, 'kl', 0, 0, tiled=True)  24.5 us
    ppermute x1, starting transfers between devices, staged(): v01 = lax.ppermute(v00, 'c', SWAP)  16.2 us
    ppermute x1, starting transfers between devices, staged(): v11 = lax.ppermute(v10, 'c', SWAP)  15.9 us
    ppermute x4, starting transfers between devices, staged(): blocks.append(lax.ppermute(blocks[i], ('c', 'ij'), Y_HOP))  12.7 us
    ppermute x3, waiting for transfers between devices, along_y(): return lax.ppermute(shard, 'ij', [(y, (y + step) % 8) for y in range(8)])  10 us
    ppermute x3, starting transfers between devices, along_y(): return lax.ppermute(shard, 'ij', [(y, (y + step) % 8) for y in range(8)])  9.31 us
  transfers between devices with their start and end apart: 11, of which 6 were waited for; matrix products, arithmetic and copies ran while one was open for 0% of the time, Pallas kernels for 0%

profile of v2, /device:TPU:1, one launch (start us, length us, event | category | flops | bytes accessed | tf_op | source)
XLA Modules:
  0.0 164.7 jit_solution(8323412358362051737)
XLA Ops:
  0.0 0.0 copy-start
  0.0 1.1 broadcast_in_dim.27
  1.1 33.2 %all_to_all.10.refs_8_ = bf16[8,64,1024]{2,1,0:T(8,128)(2,1)S(1)} all-to-all(bf16[8,64,1024]{2,1,0:T(8,128)(2,1)S(1)} %broadcast_in_dim.27), channel_id=1, replica_groups={{0,128,256,384,512,640,768,896},{64,192,320,448,576,704,832,960},{1,129..., dimensions={0} | all-to-all | bytes 2097152 | tf_op jit(solution)/shard_map/all_to_all | solution.py:89
  34.3 1.9 %collective-permute-start.7 = (bf16[8,64,1024]{2,1,0:T(8,128)(2,1)S(1)}, bf16[8,64,1024]{2,1,0:T(8,128)(2,1)S(1)}, u32[]{:S(2)}, u32[]{:S(2)}) collective-permute-start(bf16[8,64,1024]{2,1,0:T(8,128)(2,1)S(1)} %all_to_all.10.refs_8_), channel_id=1, source_target_pairs={{0,64},{64,128},{128,192},{192,256},{256,320},{320,384},{384,448},... | collective-permute-start | bytes 3145736 | tf_op jit(solution)/shard_map/ppermute | solution.py:100
  36.2 16.2 %collective-permute-start.8 = (bf16[8,64,1024]{2,1,0:T(8,128)(2,1)S(1)}, bf16[8,64,1024]{2,1,0:T(8,128)(2,1)S(1)}, u32[]{:S(2)}, u32[]{:S(2)}) collective-permute-start(bf16[8,64,1024]{2,1,0:T(8,128)(2,1)S(1)} %all_to_all.10.refs_8_), channel_id=1, source_target_pairs={{0,32},{32,0},{1,33},{33,1},{2,34},{34,2},{3,35},{35,3},{4,36},{36... | collective-permute-start | bytes 3145736 | tf_op jit(solution)/shard_map/ppermute | solution.py:101
  52.5 0.0 collective-permute-done.7.refs_9_
  52.5 15.9 %collective-permute-start.9 = (bf16[8,64,1024]{2,1,0:T(8,128)(2,1)S(1)}, bf16[8,64,1024]{2,1,0:T(8,128)(2,1)S(1)}, u32[]{:S(2)}, u32[]{:S(2)}) collective-permute-start(bf16[8,64,1024]{2,1,0:T(8,128)(2,1)S(1)} %collective-permute-done.7.refs_9_), channel_id=1, source_target_pairs={{0,32},{32,0},{1,33},{33,1},{2,34},{34,2},{3,35},{35,3},{4,36},{36... | collective-permute-start | bytes 3145736 | tf_op jit(solution)/shard_map/ppermute | solution.py:102
  68.5 0.0 copy-done
  68.5 1.9 %collective-permute-start = (bf16[512,256]{1,0:T(8,128)(2,1)S(1)}, bf16[512,256]{1,0:T(8,128)(2,1)S(1)}, u32[]{:S(2)}, u32[]{:S(2)}) collective-permute-start(bf16[512,256]{1,0:T(8,128)(2,1)S(1)} %copy-done), channel_id=1, source_target_pairs={{0,2},{1,3},{2,4},{3,5},{4,6},{5,7},{6,0},{7,1},{8,10},{9,11},{10,... | collective-permute-start | bytes 786440 | tf_op jit(solution)/shard_map/ppermute | solution.py:21
  70.4 5.5 %collective-permute-start.1 = (bf16[512,256]{1,0:T(8,128)(2,1)S(1)}, bf16[512,256]{1,0:T(8,128)(2,1)S(1)}, u32[]{:S(2)}, u32[]{:S(2)}) collective-permute-start(bf16[512,256]{1,0:T(8,128)(2,1)S(1)} %copy-done), channel_id=1, source_target_pairs={{0,6},{1,7},{2,0},{3,1},{4,2},{5,3},{6,4},{7,5},{8,14},{9,15},{10,... | collective-permute-start | bytes 786440 | tf_op jit(solution)/shard_map/ppermute | solution.py:21
  75.9 1.9 %collective-permute-start.2 = (bf16[512,256]{1,0:T(8,128)(2,1)S(1)}, bf16[512,256]{1,0:T(8,128)(2,1)S(1)}, u32[]{:S(2)}, u32[]{:S(2)}) collective-permute-start(bf16[512,256]{1,0:T(8,128)(2,1)S(1)} %copy-done), channel_id=1, source_target_pairs={{0,4},{1,5},{2,6},{3,7},{4,0},{5,1},{6,2},{7,3},{8,12},{9,13},{10,... | collective-permute-start | bytes 786440 | tf_op jit(solution)/shard_map/ppermute | solution.py:21
  77.8 4.3 %collective-permute-done.refs_1_ = bf16[512,256]{1,0:T(8,128)(2,1)S(1)} collective-permute-done((bf16[512,256]{1,0:T(8,128)(2,1)S(1)}, bf16[512,256]{1,0:T(8,128)(2,1)S(1)}, u32[]{:S(2)}, u32[]{:S(2)}) %collective-permute-start) | collective-permute-done | bytes 262176 | tf_op jit(solution)/shard_map/ppermute | solution.py:21
  82.1 1.9 %collective-permute-start.3 = (bf16[512,256]{1,0:T(8,128)(2,1)S(1)}, bf16[512,256]{1,0:T(8,128)(2,1)S(1)}, u32[]{:S(2)}, u32[]{:S(2)}) collective-permute-start(bf16[512,256]{1,0:T(8,128)(2,1)S(1)} %copy-done), channel_id=1, source_target_pairs={{0,1},{1,2},{2,3},{3,4},{4,5},{5,6},{6,7},{7,0},{32,39},{33,32},{3... | collective-permute-start | bytes 786440 | tf_op jit(solution)/shard_map/ppermute | solution.py:97
  84.0 5.0 %collective-permute-done.1.refs_2_ = bf16[512,256]{1,0:T(8,128)(2,1)S(1)} collective-permute-done((bf16[512,256]{1,0:T(8,128)(2,1)S(1)}, bf16[512,256]{1,0:T(8,128)(2,1)S(1)}, u32[]{:S(2)}, u32[]{:S(2)}) %collective-permute-start.1) | collective-permute-done | bytes 262176 | tf_op jit(solution)/shard_map/ppermute | solution.py:21
  89.0 1.9 %collective-permute-start.4 = (bf16[512,256]{1,0:T(8,128)(2,1)S(1)}, bf16[512,256]{1,0:T(8,128)(2,1)S(1)}, u32[]{:S(2)}, u32[]{:S(2)}) collective-permute-start(bf16[512,256]{1,0:T(8,128)(2,1)S(1)} %collective-permute-done.refs_1_), channel_id=1, source_target_pairs={{0,1},{1,2},{2,3},{3,4},{4,5},{5,6},{6,7},{7,0},{32,39},{33,32},{3... | collective-permute-start | bytes 786440 | tf_op jit(solution)/shard_map/ppermute | solution.py:97
  90.9 0.8 collective-permute-done.2.refs_3_
  91.7 4.8 %collective-permute-start.5 = (bf16[512,256]{1,0:T(8,128)(2,1)S(1)}, bf16[512,256]{1,0:T(8,128)(2,1)S(1)}, u32[]{:S(2)}, u32[]{:S(2)}) collective-permute-start(bf16[512,256]{1,0:T(8,128)(2,1)S(1)} %collective-permute-done.1.refs_2_), channel_id=1, source_target_pairs={{0,1},{1,2},{2,3},{3,4},{4,5},{5,6},{6,7},{7,0},{32,39},{33,32},{3... | collective-permute-start | bytes 786440 | tf_op jit(solution)/shard_map/ppermute | solution.py:97
  96.5 0.0 collective-permute-done.3.given
  96.5 4.0 %collective-permute-start.6 = (bf16[512,256]{1,0:T(8,128)(2,1)S(1)}, bf16[512,256]{1,0:T(8,128)(2,1)S(1)}, u32[]{:S(2)}, u32[]{:S(2)}) collective-permute-start(bf16[512,256]{1,0:T(8,128)(2,1)S(1)} %collective-permute-done.2.refs_3_), channel_id=1, source_target_pairs={{0,1},{1,2},{2,3},{3,4},{4,5},{5,6},{6,7},{7,0},{32,39},{33,32},{3... | collective-permute-start | bytes 786440 | tf_op jit(solution)/shard_map/ppermute | solution.py:97
  100.5 0.0 collective-permute-done.4.refs_5_
  100.5 2.1 %collective-permute-done.5.refs_6_ = bf16[512,256]{1,0:T(8,128)(2,1)S(1)} collective-permute-done((bf16[512,256]{1,0:T(8,128)(2,1)S(1)}, bf16[512,256]{1,0:T(8,128)(2,1)S(1)}, u32[]{:S(2)}, u32[]{:S(2)}) %collective-permute-start.5) | collective-permute-done | bytes 262176 | tf_op jit(solution)/shard_map/ppermute | solution.py:97
  102.6 2.7 %collective-permute-done.6.refs_7_ = bf16[512,256]{1,0:T(8,128)(2,1)S(1)} collective-permute-done((bf16[512,256]{1,0:T(8,128)(2,1)S(1)}, bf16[512,256]{1,0:T(8,128)(2,1)S(1)}, u32[]{:S(2)}, u32[]{:S(2)}) %collective-permute-start.6) | collective-permute-done | bytes 262176 | tf_op jit(solution)/shard_map/ppermute | solution.py:97
  105.4 0.0 collective-permute-done.8.refs_10_
  105.4 0.0 collective-permute-done.9.refs_11_
  105.4 3.1 %shard_map.29 = (f32[4,512,256]{2,1,0:T(8,128)S(1)}, f32[512,256]{1,0:T(8,128)S(1)}) custom-call(bf16[512,256]{1,0:T(8,128)(2,1)S(1)} %copy-done, bf16[512,256]{1,0:T(8,128)(2,1)S(1)} %collective-permute-done.refs_1_, bf16[512,256]{1,0:T(8,128)(2,1)S(1)} %collective-permute-done.1.refs_2_, bf16[512,256]{1,0:T(8,128)(2,1)S(1)} %collective-permute-done.2.refs_3_, ...), custom_call_target="tpu_custom_call" | custom-call | flops 2147483648 | bytes 8388608 | tf_op jit(solution)/shard_map/pallas_call | solution.py:53
  108.4 1.1 convert_element_type.19
  109.6 29.6 %all-to-all-start.1 = ((f16[4,512,256]{2,1,0:T(8,128)(2,1)}), f16[4,512,256]{2,1,0:T(8,128)(2,1)S(1)}, u32[]{:S(2)}, u32[]{:S(2)}) async-start(f16[4,512,256]{2,1,0:T(8,128)(2,1)} %convert_element_type.19), calls=%async_computation.1 | async-start | bytes 2097152 | tf_op jit(solution)/shard_map/all_to_all | solution.py:106
  139.2 24.5 %all-to-all-done.1 = f16[4,512,256]{2,1,0:T(8,128)(2,1)S(1)} async-done(((f16[4,512,256]{2,1,0:T(8,128)(2,1)}), f16[4,512,256]{2,1,0:T(8,128)(2,1)S(1)}, u32[]{:S(2)}, u32[]{:S(2)}) %all-to-all-start.1) | async-done | bytes 1048608 | tf_op jit(solution)/shard_map/all_to_all | solution.py:106
  163.7 1.0 fusion.1
  (2 shorter events, 0.0 us)
Async XLA Ops:
  0.0 68.5 %copy-start = (bf16[512,256]{1,0:T(8,128)(2,1)S(1)}, bf16[512,256]{1,0:T(8,128)(2,1)}, u32[]{:S(2)}) copy-start(bf16[512,256]{1,0:T(8,128)(2,1)} %refs_0_.1) | copy-start | bytes 786436
  34.3 18.2 %collective-permute-start.7 = (bf16[8,64,1024]{2,1,0:T(8,128)(2,1)S(1)}, bf16[8,64,1024]{2,1,0:T(8,128)(2,1)S(1)}, u32[]{:S(2)}, u32[]{:S(2)}) collective-permute-start(bf16[8,64,1024]{2,1,0:T(8,128)(2,1)S(1)} %all_to_all.10.refs_8_), channel_id=1, source_target_pairs={{0,64},{64,128},{128,192},{192,256},{256,320},{320,384},{384,448},... | collective-permute-start | bytes 3145736 | tf_op jit(solution)/shard_map/ppermute | solution.py:100
  36.2 69.1 %collective-permute-start.8 = (bf16[8,64,1024]{2,1,0:T(8,128)(2,1)S(1)}, bf16[8,64,1024]{2,1,0:T(8,128)(2,1)S(1)}, u32[]{:S(2)}, u32[]{:S(2)}) collective-permute-start(bf16[8,64,1024]{2,1,0:T(8,128)(2,1)S(1)} %all_to_all.10.refs_8_), channel_id=1, source_target_pairs={{0,32},{32,0},{1,33},{33,1},{2,34},{34,2},{3,35},{35,3},{4,36},{36... | collective-permute-start | bytes 3145736 | tf_op jit(solution)/shard_map/ppermute | solution.py:101
  52.5 52.9 %collective-permute-start.9 = (bf16[8,64,1024]{2,1,0:T(8,128)(2,1)S(1)}, bf16[8,64,1024]{2,1,0:T(8,128)(2,1)S(1)}, u32[]{:S(2)}, u32[]{:S(2)}) collective-permute-start(bf16[8,64,1024]{2,1,0:T(8,128)(2,1)S(1)} %collective-permute-done.7.refs_9_), channel_id=1, source_target_pairs={{0,32},{32,0},{1,33},{33,1},{2,34},{34,2},{3,35},{35,3},{4,36},{36... | collective-permute-start | bytes 3145736 | tf_op jit(solution)/shard_map/ppermute | solution.py:102
  68.5 13.6 %collective-permute-start = (bf16[512,256]{1,0:T(8,128)(2,1)S(1)}, bf16[512,256]{1,0:T(8,128)(2,1)S(1)}, u32[]{:S(2)}, u32[]{:S(2)}) collective-permute-start(bf16[512,256]{1,0:T(8,128)(2,1)S(1)} %copy-done), channel_id=1, source_target_pairs={{0,2},{1,3},{2,4},{3,5},{4,6},{5,7},{6,0},{7,1},{8,10},{9,11},{10,... | collective-permute-start | bytes 786440 | tf_op jit(solution)/shard_map/ppermute | solution.py:21
  70.4 18.6 %collective-permute-start.1 = (bf16[512,256]{1,0:T(8,128)(2,1)S(1)}, bf16[512,256]{1,0:T(8,128)(2,1)S(1)}, u32[]{:S(2)}, u32[]{:S(2)}) collective-permute-start(bf16[512,256]{1,0:T(8,128)(2,1)S(1)} %copy-done), channel_id=1, source_target_pairs={{0,6},{1,7},{2,0},{3,1},{4,2},{5,3},{6,4},{7,5},{8,14},{9,15},{10,... | collective-permute-start | bytes 786440 | tf_op jit(solution)/shard_map/ppermute | solution.py:21
  75.9 15.8 %collective-permute-start.2 = (bf16[512,256]{1,0:T(8,128)(2,1)S(1)}, bf16[512,256]{1,0:T(8,128)(2,1)S(1)}, u32[]{:S(2)}, u32[]{:S(2)}) collective-permute-start(bf16[512,256]{1,0:T(8,128)(2,1)S(1)} %copy-done), channel_id=1, source_target_pairs={{0,4},{1,5},{2,6},{3,7},{4,0},{5,1},{6,2},{7,3},{8,12},{9,13},{10,... | collective-permute-start | bytes 786440 | tf_op jit(solution)/shard_map/ppermute | solution.py:21
  82.1 14.4 %collective-permute-start.3 = (bf16[512,256]{1,0:T(8,128)(2,1)S(1)}, bf16[512,256]{1,0:T(8,128)(2,1)S(1)}, u32[]{:S(2)}, u32[]{:S(2)}) collective-permute-start(bf16[512,256]{1,0:T(8,128)(2,1)S(1)} %copy-done), channel_id=1, source_target_pairs={{0,1},{1,2},{2,3},{3,4},{4,5},{5,6},{6,7},{7,0},{32,39},{33,32},{3... | collective-permute-start | bytes 786440 | tf_op jit(solution)/shard_map/ppermute | solution.py:97
  89.0 11.6 %collective-permute-start.4 = (bf16[512,256]{1,0:T(8,128)(2,1)S(1)}, bf16[512,256]{1,0:T(8,128)(2,1)S(1)}, u32[]{:S(2)}, u32[]{:S(2)}) collective-permute-start(bf16[512,256]{1,0:T(8,128)(2,1)S(1)} %collective-permute-done.refs_1_), channel_id=1, source_target_pairs={{0,1},{1,2},{2,3},{3,4},{4,5},{5,6},{6,7},{7,0},{32,39},{33,32},{3... | collective-permute-start | bytes 786440 | tf_op jit(solution)/shard_map/ppermute | solution.py:97
  91.7 11.0 %collective-permute-start.5 = (bf16[512,256]{1,0:T(8,128)(2,1)S(1)}, bf16[512,256]{1,0:T(8,128)(2,1)S(1)}, u32[]{:S(2)}, u32[]{:S(2)}) collective-permute-start(bf16[512,256]{1,0:T(8,128)(2,1)S(1)} %collective-permute-done.1.refs_2_), channel_id=1, source_target_pairs={{0,1},{1,2},{2,3},{3,4},{4,5},{5,6},{6,7},{7,0},{32,39},{33,32},{3... | collective-permute-start | bytes 786440 | tf_op jit(solution)/shard_map/ppermute | solution.py:97
  96.5 8.8 %collective-permute-start.6 = (bf16[512,256]{1,0:T(8,128)(2,1)S(1)}, bf16[512,256]{1,0:T(8,128)(2,1)S(1)}, u32[]{:S(2)}, u32[]{:S(2)}) collective-permute-start(bf16[512,256]{1,0:T(8,128)(2,1)S(1)} %collective-permute-done.2.refs_3_), channel_id=1, source_target_pairs={{0,1},{1,2},{2,3},{3,4},{4,5},{5,6},{6,7},{7,0},{32,39},{33,32},{3... | collective-permute-start | bytes 786440 | tf_op jit(solution)/shard_map/ppermute | solution.py:97
  109.6 54.1 %all-to-all-start.1 = ((f16[4,512,256]{2,1,0:T(8,128)(2,1)}), f16[4,512,256]{2,1,0:T(8,128)(2,1)S(1)}, u32[]{:S(2)}, u32[]{:S(2)}) async-start(f16[4,512,256]{2,1,0:T(8,128)(2,1)} %convert_element_type.19), calls=%async_computation.1 | async-start | bytes 2097152 | tf_op jit(solution)/shard_map/all_to_all | solution.py:106

commit v3 on v2

--- a/solution.py
+++ b/solution.py
@@ -21,10 +21,14 @@
     return lax.ppermute(shard, "ij", [(y, (y + step) % 8) for y in range(8)])
 
 
-def product_kernel(*refs):
-    a_refs, v_refs, (out, own, a_all, v_all) = refs[:8], refs[8:12], refs[12:]
+def shifted(term, ahead):
+    pairs = [(k, (k + ahead) % 4) for k in range(4)]
+    return lax.ppermute(term.astype(jnp.float16), "kl", pairs).astype(jnp.float32)
+
+
+def first_kernel(*refs):
+    a_refs, v_refs, (a_all, v_all) = refs[:8], refs[8:12], refs[12:14]
     x, y, c = (lax.axis_index(name) for name in ("x", "ij", "c"))
-    kl = lax.axis_index("kl")
     near = 2 * c - 1
     places = [0, -2, 2, 4]
     places += [near + place for place in places]
@@ -37,36 +41,58 @@
             start = pl.multiple_of(offset + k * 256, 64)
             v_all[pl.ds(start, 64), :] = ref[k]
 
-    @pl.when(kl == 3)
+    @pl.when(lax.axis_index("kl") == 3)
     def _():
         v_all[pl.ds(1984, 64), :] = jnp.zeros((64, 1024), jnp.bfloat16)
 
-    for k in range(4):
-        out[k] = SCALE * jnp.dot(
-            a_all[...], v_all[:, k * 256 : (k + 1) * 256],
-            preferred_element_type=jnp.float32,
-        )
-    own[...] = out[kl]
+
+    place_product(2, a_all, v_all, refs[14])
 
 
-def product(*pieces):
+def place_product(ahead, a_all, v_all, out):
+    start = pl.multiple_of((lax.axis_index("kl") + ahead) % 4 * 256, 256)
+    out[...] = SCALE * jnp.dot(
+        a_all[...], v_all[:, pl.ds(start, 256)], preferred_element_type=jnp.float32
+    )
+
+
+def later_kernel(a_all, v_all, *outs):
+    for ahead, out in zip((1, 3, 0), outs):
+        place_product(ahead, a_all, v_all, out)
+
+
+VMEM = pl.BlockSpec(memory_space=pltpu.VMEM)
+TERM = jax.ShapeDtypeStruct((512, 256), jnp.float32)
+
+
+def first_product(*pieces):
     return pl.pallas_call(
-        product_kernel,
+        first_kernel,
         out_shape=(
-            jax.ShapeDtypeStruct((4, 512, 256), jnp.float32),
-            jax.ShapeDtypeStruct((512, 256), jnp.float32),
+            jax.ShapeDtypeStruct((512, 2048), jnp.bfloat16),
+            jax.ShapeDtypeStruct((2048, 1024), jnp.bfloat16),
+            TERM,
         ),
-        in_specs=[pl.BlockSpec(memory_space=pltpu.VMEM)] * 12,
-        out_specs=[pl.BlockSpec(memory_space=pltpu.VMEM)] * 2,
-        scratch_shapes=[
-            pltpu.VMEM((512, 2048), jnp.bfloat16),
-            pltpu.VMEM((2048, 1024), jnp.bfloat16),
-        ],
-        compiler_params=pltpu.CompilerParams(vmem_limit_bytes=24 << 20),
+        in_specs=[VMEM] * 12,
+        out_specs=[VMEM] * 3,
+        compiler_params=pltpu.CompilerParams(vmem_limit_bytes=16 << 20),
         cost_estimate=pl.CostEstimate(
-            flops=2 * 512 * 2048 * 1024, bytes_accessed=8 << 20, transcendentals=0
+            flops=2 * 512 * 2048 * 256, bytes_accessed=12 << 20, transcendentals=0
         ),
     )(*pieces)
+
+
+def later_products(a_all, v_all):
+    return pl.pallas_call(
+        later_kernel,
+        out_shape=(TERM,) * 3,
+        in_specs=[VMEM] * 2,
+        out_specs=[VMEM] * 3,
+        compiler_params=pltpu.CompilerParams(vmem_limit_bytes=16 << 20),
+        cost_estimate=pl.CostEstimate(
+            flops=6 * 512 * 2048 * 256, bytes_accessed=8 << 20, transcendentals=0
+        ),
+    )(a_all, v_all)
 
 
 def untouched_kernel(given, out):
@@ -100,13 +126,13 @@
     v10 = lax.ppermute(v00, ("x", "c"), X_HOP)
     v01 = lax.ppermute(v00, "c", SWAP)
     v11 = lax.ppermute(v10, "c", SWAP)
-    terms, own = product(*blocks, v00, v10, v01, v11)
-    terms = terms.astype(jnp.float16)
+    a_all, v_all, term = first_product(*blocks, v00, v10, v01, v11)
+    total = [shifted(term, 2)]
+    term_1, term_3, own = later_products(a_all, v_all)
+    total.append(shifted(term_1, 1))
+    total.append(shifted(term_3, 3))
+    total = own + (total[1] + total[2]) + total[0]
     kl = lax.axis_index("kl")
-    got = lax.all_to_all(terms, "kl", 0, 0, tiled=True)
-    total = own
-    for k in range(4):
-        total = total + jnp.where(kl == k, 0.0, got[k].astype(jnp.float32))
     out_ids = lax.axis_index("ij") * 1024 + kl * 256 + jnp.arange(256)
     return jnp.where((out_ids < PAIRS)[None, :], total * (1.0 / SCALE), jnp.float32(0.0))
 

time: 167 us -> 166 us (level)
  starting transfers between devices: 85.6 us -> 92.2 us
  waiting for transfers between devices: 39.4 us -> 33.5 us
    ppermute x0 -> x3, starting transfers between devices: none -> 36 us  [shifted(): lax.ppermute(term.astype(jnp.float16), 'kl', pairs).astype(jnp.float32)]
    all_to_all x1 -> x0, starting transfers between devices: 29.6 us -> none  [staged(): got = lax.all_to_all(terms, 'kl', 0, 0, tiled=True)]
    all_to_all x1 -> x0, waiting for transfers between devices: 24.5 us -> none  [staged(): got = lax.all_to_all(terms, 'kl', 0, 0, tiled=True)]
    ppermute x0 -> x3, waiting for transfers between devices: none -> 18.4 us  [shifted(): lax.ppermute(term.astype(jnp.float16), 'kl', pairs).astype(jnp.float32)]
  transfers between devices with their start and end apart: 11 -> 13, of which waited for: 6 -> 6; matrix products, arithmetic and copies ran while one was open for 0% -> 0% of each run, Pallas kernels for 0% -> 0%
where the time goes in v3:
time: 166 us; the launch traced here: 165 us
  starting transfers between devices  92.2 us (56%)
  waiting for transfers between devices  33.5 us (20%)
  blocking collectives  33.2 us (20%)
  Pallas kernels  3.23 us (2%)
  local copies, waits for them, and re-layouts  1.97 us (1%)
    ppermute x3, starting transfers between devices, shifted(): lax.ppermute(term.astype(jnp.float16), 'kl', pairs).astype(jnp.float32)  36 us
    all_to_all x1, blocking collectives, staged(): lax.all_to_all(jnp.broadcast_to(integrals[None], (8, 64, 1024)), ('zl', '...  33.2 us
    ppermute x3, waiting for transfers between devices, shifted(): lax.ppermute(term.astype(jnp.float16), 'kl', pairs).astype(jnp.float32)  18.4 us
    ppermute x1, starting transfers between devices, staged(): v01 = lax.ppermute(v00, 'c', SWAP)  16.2 us
    ppermute x1, starting transfers between devices, staged(): v11 = lax.ppermute(v10, 'c', SWAP)  15.9 us
    ppermute x4, starting transfers between devices, staged(): blocks.append(lax.ppermute(blocks[i], ('c', 'ij'), Y_HOP))  12.7 us
    ppermute x3, waiting for transfers between devices, along_y(): return lax.ppermute(shard, 'ij', [(y, (y + step) % 8) for y in range(8)])  10.2 us
    ppermute x3, starting transfers between devices, along_y(): return lax.ppermute(shard, 'ij', [(y, (y + step) % 8) for y in range(8)])  9.32 us
  transfers between devices with their start and end apart: 13, of which 6 were waited for; matrix products, arithmetic and copies ran while one was open for 0% of the time, Pallas kernels for 0%

profile of v3, /device:TPU:1, one launch (start us, length us, event | category | flops | bytes accessed | tf_op | source)
XLA Modules:
  0.0 165.3 jit_solution(8443614522684751714)
XLA Ops:
  0.0 1.0 broadcast_in_dim.20
  1.0 33.2 %all_to_all.5.refs_8_ = bf16[8,64,1024]{2,1,0:T(8,128)(2,1)S(1)} all-to-all(bf16[8,64,1024]{2,1,0:T(8,128)(2,1)S(1)} %broadcast_in_dim.20), channel_id=1, replica_groups={{0,128,256,384,512,640,768,896},{64,192,320,448,576,704,832,960},{1,129..., dimensions={0} | all-to-all | bytes 2097152 | tf_op jit(solution)/shard_map/all_to_all | solution.py:115
  34.3 1.9 %collective-permute-start.7 = (bf16[8,64,1024]{2,1,0:T(8,128)(2,1)S(1)}, bf16[8,64,1024]{2,1,0:T(8,128)(2,1)S(1)}, u32[]{:S(2)}, u32[]{:S(2)}) collective-permute-start(bf16[8,64,1024]{2,1,0:T(8,128)(2,1)S(1)} %all_to_all.5.refs_8_), channel_id=1, source_target_pairs={{0,64},{64,128},{128,192},{192,256},{256,320},{320,384},{384,448},... | collective-permute-start | bytes 3145736 | tf_op jit(solution)/shard_map/ppermute | solution.py:126
  36.2 16.2 %collective-permute-start.8 = (bf16[8,64,1024]{2,1,0:T(8,128)(2,1)S(1)}, bf16[8,64,1024]{2,1,0:T(8,128)(2,1)S(1)}, u32[]{:S(2)}, u32[]{:S(2)}) collective-permute-start(bf16[8,64,1024]{2,1,0:T(8,128)(2,1)S(1)} %all_to_all.5.refs_8_), channel_id=1, source_target_pairs={{0,32},{32,0},{1,33},{33,1},{2,34},{34,2},{3,35},{35,3},{4,36},{36... | collective-permute-start | bytes 3145736 | tf_op jit(solution)/shard_map/ppermute | solution.py:127
  52.4 0.0 collective-permute-done.7.refs_9_
  52.4 15.9 %collective-permute-start.9 = (bf16[8,64,1024]{2,1,0:T(8,128)(2,1)S(1)}, bf16[8,64,1024]{2,1,0:T(8,128)(2,1)S(1)}, u32[]{:S(2)}, u32[]{:S(2)}) collective-permute-start(bf16[8,64,1024]{2,1,0:T(8,128)(2,1)S(1)} %collective-permute-done.7.refs_9_), channel_id=1, source_target_pairs={{0,32},{32,0},{1,33},{33,1},{2,34},{34,2},{3,35},{35,3},{4,36},{36... | collective-permute-start | bytes 3145736 | tf_op jit(solution)/shard_map/ppermute | solution.py:128
  68.4 1.9 %collective-permute-start = (bf16[512,256]{1,0:T(8,128)(2,1)}, bf16[512,256]{1,0:T(8,128)(2,1)S(1)}, u32[]{:S(2)}, u32[]{:S(2)}) collective-permute-start(bf16[512,256]{1,0:T(8,128)(2,1)} %refs_0_.1), channel_id=1, source_target_pairs={{0,2},{1,3},{2,4},{3,5},{4,6},{5,7},{6,0},{7,1},{8,10},{9,11},{10,... | collective-permute-start | bytes 786440 | tf_op jit(solution)/shard_map/ppermute | solution.py:21
  70.3 5.5 %collective-permute-start.1 = (bf16[512,256]{1,0:T(8,128)(2,1)}, bf16[512,256]{1,0:T(8,128)(2,1)S(1)}, u32[]{:S(2)}, u32[]{:S(2)}) collective-permute-start(bf16[512,256]{1,0:T(8,128)(2,1)} %refs_0_.1), channel_id=1, source_target_pairs={{0,6},{1,7},{2,0},{3,1},{4,2},{5,3},{6,4},{7,5},{8,14},{9,15},{10,... | collective-permute-start | bytes 786440 | tf_op jit(solution)/shard_map/ppermute | solution.py:21
  75.8 1.9 %collective-permute-start.2 = (bf16[512,256]{1,0:T(8,128)(2,1)}, bf16[512,256]{1,0:T(8,128)(2,1)S(1)}, u32[]{:S(2)}, u32[]{:S(2)}) collective-permute-start(bf16[512,256]{1,0:T(8,128)(2,1)} %refs_0_.1), channel_id=1, source_target_pairs={{0,4},{1,5},{2,6},{3,7},{4,0},{5,1},{6,2},{7,3},{8,12},{9,13},{10,... | collective-permute-start | bytes 786440 | tf_op jit(solution)/shard_map/ppermute | solution.py:21
  77.7 4.5 %collective-permute-done.refs_1_ = bf16[512,256]{1,0:T(8,128)(2,1)S(1)} collective-permute-done((bf16[512,256]{1,0:T(8,128)(2,1)}, bf16[512,256]{1,0:T(8,128)(2,1)S(1)}, u32[]{:S(2)}, u32[]{:S(2)}) %collective-permute-start) | collective-permute-done | bytes 262176 | tf_op jit(solution)/shard_map/ppermute | solution.py:21
  82.2 1.9 %collective-permute-start.3 = (bf16[512,256]{1,0:T(8,128)(2,1)}, bf16[512,256]{1,0:T(8,128)(2,1)S(1)}, u32[]{:S(2)}, u32[]{:S(2)}) collective-permute-start(bf16[512,256]{1,0:T(8,128)(2,1)} %refs_0_.1), channel_id=1, source_target_pairs={{0,1},{1,2},{2,3},{3,4},{4,5},{5,6},{6,7},{7,0},{32,39},{33,32},{3... | collective-permute-start | bytes 786440 | tf_op jit(solution)/shard_map/ppermute | solution.py:123
  84.2 5.0 %collective-permute-done.1.refs_2_ = bf16[512,256]{1,0:T(8,128)(2,1)S(1)} collective-permute-done((bf16[512,256]{1,0:T(8,128)(2,1)}, bf16[512,256]{1,0:T(8,128)(2,1)S(1)}, u32[]{:S(2)}, u32[]{:S(2)}) %collective-permute-start.1) | collective-permute-done | bytes 262176 | tf_op jit(solution)/shard_map/ppermute | solution.py:21
  89.1 1.9 %collective-permute-start.4 = (bf16[512,256]{1,0:T(8,128)(2,1)S(1)}, bf16[512,256]{1,0:T(8,128)(2,1)S(1)}, u32[]{:S(2)}, u32[]{:S(2)}) collective-permute-start(bf16[512,256]{1,0:T(8,128)(2,1)S(1)} %collective-permute-done.refs_1_), channel_id=1, source_target_pairs={{0,1},{1,2},{2,3},{3,4},{4,5},{5,6},{6,7},{7,0},{32,39},{33,32},{3... | collective-permute-start | bytes 786440 | tf_op jit(solution)/shard_map/ppermute | solution.py:123
  91.1 0.7 collective-permute-done.2.refs_3_
  91.8 4.9 %collective-permute-start.5 = (bf16[512,256]{1,0:T(8,128)(2,1)S(1)}, bf16[512,256]{1,0:T(8,128)(2,1)S(1)}, u32[]{:S(2)}, u32[]{:S(2)}) collective-permute-start(bf16[512,256]{1,0:T(8,128)(2,1)S(1)} %collective-permute-done.1.refs_2_), channel_id=1, source_target_pairs={{0,1},{1,2},{2,3},{3,4},{4,5},{5,6},{6,7},{7,0},{32,39},{33,32},{3... | collective-permute-start | bytes 786440 | tf_op jit(solution)/shard_map/ppermute | solution.py:123
  96.7 0.0 collective-permute-done.3.given
  96.7 4.0 %collective-permute-start.6 = (bf16[512,256]{1,0:T(8,128)(2,1)S(1)}, bf16[512,256]{1,0:T(8,128)(2,1)S(1)}, u32[]{:S(2)}, u32[]{:S(2)}) collective-permute-start(bf16[512,256]{1,0:T(8,128)(2,1)S(1)} %collective-permute-done.2.refs_3_), channel_id=1, source_target_pairs={{0,1},{1,2},{2,3},{3,4},{4,5},{5,6},{6,7},{7,0},{32,39},{33,32},{3... | collective-permute-start | bytes 786440 | tf_op jit(solution)/shard_map/ppermute | solution.py:123
  100.7 0.0 collective-permute-done.4.refs_5_
  100.7 2.1 %collective-permute-done.5.refs_6_ = bf16[512,256]{1,0:T(8,128)(2,1)S(1)} collective-permute-done((bf16[512,256]{1,0:T(8,128)(2,1)S(1)}, bf16[512,256]{1,0:T(8,128)(2,1)S(1)}, u32[]{:S(2)}, u32[]{:S(2)}) %collective-permute-start.5) | collective-permute-done | bytes 262176 | tf_op jit(solution)/shard_map/ppermute | solution.py:123
  102.8 2.7 %collective-permute-done.6.refs_7_ = bf16[512,256]{1,0:T(8,128)(2,1)S(1)} collective-permute-done((bf16[512,256]{1,0:T(8,128)(2,1)S(1)}, bf16[512,256]{1,0:T(8,128)(2,1)S(1)}, u32[]{:S(2)}, u32[]{:S(2)}) %collective-permute-start.6) | collective-permute-done | bytes 262176 | tf_op jit(solution)/shard_map/ppermute | solution.py:123
  105.5 0.0 collective-permute-done.8.refs_10_
  105.5 0.0 collective-permute-done.9.refs_11_
  105.5 0.0 copy-start
  105.5 0.9 copy-done
  106.5 1.4 shard_map.29
  107.9 1.9 %shard_map.30 = (f32[512,256]{1,0:T(8,128)S(1)}, f32[512,256]{1,0:T(8,128)S(1)}, f32[512,256]{1,0:T(8,128)S(1)}) custom-call(bf16[512,2048]{1,0:T(8,128)(2,1)S(1)} %get-tuple-element.11.a_all, bf16[2048,1024]{1,0:T(8,128)(2,1)S(1)} %get-tuple-element.12.v_all), custom_call_target="tpu_custom_call" | custom-call | flops 1610612736 | bytes 8388608 | tf_op jit(solution)/shard_map/pallas_call | solution.py:86
  109.8 7.2 %collective-permute-start.10 = (f16[512,256]{1,0:T(8,128)(2,1)S(1)}, f16[512,256]{1,0:T(8,128)(2,1)S(1)}, u32[]{:S(2)}, u32[]{:S(2)}) collective-permute-start(f16[512,256]{1,0:T(8,128)(2,1)S(1)} %convert_element_type.18), channel_id=1, source_target_pairs={{0,8},{8,16},{16,24},{24,0},{1,9},{9,17},{17,25},{25,1},{2,10},{10... | collective-permute-start | bytes 786440 | tf_op jit(solution)/shard_map/ppermute | solution.py:26
  117.0 24.9 %collective-permute-start.11 = (f16[512,256]{1,0:T(8,128)(2,1)S(1)}, f16[512,256]{1,0:T(8,128)(2,1)S(1)}, u32[]{:S(2)}, u32[]{:S(2)}) collective-permute-start(f16[512,256]{1,0:T(8,128)(2,1)S(1)} %convert_element_type.20), channel_id=1, source_target_pairs={{0,24},{8,0},{16,8},{24,16},{1,25},{9,1},{17,9},{25,17},{2,26},{10... | collective-permute-start | bytes 786440 | tf_op jit(solution)/shard_map/ppermute | solution.py:26
  141.9 4.0 %collective-permute-start.12 = (f16[512,256]{1,0:T(8,128)(2,1)S(1)}, f16[512,256]{1,0:T(8,128)(2,1)S(1)}, u32[]{:S(2)}, u32[]{:S(2)}) collective-permute-start(f16[512,256]{1,0:T(8,128)(2,1)S(1)} %convert_element_type.22), channel_id=1, source_target_pairs={{0,16},{8,24},{16,0},{24,8},{1,17},{9,25},{17,1},{25,9},{2,18},{10... | collective-permute-start | bytes 786440 | tf_op jit(solution)/shard_map/ppermute | solution.py:26
  146.0 0.0 collective-permute-done.10
  146.0 18.4 %collective-permute-done.11 = f16[512,256]{1,0:T(8,128)(2,1)S(1)} collective-permute-done((f16[512,256]{1,0:T(8,128)(2,1)S(1)}, f16[512,256]{1,0:T(8,128)(2,1)S(1)}, u32[]{:S(2)}, u32[]{:S(2)}) %collective-permute-start.11) | collective-permute-done | bytes 262176 | tf_op jit(solution)/shard_map/ppermute | solution.py:26
  164.4 0.0 collective-permute-done.12
  164.4 0.9 multiply_select_fusion
  (5 shorter events, 0.1 us)
Async XLA Ops:
  34.3 18.1 %collective-permute-start.7 = (bf16[8,64,1024]{2,1,0:T(8,128)(2,1)S(1)}, bf16[8,64,1024]{2,1,0:T(8,128)(2,1)S(1)}, u32[]{:S(2)}, u32[]{:S(2)}) collective-permute-start(bf16[8,64,1024]{2,1,0:T(8,128)(2,1)S(1)} %all_to_all.5.refs_8_), channel_id=1, source_target_pairs={{0,64},{64,128},{128,192},{192,256},{256,320},{320,384},{384,448},... | collective-permute-start | bytes 3145736 | tf_op jit(solution)/shard_map/ppermute | solution.py:126
  36.2 69.3 %collective-permute-start.8 = (bf16[8,64,1024]{2,1,0:T(8,128)(2,1)S(1)}, bf16[8,64,1024]{2,1,0:T(8,128)(2,1)S(1)}, u32[]{:S(2)}, u32[]{:S(2)}) collective-permute-start(bf16[8,64,1024]{2,1,0:T(8,128)(2,1)S(1)} %all_to_all.5.refs_8_), channel_id=1, source_target_pairs={{0,32},{32,0},{1,33},{33,1},{2,34},{34,2},{3,35},{35,3},{4,36},{36... | collective-permute-start | bytes 3145736 | tf_op jit(solution)/shard_map/ppermute | solution.py:127
  52.4 53.1 %collective-permute-start.9 = (bf16[8,64,1024]{2,1,0:T(8,128)(2,1)S(1)}, bf16[8,64,1024]{2,1,0:T(8,128)(2,1)S(1)}, u32[]{:S(2)}, u32[]{:S(2)}) collective-permute-start(bf16[8,64,1024]{2,1,0:T(8,128)(2,1)S(1)} %collective-permute-done.7.refs_9_), channel_id=1, source_target_pairs={{0,32},{32,0},{1,33},{33,1},{2,34},{34,2},{3,35},{35,3},{4,36},{36... | collective-permute-start | bytes 3145736 | tf_op jit(solution)/shard_map/ppermute | solution.py:128
  68.4 13.9 %collective-permute-start = (bf16[512,256]{1,0:T(8,128)(2,1)}, bf16[512,256]{1,0:T(8,128)(2,1)S(1)}, u32[]{:S(2)}, u32[]{:S(2)}) collective-permute-start(bf16[512,256]{1,0:T(8,128)(2,1)} %refs_0_.1), channel_id=1, source_target_pairs={{0,2},{1,3},{2,4},{3,5},{4,6},{5,7},{6,0},{7,1},{8,10},{9,11},{10,... | collective-permute-start | bytes 786440 | tf_op jit(solution)/shard_map/ppermute | solution.py:21
  70.3 18.8 %collective-permute-start.1 = (bf16[512,256]{1,0:T(8,128)(2,1)}, bf16[512,256]{1,0:T(8,128)(2,1)S(1)}, u32[]{:S(2)}, u32[]{:S(2)}) collective-permute-start(bf16[512,256]{1,0:T(8,128)(2,1)} %refs_0_.1), channel_id=1, source_target_pairs={{0,6},{1,7},{2,0},{3,1},{4,2},{5,3},{6,4},{7,5},{8,14},{9,15},{10,... | collective-permute-start | bytes 786440 | tf_op jit(solution)/shard_map/ppermute | solution.py:21
  75.8 16.0 %collective-permute-start.2 = (bf16[512,256]{1,0:T(8,128)(2,1)}, bf16[512,256]{1,0:T(8,128)(2,1)S(1)}, u32[]{:S(2)}, u32[]{:S(2)}) collective-permute-start(bf16[512,256]{1,0:T(8,128)(2,1)} %refs_0_.1), channel_id=1, source_target_pairs={{0,4},{1,5},{2,6},{3,7},{4,0},{5,1},{6,2},{7,3},{8,12},{9,13},{10,... | collective-permute-start | bytes 786440 | tf_op jit(solution)/shard_map/ppermute | solution.py:21
  82.2 14.4 %collective-permute-start.3 = (bf16[512,256]{1,0:T(8,128)(2,1)}, bf16[512,256]{1,0:T(8,128)(2,1)S(1)}, u32[]{:S(2)}, u32[]{:S(2)}) collective-permute-start(bf16[512,256]{1,0:T(8,128)(2,1)} %refs_0_.1), channel_id=1, source_target_pairs={{0,1},{1,2},{2,3},{3,4},{4,5},{5,6},{6,7},{7,0},{32,39},{33,32},{3... | collective-permute-start | bytes 786440 | tf_op jit(solution)/shard_map/ppermute | solution.py:123
  89.1 11.6 %collective-permute-start.4 = (bf16[512,256]{1,0:T(8,128)(2,1)S(1)}, bf16[512,256]{1,0:T(8,128)(2,1)S(1)}, u32[]{:S(2)}, u32[]{:S(2)}) collective-permute-start(bf16[512,256]{1,0:T(8,128)(2,1)S(1)} %collective-permute-done.refs_1_), channel_id=1, source_target_pairs={{0,1},{1,2},{2,3},{3,4},{4,5},{5,6},{6,7},{7,0},{32,39},{33,32},{3... | collective-permute-start | bytes 786440 | tf_op jit(solution)/shard_map/ppermute | solution.py:123
  91.8 11.0 %collective-permute-start.5 = (bf16[512,256]{1,0:T(8,128)(2,1)S(1)}, bf16[512,256]{1,0:T(8,128)(2,1)S(1)}, u32[]{:S(2)}, u32[]{:S(2)}) collective-permute-start(bf16[512,256]{1,0:T(8,128)(2,1)S(1)} %collective-permute-done.1.refs_2_), channel_id=1, source_target_pairs={{0,1},{1,2},{2,3},{3,4},{4,5},{5,6},{6,7},{7,0},{32,39},{33,32},{3... | collective-permute-start | bytes 786440 | tf_op jit(solution)/shard_map/ppermute | solution.py:123
  96.7 8.8 %collective-permute-start.6 = (bf16[512,256]{1,0:T(8,128)(2,1)S(1)}, bf16[512,256]{1,0:T(8,128)(2,1)S(1)}, u32[]{:S(2)}, u32[]{:S(2)}) collective-permute-start(bf16[512,256]{1,0:T(8,128)(2,1)S(1)} %collective-permute-done.2.refs_3_), channel_id=1, source_target_pairs={{0,1},{1,2},{2,3},{3,4},{4,5},{5,6},{6,7},{7,0},{32,39},{33,32},{3... | collective-permute-start | bytes 786440 | tf_op jit(solution)/shard_map/ppermute | solution.py:123
  105.5 1.0 copy-start
  109.8 36.2 %collective-permute-start.10 = (f16[512,256]{1,0:T(8,128)(2,1)S(1)}, f16[512,256]{1,0:T(8,128)(2,1)S(1)}, u32[]{:S(2)}, u32[]{:S(2)}) collective-permute-start(f16[512,256]{1,0:T(8,128)(2,1)S(1)} %convert_element_type.18), channel_id=1, source_target_pairs={{0,8},{8,16},{16,24},{24,0},{1,9},{9,17},{17,25},{25,1},{2,10},{10... | collective-permute-start | bytes 786440 | tf_op jit(solution)/shard_map/ppermute | solution.py:26
  117.0 47.4 %collective-permute-start.11 = (f16[512,256]{1,0:T(8,128)(2,1)S(1)}, f16[512,256]{1,0:T(8,128)(2,1)S(1)}, u32[]{:S(2)}, u32[]{:S(2)}) collective-permute-start(f16[512,256]{1,0:T(8,128)(2,1)S(1)} %convert_element_type.20), channel_id=1, source_target_pairs={{0,24},{8,0},{16,8},{24,16},{1,25},{9,1},{17,9},{25,17},{2,26},{10... | collective-permute-start | bytes 786440 | tf_op jit(solution)/shard_map/ppermute | solution.py:26
  141.9 22.5 %collective-permute-start.12 = (f16[512,256]{1,0:T(8,128)(2,1)S(1)}, f16[512,256]{1,0:T(8,128)(2,1)S(1)}, u32[]{:S(2)}, u32[]{:S(2)}) collective-permute-start(f16[512,256]{1,0:T(8,128)(2,1)S(1)} %convert_element_type.22), channel_id=1, source_target_pairs={{0,16},{8,24},{16,0},{24,8},{1,17},{9,25},{17,1},{25,9},{2,18},{10... | collective-permute-start | bytes 786440 | tf_op jit(solution)/shard_map/ppermute | solution.py:26

commit v4 on v2

--- a/solution.py
+++ b/solution.py
@@ -12,24 +12,24 @@
 SCALE = 64.0
 
 X_PARITY = [[zl * 8 + x for zl in range(2) for x in range(p, 8, 2)] for p in range(2)]
-Y_HOP = [(c * 8 + y, c * 8 + (y + 1 - 2 * c) % 8) for c in range(2) for y in range(8)]
 X_HOP = [(x * 2 + c, (x + 1 - 2 * c) % 8 * 2 + c) for c in range(2) for x in range(8)]
 SWAP = [(0, 1), (1, 0)]
 
 
-def along_y(shard, step):
-    return lax.ppermute(shard, "ij", [(y, (y + step) % 8) for y in range(8)])
+def along_y(shard, hops):
+    pairs = [
+        (c * 8 + y, c * 8 + (y + hops * (1 - 2 * c)) % 8)
+        for c in range(2) for y in range(8)
+    ]
+    return lax.ppermute(shard, ("c", "ij"), pairs)
 
 
 def product_kernel(*refs):
     a_refs, v_refs, (out, own, a_all, v_all) = refs[:8], refs[8:12], refs[12:]
     x, y, c = (lax.axis_index(name) for name in ("x", "ij", "c"))
     kl = lax.axis_index("kl")
-    near = 2 * c - 1
-    places = [0, -2, 2, 4]
-    places += [near + place for place in places]
-    for place, ref in zip(places, a_refs):
-        start = pl.multiple_of((y + place + 16) % 8 * 256, 256)
+    for place, ref in zip((0, 2, 4, 6, 1, 3, 5, 7), a_refs):
+        start = pl.multiple_of((y + (2 * c - 1) * place + 8) % 8 * 256, 256)
         a_all[:, pl.ds(start, 256)] = ref[...]
     for s, t, ref in ((0, 0, v_refs[0]), (1, 0, v_refs[1]), (0, 1, v_refs[2]), (1, 1, v_refs[3])):
         offset = (x + s) % 2 * 128 + (c + t) % 2 * 64
@@ -39,7 +39,13 @@
 
     @pl.when(kl == 3)
     def _():
-        v_all[pl.ds(1984, 64), :] = jnp.zeros((64, 1024), jnp.bfloat16)
+        v_all[PAIRS - 6144 :, :] = jnp.zeros((8192 - PAIRS, 1024), jnp.bfloat16)
+
+    @pl.when(y == 7)
+    def _():
+        kept = lax.broadcasted_iota(jnp.int32, (2048, 128), 1) < PAIRS - 7168 - 896
+        last = v_all[:, 896:].astype(jnp.float32)
+        v_all[:, 896:] = jnp.where(kept, last, 0.0).astype(jnp.bfloat16)
 
     for k in range(4):
         out[k] = SCALE * jnp.dot(
@@ -47,6 +53,10 @@
             preferred_element_type=jnp.float32,
         )
     own[...] = out[kl]
+    out[kl] = jnp.zeros((512, 256), jnp.float32)
+
+
+VMEM = pl.BlockSpec(memory_space=pltpu.VMEM)
 
 
 def product(*pieces):
@@ -56,8 +66,8 @@
             jax.ShapeDtypeStruct((4, 512, 256), jnp.float32),
             jax.ShapeDtypeStruct((512, 256), jnp.float32),
         ),
-        in_specs=[pl.BlockSpec(memory_space=pltpu.VMEM)] * 12,
-        out_specs=[pl.BlockSpec(memory_space=pltpu.VMEM)] * 2,
+        in_specs=[VMEM] * 12,
+        out_specs=[VMEM] * 2,
         scratch_shapes=[
             pltpu.VMEM((512, 2048), jnp.bfloat16),
             pltpu.VMEM((2048, 1024), jnp.bfloat16),
@@ -91,24 +101,20 @@
         tiled=True, axis_index_groups=X_PARITY,
     )
     blocks = [amplitudes]
-    for step in (2, -2, 4):
-        blocks.append(along_y(amplitudes, step))
+    for i in range(3):
+        blocks.append(along_y(blocks[i], 2))
     for i in range(4):
-        blocks.append(lax.ppermute(blocks[i], ("c", "ij"), Y_HOP))
+        block = along_y(blocks[i], 1)
         if i == 0:
-            blocks[4] = untouched(blocks[4])
+            block = untouched(block)
+        blocks.append(block)
     v10 = lax.ppermute(v00, ("x", "c"), X_HOP)
     v01 = lax.ppermute(v00, "c", SWAP)
     v11 = lax.ppermute(v10, "c", SWAP)
     terms, own = product(*blocks, v00, v10, v01, v11)
-    terms = terms.astype(jnp.float16)
-    kl = lax.axis_index("kl")
-    got = lax.all_to_all(terms, "kl", 0, 0, tiled=True)
-    total = own
-    for k in range(4):
-        total = total + jnp.where(kl == k, 0.0, got[k].astype(jnp.float32))
-    out_ids = lax.axis_index("ij") * 1024 + kl * 256 + jnp.arange(256)
-    return jnp.where((out_ids < PAIRS)[None, :], total * (1.0 / SCALE), jnp.float32(0.0))
+    got = lax.all_to_all(terms.astype(jnp.float16), "kl", 0, 0, tiled=True)
+    got = got.astype(jnp.float32)
+    return ((got[0] + got[1]) + (got[2] + got[3]) + own) * (1.0 / SCALE)
 
 
 def solution(mesh):

time: 167 us -> 151 us (0.904)
  the two profiles are of different devices: /device:TPU:1 before, /device:TPU:2 now
where the time goes in v4:
time: 151 us
  blocking collectives  85 us (56%)
  starting transfers between devices  31.5 us (21%)
  waiting for transfers between devices  28.6 us (19%)
  Pallas kernels  3.07 us (2%)
    all_to_all x1, blocking collectives, staged(): got = lax.all_to_all(terms.astype(jnp.float16), 'kl', 0, 0, tiled=True)  51.4 us
    all_to_all x1, blocking collectives, staged(): lax.all_to_all(jnp.broadcast_to(integrals[None], (8, 64, 1024)), ('zl', '...  33.6 us
    ppermute x7, waiting for transfers between devices, along_y(): return lax.ppermute(shard, ('c', 'ij'), pairs)  18.8 us
    ppermute x1, starting transfers between devices, staged(): v10 = lax.ppermute(v00, ('x', 'c'), X_HOP)  14 us
    ppermute x7, starting transfers between devices, along_y(): return lax.ppermute(shard, ('c', 'ij'), pairs)  13.6 us
    ppermute x1, waiting for transfers between devices, staged(): v10 = lax.ppermute(v00, ('x', 'c'), X_HOP)  9.8 us
    pallas_call x1, Pallas kernels, product(): pl.pallas_call(product_kernel, out_shape=(jax.ShapeDtypeStruct((4, 512, 2...  3.07 us
  transfers between devices with their start and end apart: 10, of which 6 were waited for; matrix products, arithmetic and copies ran while one was open for 0% of the time, Pallas kernels for 0%

profile of v4, /device:TPU:2, one launch (start us, length us, event | category | flops | bytes accessed | tf_op | source)
XLA Modules:
  0.0 150.7 jit_solution(323809619783359291)
XLA Ops:
  0.0 0.0 copy-start
  0.0 1.1 broadcast_in_dim.2
  1.1 33.6 %all_to_all.10.refs_8_ = bf16[8,64,1024]{2,1,0:T(8,128)(2,1)S(1)} all-to-all(bf16[8,64,1024]{2,1,0:T(8,128)(2,1)S(1)} %broadcast_in_dim.2), channel_id=1, replica_groups={{0,128,256,384,512,640,768,896},{64,192,320,448,576,704,832,960},{1,129..., dimensions={0} | all-to-all | bytes 2097152 | tf_op jit(solution)/shard_map/all_to_all | solution.py:99
  34.7 14.0 %collective-permute-start.7 = (bf16[8,64,1024]{2,1,0:T(8,128)(2,1)S(1)}, bf16[8,64,1024]{2,1,0:T(8,128)(2,1)S(1)}, u32[]{:S(2)}, u32[]{:S(2)}) collective-permute-start(bf16[8,64,1024]{2,1,0:T(8,128)(2,1)S(1)} %all_to_all.10.refs_8_), channel_id=1, source_target_pairs={{0,64},{64,128},{128,192},{192,256},{256,320},{320,384},{384,448},... | collective-permute-start | bytes 3145736 | tf_op jit(solution)/shard_map/ppermute | solution.py:111
  48.7 0.0 copy-done
  48.7 1.9 %collective-permute-start = (bf16[512,256]{1,0:T(8,128)(2,1)S(1)}, bf16[512,256]{1,0:T(8,128)(2,1)S(1)}, u32[]{:S(2)}, u32[]{:S(2)}) collective-permute-start(bf16[512,256]{1,0:T(8,128)(2,1)S(1)} %copy-done), channel_id=1, source_target_pairs={{0,2},{1,3},{2,4},{3,5},{4,6},{5,7},{6,0},{7,1},{32,38},{33,39},{3... | collective-permute-start | bytes 786440 | tf_op jit(solution)/shard_map/ppermute | solution.py:24
  50.6 1.9 %collective-permute-start.8 = (bf16[8,64,1024]{2,1,0:T(8,128)(2,1)S(1)}, bf16[8,64,1024]{2,1,0:T(8,128)(2,1)S(1)}, u32[]{:S(2)}, u32[]{:S(2)}) collective-permute-start(bf16[8,64,1024]{2,1,0:T(8,128)(2,1)S(1)} %all_to_all.10.refs_8_), channel_id=1, source_target_pairs={{0,32},{32,0},{1,33},{33,1},{2,34},{34,2},{3,35},{35,3},{4,36},{36... | collective-permute-start | bytes 3145736 | tf_op jit(solution)/shard_map/ppermute | solution.py:112
  52.6 9.8 %collective-permute-done.7.refs_9_ = bf16[8,64,1024]{2,1,0:T(8,128)(2,1)S(1)} collective-permute-done((bf16[8,64,1024]{2,1,0:T(8,128)(2,1)S(1)}, bf16[8,64,1024]{2,1,0:T(8,128)(2,1)S(1)}, u32[]{:S(2)}, u32[]{:S(2)}) %collective-permute-start.7) | collective-permute-done | bytes 1048608 | tf_op jit(solution)/shard_map/ppermute | solution.py:111
  62.4 1.9 %collective-permute-start.9 = (bf16[8,64,1024]{2,1,0:T(8,128)(2,1)S(1)}, bf16[8,64,1024]{2,1,0:T(8,128)(2,1)S(1)}, u32[]{:S(2)}, u32[]{:S(2)}) collective-permute-start(bf16[8,64,1024]{2,1,0:T(8,128)(2,1)S(1)} %collective-permute-done.7.refs_9_), channel_id=1, source_target_pairs={{0,32},{32,0},{1,33},{33,1},{2,34},{34,2},{3,35},{35,3},{4,36},{36... | collective-permute-start | bytes 3145736 | tf_op jit(solution)/shard_map/ppermute | solution.py:113
  64.3 0.0 collective-permute-done.refs_1_
  64.3 1.9 %collective-permute-start.1 = (bf16[512,256]{1,0:T(8,128)(2,1)S(1)}, bf16[512,256]{1,0:T(8,128)(2,1)S(1)}, u32[]{:S(2)}, u32[]{:S(2)}) collective-permute-start(bf16[512,256]{1,0:T(8,128)(2,1)S(1)} %collective-permute-done.refs_1_), channel_id=1, source_target_pairs={{0,2},{1,3},{2,4},{3,5},{4,6},{5,7},{6,0},{7,1},{32,38},{33,39},{3... | collective-permute-start | bytes 786440 | tf_op jit(solution)/shard_map/ppermute | solution.py:24
  66.2 1.9 %collective-permute-start.3 = (bf16[512,256]{1,0:T(8,128)(2,1)S(1)}, bf16[512,256]{1,0:T(8,128)(2,1)S(1)}, u32[]{:S(2)}, u32[]{:S(2)}) collective-permute-start(bf16[512,256]{1,0:T(8,128)(2,1)S(1)} %copy-done), channel_id=1, source_target_pairs={{0,1},{1,2},{2,3},{3,4},{4,5},{5,6},{6,7},{7,0},{32,39},{33,32},{3... | collective-permute-start | bytes 786440 | tf_op jit(solution)/shard_map/ppermute | solution.py:24
  68.2 6.6 %collective-permute-done.1.refs_2_ = bf16[512,256]{1,0:T(8,128)(2,1)S(1)} collective-permute-done((bf16[512,256]{1,0:T(8,128)(2,1)S(1)}, bf16[512,256]{1,0:T(8,128)(2,1)S(1)}, u32[]{:S(2)}, u32[]{:S(2)}) %collective-permute-start.1) | collective-permute-done | bytes 262176 | tf_op jit(solution)/shard_map/ppermute | solution.py:24
  74.8 1.9 %collective-permute-start.2 = (bf16[512,256]{1,0:T(8,128)(2,1)S(1)}, bf16[512,256]{1,0:T(8,128)(2,1)S(1)}, u32[]{:S(2)}, u32[]{:S(2)}) collective-permute-start(bf16[512,256]{1,0:T(8,128)(2,1)S(1)} %collective-permute-done.1.refs_2_), channel_id=1, source_target_pairs={{0,2},{1,3},{2,4},{3,5},{4,6},{5,7},{6,0},{7,1},{32,38},{33,39},{3... | collective-permute-start | bytes 786440 | tf_op jit(solution)/shard_map/ppermute | solution.py:24
  76.7 1.9 %collective-permute-start.4 = (bf16[512,256]{1,0:T(8,128)(2,1)S(1)}, bf16[512,256]{1,0:T(8,128)(2,1)S(1)}, u32[]{:S(2)}, u32[]{:S(2)}) collective-permute-start(bf16[512,256]{1,0:T(8,128)(2,1)S(1)} %collective-permute-done.refs_1_), channel_id=1, source_target_pairs={{0,1},{1,2},{2,3},{3,4},{4,5},{5,6},{6,7},{7,0},{32,39},{33,32},{3... | collective-permute-start | bytes 786440 | tf_op jit(solution)/shard_map/ppermute | solution.py:24
  78.6 0.0 collective-permute-done.3.given
  78.6 2.1 %collective-permute-start.5 = (bf16[512,256]{1,0:T(8,128)(2,1)S(1)}, bf16[512,256]{1,0:T(8,128)(2,1)S(1)}, u32[]{:S(2)}, u32[]{:S(2)}) collective-permute-start(bf16[512,256]{1,0:T(8,128)(2,1)S(1)} %collective-permute-done.1.refs_2_), channel_id=1, source_target_pairs={{0,1},{1,2},{2,3},{3,4},{4,5},{5,6},{6,7},{7,0},{32,39},{33,32},{3... | collective-permute-start | bytes 786440 | tf_op jit(solution)/shard_map/ppermute | solution.py:24
  80.7 4.7 %collective-permute-done.2.refs_3_ = bf16[512,256]{1,0:T(8,128)(2,1)S(1)} collective-permute-done((bf16[512,256]{1,0:T(8,128)(2,1)S(1)}, bf16[512,256]{1,0:T(8,128)(2,1)S(1)}, u32[]{:S(2)}, u32[]{:S(2)}) %collective-permute-start.2) | collective-permute-done | bytes 262176 | tf_op jit(solution)/shard_map/ppermute | solution.py:24
  85.4 1.9 %collective-permute-start.6 = (bf16[512,256]{1,0:T(8,128)(2,1)S(1)}, bf16[512,256]{1,0:T(8,128)(2,1)S(1)}, u32[]{:S(2)}, u32[]{:S(2)}) collective-permute-start(bf16[512,256]{1,0:T(8,128)(2,1)S(1)} %collective-permute-done.2.refs_3_), channel_id=1, source_target_pairs={{0,1},{1,2},{2,3},{3,4},{4,5},{5,6},{6,7},{7,0},{32,39},{33,32},{3... | collective-permute-start | bytes 786440 | tf_op jit(solution)/shard_map/ppermute | solution.py:24
  87.4 0.8 collective-permute-done.4.refs_5_
  88.1 2.8 %collective-permute-done.5.refs_6_ = bf16[512,256]{1,0:T(8,128)(2,1)S(1)} collective-permute-done((bf16[512,256]{1,0:T(8,128)(2,1)S(1)}, bf16[512,256]{1,0:T(8,128)(2,1)S(1)}, u32[]{:S(2)}, u32[]{:S(2)}) %collective-permute-start.5) | collective-permute-done | bytes 262176 | tf_op jit(solution)/shard_map/ppermute | solution.py:24
  90.9 3.9 %collective-permute-done.6.refs_7_ = bf16[512,256]{1,0:T(8,128)(2,1)S(1)} collective-permute-done((bf16[512,256]{1,0:T(8,128)(2,1)S(1)}, bf16[512,256]{1,0:T(8,128)(2,1)S(1)}, u32[]{:S(2)}, u32[]{:S(2)}) %collective-permute-start.6) | collective-permute-done | bytes 262176 | tf_op jit(solution)/shard_map/ppermute | solution.py:24
  94.9 0.0 collective-permute-done.8.refs_10_
  94.9 0.0 collective-permute-done.9.refs_11_
  94.9 3.1 %shard_map.29 = (f32[4,512,256]{2,1,0:T(8,128)S(1)}, f32[512,256]{1,0:T(8,128)S(1)}) custom-call(bf16[512,256]{1,0:T(8,128)(2,1)S(1)} %copy-done, bf16[512,256]{1,0:T(8,128)(2,1)S(1)} %collective-permute-done.refs_1_, bf16[512,256]{1,0:T(8,128)(2,1)S(1)} %collective-permute-done.1.refs_2_, bf16[512,256]{1,0:T(8,128)(2,1)S(1)} %collective-permute-done.2.refs_3_, ...), custom_call_target="tpu_custom_call" | custom-call | flops 2147483648 | bytes 8388608 | tf_op jit(solution)/shard_map/pallas_call | solution.py:63
  98.0 0.2 convert_element_type.6
  98.2 51.4 %all_to_all.11 = f16[4,512,256]{2,1,0:T(8,128)(2,1)S(1)} all-to-all(f16[4,512,256]{2,1,0:T(8,128)(2,1)S(1)} %convert_element_type.6), channel_id=1, replica_groups=mesh['zl'=2,'x'=8,'c'=2,'kl'=4,'ij'=8] {'kl'}, dimensions={0} | all-to-all | bytes 2097152 | tf_op jit(solution)/shard_map/all_to_all | solution.py:115
  149.6 0.2 convert_element_type.7
  149.8 1.0 fusion.3
  (1 shorter events, 0.0 us)
Async XLA Ops:
  0.0 48.7 %copy-start = (bf16[512,256]{1,0:T(8,128)(2,1)S(1)}, bf16[512,256]{1,0:T(8,128)(2,1)}, u32[]{:S(2)}) copy-start(bf16[512,256]{1,0:T(8,128)(2,1)} %refs_0_.1) | copy-start | bytes 786436
  34.7 27.7 %collective-permute-start.7 = (bf16[8,64,1024]{2,1,0:T(8,128)(2,1)S(1)}, bf16[8,64,1024]{2,1,0:T(8,128)(2,1)S(1)}, u32[]{:S(2)}, u32[]{:S(2)}) collective-permute-start(bf16[8,64,1024]{2,1,0:T(8,128)(2,1)S(1)} %all_to_all.10.refs_8_), channel_id=1, source_target_pairs={{0,64},{64,128},{128,192},{192,256},{256,320},{320,384},{384,448},... | collective-permute-start | bytes 3145736 | tf_op jit(solution)/shard_map/ppermute | solution.py:111
  48.7 15.6 %collective-permute-start = (bf16[512,256]{1,0:T(8,128)(2,1)S(1)}, bf16[512,256]{1,0:T(8,128)(2,1)S(1)}, u32[]{:S(2)}, u32[]{:S(2)}) collective-permute-start(bf16[512,256]{1,0:T(8,128)(2,1)S(1)} %copy-done), channel_id=1, source_target_pairs={{0,2},{1,3},{2,4},{3,5},{4,6},{5,7},{6,0},{7,1},{32,38},{33,39},{3... | collective-permute-start | bytes 786440 | tf_op jit(solution)/shard_map/ppermute | solution.py:24
  50.6 44.3 %collective-permute-start.8 = (bf16[8,64,1024]{2,1,0:T(8,128)(2,1)S(1)}, bf16[8,64,1024]{2,1,0:T(8,128)(2,1)S(1)}, u32[]{:S(2)}, u32[]{:S(2)}) collective-permute-start(bf16[8,64,1024]{2,1,0:T(8,128)(2,1)S(1)} %all_to_all.10.refs_8_), channel_id=1, source_target_pairs={{0,32},{32,0},{1,33},{33,1},{2,34},{34,2},{3,35},{35,3},{4,36},{36... | collective-permute-start | bytes 3145736 | tf_op jit(solution)/shard_map/ppermute | solution.py:112
  62.4 32.5 %collective-permute-start.9 = (bf16[8,64,1024]{2,1,0:T(8,128)(2,1)S(1)}, bf16[8,64,1024]{2,1,0:T(8,128)(2,1)S(1)}, u32[]{:S(2)}, u32[]{:S(2)}) collective-permute-start(bf16[8,64,1024]{2,1,0:T(8,128)(2,1)S(1)} %collective-permute-done.7.refs_9_), channel_id=1, source_target_pairs={{0,32},{32,0},{1,33},{33,1},{2,34},{34,2},{3,35},{35,3},{4,36},{36... | collective-permute-start | bytes 3145736 | tf_op jit(solution)/shard_map/ppermute | solution.py:113
  64.3 10.5 %collective-permute-start.1 = (bf16[512,256]{1,0:T(8,128)(2,1)S(1)}, bf16[512,256]{1,0:T(8,128)(2,1)S(1)}, u32[]{:S(2)}, u32[]{:S(2)}) collective-permute-start(bf16[512,256]{1,0:T(8,128)(2,1)S(1)} %collective-permute-done.refs_1_), channel_id=1, source_target_pairs={{0,2},{1,3},{2,4},{3,5},{4,6},{5,7},{6,0},{7,1},{32,38},{33,39},{3... | collective-permute-start | bytes 786440 | tf_op jit(solution)/shard_map/ppermute | solution.py:24
  66.2 12.4 %collective-permute-start.3 = (bf16[512,256]{1,0:T(8,128)(2,1)S(1)}, bf16[512,256]{1,0:T(8,128)(2,1)S(1)}, u32[]{:S(2)}, u32[]{:S(2)}) collective-permute-start(bf16[512,256]{1,0:T(8,128)(2,1)S(1)} %copy-done), channel_id=1, source_target_pairs={{0,1},{1,2},{2,3},{3,4},{4,5},{5,6},{6,7},{7,0},{32,39},{33,32},{3... | collective-permute-start | bytes 786440 | tf_op jit(solution)/shard_map/ppermute | solution.py:24
  74.8 10.7 %collective-permute-start.2 = (bf16[512,256]{1,0:T(8,128)(2,1)S(1)}, bf16[512,256]{1,0:T(8,128)(2,1)S(1)}, u32[]{:S(2)}, u32[]{:S(2)}) collective-permute-start(bf16[512,256]{1,0:T(8,128)(2,1)S(1)} %collective-permute-done.1.refs_2_), channel_id=1, source_target_pairs={{0,2},{1,3},{2,4},{3,5},{4,6},{5,7},{6,0},{7,1},{32,38},{33,39},{3... | collective-permute-start | bytes 786440 | tf_op jit(solution)/shard_map/ppermute | solution.py:24
  76.7 11.4 %collective-permute-start.4 = (bf16[512,256]{1,0:T(8,128)(2,1)S(1)}, bf16[512,256]{1,0:T(8,128)(2,1)S(1)}, u32[]{:S(2)}, u32[]{:S(2)}) collective-permute-start(bf16[512,256]{1,0:T(8,128)(2,1)S(1)} %collective-permute-done.refs_1_), channel_id=1, source_target_pairs={{0,1},{1,2},{2,3},{3,4},{4,5},{5,6},{6,7},{7,0},{32,39},{33,32},{3... | collective-permute-start | bytes 786440 | tf_op jit(solution)/shard_map/ppermute | solution.py:24
  78.6 12.3 %collective-permute-start.5 = (bf16[512,256]{1,0:T(8,128)(2,1)S(1)}, bf16[512,256]{1,0:T(8,128)(2,1)S(1)}, u32[]{:S(2)}, u32[]{:S(2)}) collective-permute-start(bf16[512,256]{1,0:T(8,128)(2,1)S(1)} %collective-permute-done.1.refs_2_), channel_id=1, source_target_pairs={{0,1},{1,2},{2,3},{3,4},{4,5},{5,6},{6,7},{7,0},{32,39},{33,32},{3... | collective-permute-start | bytes 786440 | tf_op jit(solution)/shard_map/ppermute | solution.py:24
  85.4 9.5 %collective-permute-start.6 = (bf16[512,256]{1,0:T(8,128)(2,1)S(1)}, bf16[512,256]{1,0:T(8,128)(2,1)S(1)}, u32[]{:S(2)}, u32[]{:S(2)}) collective-permute-start(bf16[512,256]{1,0:T(8,128)(2,1)S(1)} %collective-permute-done.2.refs_3_), channel_id=1, source_target_pairs={{0,1},{1,2},{2,3},{3,4},{4,5},{5,6},{6,7},{7,0},{32,39},{33,32},{3... | collective-permute-start | bytes 786440 | tf_op jit(solution)/shard_map/ppermute | solution.py:24

commit v5 on v4

--- a/solution.py
+++ b/solution.py
@@ -25,12 +25,14 @@
 
 
 def product_kernel(*refs):
-    a_refs, v_refs, (out, own, a_all, v_all) = refs[:8], refs[8:12], refs[12:]
+    a_refs, v_refs, (out, own, a_all, v_all) = refs[:6], refs[6:10], refs[10:]
     x, y, c = (lax.axis_index(name) for name in ("x", "ij", "c"))
     kl = lax.axis_index("kl")
-    for place, ref in zip((0, 2, 4, 6, 1, 3, 5, 7), a_refs):
+    a_blocks = [ref[...] for ref in a_refs[:4]]
+    a_blocks += [ref[i] for ref in a_refs[4:] for i in range(2)]
+    for place, block in zip((0, 2, 4, 6, 1, 3, 5, 7), a_blocks):
         start = pl.multiple_of((y + (2 * c - 1) * place + 8) % 8 * 256, 256)
-        a_all[:, pl.ds(start, 256)] = ref[...]
+        a_all[:, pl.ds(start, 256)] = block
     for s, t, ref in ((0, 0, v_refs[0]), (1, 0, v_refs[1]), (0, 1, v_refs[2]), (1, 1, v_refs[3])):
         offset = (x + s) % 2 * 128 + (c + t) % 2 * 64
         for k in range(8):
@@ -66,7 +68,7 @@
             jax.ShapeDtypeStruct((4, 512, 256), jnp.float32),
             jax.ShapeDtypeStruct((512, 256), jnp.float32),
         ),
-        in_specs=[VMEM] * 12,
+        in_specs=[VMEM] * 10,
         out_specs=[VMEM] * 2,
         scratch_shapes=[
             pltpu.VMEM((512, 2048), jnp.bfloat16),
@@ -102,12 +104,12 @@
     )
     blocks = [amplitudes]
     for i in range(3):
-        blocks.append(along_y(blocks[i], 2))
-    for i in range(4):
-        block = along_y(blocks[i], 1)
+        block = along_y(blocks[i], 2)
         if i == 0:
             block = untouched(block)
         blocks.append(block)
+    for i in range(2):
+        blocks.append(along_y(jnp.stack(blocks[2 * i : 2 * i + 2]), 1))
     v10 = lax.ppermute(v00, ("x", "c"), X_HOP)
     v01 = lax.ppermute(v00, "c", SWAP)
     v11 = lax.ppermute(v10, "c", SWAP)

time: 151 us -> 150 us (level)
  the two profiles are of different devices: /device:TPU:2 before, /device:TPU:1 now
where the time goes in v5:
time: 150 us; the launch traced here: 148 us
  blocking collectives  87.6 us (58%)
  starting transfers between devices  35.9 us (24%)
  waiting for transfers between devices  18.3 us (12%)
  Pallas kernels  3.07 us (2%)
    all_to_all x1, blocking collectives, staged(): got = lax.all_to_all(terms.astype(jnp.float16), 'kl', 0, 0, tiled=True)  54.4 us
    all_to_all x1, blocking collectives, staged(): lax.all_to_all(jnp.broadcast_to(integrals[None], (8, 64, 1024)), ('zl', '...  33.2 us
    ppermute x5, starting transfers between devices, along_y(): return lax.ppermute(shard, ('c', 'ij'), pairs)  24 us
    ppermute x5, waiting for transfers between devices, along_y(): return lax.ppermute(shard, ('c', 'ij'), pairs)  18.3 us
    ppermute x1, starting transfers between devices, staged(): v01 = lax.ppermute(v00, 'c', SWAP)  6.3 us
    ppermute x1, starting transfers between devices, staged(): v11 = lax.ppermute(v10, 'c', SWAP)  3.61 us
    pallas_call x1, Pallas kernels, product(): pl.pallas_call(product_kernel, out_shape=(jax.ShapeDtypeStruct((4, 512, 2...  3.07 us
  transfers between devices with their start and end apart: 8, of which 4 were waited for; matrix products, arithmetic and copies ran while one was open for 0% of the time, Pallas kernels for 0%

profile of v5, /device:TPU:1, one launch (start us, length us, event | category | flops | bytes accessed | tf_op | source)
XLA Modules:
  0.0 147.5 jit_solution(6840197809123524925)
XLA Ops:
  0.0 0.0 copy-start
  0.0 1.1 broadcast_in_dim.2
  1.1 33.2 %all_to_all.10.refs_6_ = bf16[8,64,1024]{2,1,0:T(8,128)(2,1)S(1)} all-to-all(bf16[8,64,1024]{2,1,0:T(8,128)(2,1)S(1)} %broadcast_in_dim.2), channel_id=1, replica_groups={{0,128,256,384,512,640,768,896},{64,192,320,448,576,704,832,960},{1,129..., dimensions={0} | all-to-all | bytes 2097152 | tf_op jit(solution)/shard_map/all_to_all | solution.py:101
  34.3 1.9 %collective-permute-start.5 = (bf16[8,64,1024]{2,1,0:T(8,128)(2,1)S(1)}, bf16[8,64,1024]{2,1,0:T(8,128)(2,1)S(1)}, u32[]{:S(2)}, u32[]{:S(2)}) collective-permute-start(bf16[8,64,1024]{2,1,0:T(8,128)(2,1)S(1)} %all_to_all.10.refs_6_), channel_id=1, source_target_pairs={{0,64},{64,128},{128,192},{192,256},{256,320},{320,384},{384,448},... | collective-permute-start | bytes 3145736 | tf_op jit(solution)/shard_map/ppermute | solution.py:113
  36.2 0.0 copy-done
  36.2 10.2 %collective-permute-start = (bf16[512,256]{1,0:T(8,128)(2,1)S(1)}, bf16[512,256]{1,0:T(8,128)(2,1)S(1)}, u32[]{:S(2)}, u32[]{:S(2)}) collective-permute-start(bf16[512,256]{1,0:T(8,128)(2,1)S(1)} %copy-done), channel_id=1, source_target_pairs={{0,2},{1,3},{2,4},{3,5},{4,6},{5,7},{6,0},{7,1},{32,38},{33,39},{3... | collective-permute-start | bytes 786440 | tf_op jit(solution)/shard_map/ppermute | solution.py:24
  46.5 6.1 %collective-permute-done.given = bf16[512,256]{1,0:T(8,128)(2,1)S(1)} collective-permute-done((bf16[512,256]{1,0:T(8,128)(2,1)S(1)}, bf16[512,256]{1,0:T(8,128)(2,1)S(1)}, u32[]{:S(2)}, u32[]{:S(2)}) %collective-permute-start) | collective-permute-done | bytes 262176 | tf_op jit(solution)/shard_map/ppermute | solution.py:24
  52.6 5.9 %collective-permute-start.1 = (bf16[512,256]{1,0:T(8,128)(2,1)S(1)}, bf16[512,256]{1,0:T(8,128)(2,1)S(1)}, u32[]{:S(2)}, u32[]{:S(2)}) collective-permute-start(bf16[512,256]{1,0:T(8,128)(2,1)S(1)} %shard_map.28.refs_1_), channel_id=1, source_target_pairs={{0,2},{1,3},{2,4},{3,5},{4,6},{5,7},{6,0},{7,1},{32,38},{33,39},{3... | collective-permute-start | bytes 786440 | tf_op jit(solution)/shard_map/ppermute | solution.py:24
  58.5 6.3 %collective-permute-start.6 = (bf16[8,64,1024]{2,1,0:T(8,128)(2,1)S(1)}, bf16[8,64,1024]{2,1,0:T(8,128)(2,1)S(1)}, u32[]{:S(2)}, u32[]{:S(2)}) collective-permute-start(bf16[8,64,1024]{2,1,0:T(8,128)(2,1)S(1)} %all_to_all.10.refs_6_), channel_id=1, source_target_pairs={{0,32},{32,0},{1,33},{33,1},{2,34},{34,2},{3,35},{35,3},{4,36},{36... | collective-permute-start | bytes 3145736 | tf_op jit(solution)/shard_map/ppermute | solution.py:114
  64.8 0.0 collective-permute-done.5.refs_7_
  64.8 3.6 %collective-permute-start.7 = (bf16[8,64,1024]{2,1,0:T(8,128)(2,1)S(1)}, bf16[8,64,1024]{2,1,0:T(8,128)(2,1)S(1)}, u32[]{:S(2)}, u32[]{:S(2)}) collective-permute-start(bf16[8,64,1024]{2,1,0:T(8,128)(2,1)S(1)} %collective-permute-done.5.refs_7_), channel_id=1, source_target_pairs={{0,32},{32,0},{1,33},{33,1},{2,34},{34,2},{3,35},{35,3},{4,36},{36... | collective-permute-start | bytes 3145736 | tf_op jit(solution)/shard_map/ppermute | solution.py:115
  68.5 0.0 collective-permute-done.1.refs_2_
  68.5 4.1 %collective-permute-start.2 = (bf16[512,256]{1,0:T(8,128)(2,1)S(1)}, bf16[512,256]{1,0:T(8,128)(2,1)S(1)}, u32[]{:S(2)}, u32[]{:S(2)}) collective-permute-start(bf16[512,256]{1,0:T(8,128)(2,1)S(1)} %collective-permute-done.1.refs_2_), channel_id=1, source_target_pairs={{0,2},{1,3},{2,4},{3,5},{4,6},{5,7},{6,0},{7,1},{32,38},{33,39},{3... | collective-permute-start | bytes 786440 | tf_op jit(solution)/shard_map/ppermute | solution.py:24
  72.5 0.1 pad_maximum_fusion
  72.6 1.9 %collective-permute-start.3 = (bf16[2,512,256]{2,1,0:T(8,128)(2,1)S(1)}, bf16[2,512,256]{2,1,0:T(8,128)(2,1)S(1)}, u32[]{:S(2)}, u32[]{:S(2)}) collective-permute-start(bf16[2,512,256]{2,1,0:T(8,128)(2,1)S(1)} %pad_maximum_fusion), channel_id=1, source_target_pairs={{0,1},{1,2},{2,3},{3,4},{4,5},{5,6},{6,7},{7,0},{32,39},{33,32},{3... | collective-permute-start | bytes 1572872 | tf_op jit(solution)/shard_map/ppermute | solution.py:24
  74.5 3.0 %collective-permute-done.2.refs_3_ = bf16[512,256]{1,0:T(8,128)(2,1)S(1)} collective-permute-done((bf16[512,256]{1,0:T(8,128)(2,1)S(1)}, bf16[512,256]{1,0:T(8,128)(2,1)S(1)}, u32[]{:S(2)}, u32[]{:S(2)}) %collective-permute-start.2) | collective-permute-done | bytes 262176 | tf_op jit(solution)/shard_map/ppermute | solution.py:24
  77.5 0.1 pad_maximum_fusion.1
  77.6 1.9 %collective-permute-start.4 = (bf16[2,512,256]{2,1,0:T(8,128)(2,1)S(1)}, bf16[2,512,256]{2,1,0:T(8,128)(2,1)S(1)}, u32[]{:S(2)}, u32[]{:S(2)}) collective-permute-start(bf16[2,512,256]{2,1,0:T(8,128)(2,1)S(1)} %pad_maximum_fusion.1), channel_id=1, source_target_pairs={{0,1},{1,2},{2,3},{3,4},{4,5},{5,6},{6,7},{7,0},{32,39},{33,32},{3... | collective-permute-start | bytes 1572872 | tf_op jit(solution)/shard_map/ppermute | solution.py:24
  79.5 3.9 %collective-permute-done.3.refs_4_ = bf16[2,512,256]{2,1,0:T(8,128)(2,1)S(1)} collective-permute-done((bf16[2,512,256]{2,1,0:T(8,128)(2,1)S(1)}, bf16[2,512,256]{2,1,0:T(8,128)(2,1)S(1)}, u32[]{:S(2)}, u32[]{:S(2)}) %collective-permute-start.3) | collective-permute-done | bytes 524320 | tf_op jit(solution)/shard_map/ppermute | solution.py:24
  83.4 5.3 %collective-permute-done.4.refs_5_ = bf16[2,512,256]{2,1,0:T(8,128)(2,1)S(1)} collective-permute-done((bf16[2,512,256]{2,1,0:T(8,128)(2,1)S(1)}, bf16[2,512,256]{2,1,0:T(8,128)(2,1)S(1)}, u32[]{:S(2)}, u32[]{:S(2)}) %collective-permute-start.4) | collective-permute-done | bytes 524320 | tf_op jit(solution)/shard_map/ppermute | solution.py:24
  88.7 0.0 collective-permute-done.6.refs_8_
  88.7 0.0 collective-permute-done.7.refs_9_
  88.7 3.1 %shard_map.29 = (f32[4,512,256]{2,1,0:T(8,128)S(1)}, f32[512,256]{1,0:T(8,128)S(1)}) custom-call(bf16[512,256]{1,0:T(8,128)(2,1)S(1)} %copy-done, bf16[512,256]{1,0:T(8,128)(2,1)S(1)} %shard_map.28.refs_1_, bf16[512,256]{1,0:T(8,128)(2,1)S(1)} %collective-permute-done.1.refs_2_, bf16[512,256]{1,0:T(8,128)(2,1)S(1)} %collective-permute-done.2.refs_3_, ...), custom_call_target="tpu_custom_call" | custom-call | flops 2147483648 | bytes 8388608 | tf_op jit(solution)/shard_map/pallas_call | solution.py:65
  91.8 0.2 convert_element_type.6
  92.0 54.4 %all_to_all.11 = f16[4,512,256]{2,1,0:T(8,128)(2,1)S(1)} all-to-all(f16[4,512,256]{2,1,0:T(8,128)(2,1)S(1)} %convert_element_type.6), channel_id=1, replica_groups=mesh['zl'=2,'x'=8,'c'=2,'kl'=4,'ij'=8] {'kl'}, dimensions={0} | all-to-all | bytes 2097152 | tf_op jit(solution)/shard_map/all_to_all | solution.py:117
  146.4 0.2 convert_element_type.7
  146.5 1.0 fusion.3
  (1 shorter events, 0.0 us)
Async XLA Ops:
  0.0 36.2 %copy-start = (bf16[512,256]{1,0:T(8,128)(2,1)S(1)}, bf16[512,256]{1,0:T(8,128)(2,1)}, u32[]{:S(2)}) copy-start(bf16[512,256]{1,0:T(8,128)(2,1)} %refs_0_.1) | copy-start | bytes 786436
  34.3 30.5 %collective-permute-start.5 = (bf16[8,64,1024]{2,1,0:T(8,128)(2,1)S(1)}, bf16[8,64,1024]{2,1,0:T(8,128)(2,1)S(1)}, u32[]{:S(2)}, u32[]{:S(2)}) collective-permute-start(bf16[8,64,1024]{2,1,0:T(8,128)(2,1)S(1)} %all_to_all.10.refs_6_), channel_id=1, source_target_pairs={{0,64},{64,128},{128,192},{192,256},{256,320},{320,384},{384,448},... | collective-permute-start | bytes 3145736 | tf_op jit(solution)/shard_map/ppermute | solution.py:113
  36.2 16.4 %collective-permute-start = (bf16[512,256]{1,0:T(8,128)(2,1)S(1)}, bf16[512,256]{1,0:T(8,128)(2,1)S(1)}, u32[]{:S(2)}, u32[]{:S(2)}) collective-permute-start(bf16[512,256]{1,0:T(8,128)(2,1)S(1)} %copy-done), channel_id=1, source_target_pairs={{0,2},{1,3},{2,4},{3,5},{4,6},{5,7},{6,0},{7,1},{32,38},{33,39},{3... | collective-permute-start | bytes 786440 | tf_op jit(solution)/shard_map/ppermute | solution.py:24
  52.6 15.9 %collective-permute-start.1 = (bf16[512,256]{1,0:T(8,128)(2,1)S(1)}, bf16[512,256]{1,0:T(8,128)(2,1)S(1)}, u32[]{:S(2)}, u32[]{:S(2)}) collective-permute-start(bf16[512,256]{1,0:T(8,128)(2,1)S(1)} %shard_map.28.refs_1_), channel_id=1, source_target_pairs={{0,2},{1,3},{2,4},{3,5},{4,6},{5,7},{6,0},{7,1},{32,38},{33,39},{3... | collective-permute-start | bytes 786440 | tf_op jit(solution)/shard_map/ppermute | solution.py:24
  58.5 30.2 %collective-permute-start.6 = (bf16[8,64,1024]{2,1,0:T(8,128)(2,1)S(1)}, bf16[8,64,1024]{2,1,0:T(8,128)(2,1)S(1)}, u32[]{:S(2)}, u32[]{:S(2)}) collective-permute-start(bf16[8,64,1024]{2,1,0:T(8,128)(2,1)S(1)} %all_to_all.10.refs_6_), channel_id=1, source_target_pairs={{0,32},{32,0},{1,33},{33,1},{2,34},{34,2},{3,35},{35,3},{4,36},{36... | collective-permute-start | bytes 3145736 | tf_op jit(solution)/shard_map/ppermute | solution.py:114
  64.8 23.9 %collective-permute-start.7 = (bf16[8,64,1024]{2,1,0:T(8,128)(2,1)S(1)}, bf16[8,64,1024]{2,1,0:T(8,128)(2,1)S(1)}, u32[]{:S(2)}, u32[]{:S(2)}) collective-permute-start(bf16[8,64,1024]{2,1,0:T(8,128)(2,1)S(1)} %collective-permute-done.5.refs_7_), channel_id=1, source_target_pairs={{0,32},{32,0},{1,33},{33,1},{2,34},{34,2},{3,35},{35,3},{4,36},{36... | collective-permute-start | bytes 3145736 | tf_op jit(solution)/shard_map/ppermute | solution.py:115
  68.5 9.1 %collective-permute-start.2 = (bf16[512,256]{1,0:T(8,128)(2,1)S(1)}, bf16[512,256]{1,0:T(8,128)(2,1)S(1)}, u32[]{:S(2)}, u32[]{:S(2)}) collective-permute-start(bf16[512,256]{1,0:T(8,128)(2,1)S(1)} %collective-permute-done.1.refs_2_), channel_id=1, source_target_pairs={{0,2},{1,3},{2,4},{3,5},{4,6},{5,7},{6,0},{7,1},{32,38},{33,39},{3... | collective-permute-start | bytes 786440 | tf_op jit(solution)/shard_map/ppermute | solution.py:24
  72.6 10.8 %collective-permute-start.3 = (bf16[2,512,256]{2,1,0:T(8,128)(2,1)S(1)}, bf16[2,512,256]{2,1,0:T(8,128)(2,1)S(1)}, u32[]{:S(2)}, u32[]{:S(2)}) collective-permute-start(bf16[2,512,256]{2,1,0:T(8,128)(2,1)S(1)} %pad_maximum_fusion), channel_id=1, source_target_pairs={{0,1},{1,2},{2,3},{3,4},{4,5},{5,6},{6,7},{7,0},{32,39},{33,32},{3... | collective-permute-start | bytes 1572872 | tf_op jit(solution)/shard_map/ppermute | solution.py:24
  77.6 11.1 %collective-permute-start.4 = (bf16[2,512,256]{2,1,0:T(8,128)(2,1)S(1)}, bf16[2,512,256]{2,1,0:T(8,128)(2,1)S(1)}, u32[]{:S(2)}, u32[]{:S(2)}) collective-permute-start(bf16[2,512,256]{2,1,0:T(8,128)(2,1)S(1)} %pad_maximum_fusion.1), channel_id=1, source_target_pairs={{0,1},{1,2},{2,3},{3,4},{4,5},{5,6},{6,7},{7,0},{32,39},{33,32},{3... | collective-permute-start | bytes 1572872 | tf_op jit(solution)/shard_map/ppermute | solution.py:24

commit v6 on v3

--- a/solution.py
+++ b/solution.py
@@ -12,13 +12,16 @@
 SCALE = 64.0
 
 X_PARITY = [[zl * 8 + x for zl in range(2) for x in range(p, 8, 2)] for p in range(2)]
-Y_HOP = [(c * 8 + y, c * 8 + (y + 1 - 2 * c) % 8) for c in range(2) for y in range(8)]
 X_HOP = [(x * 2 + c, (x + 1 - 2 * c) % 8 * 2 + c) for c in range(2) for x in range(8)]
 SWAP = [(0, 1), (1, 0)]
 
 
-def along_y(shard, step):
-    return lax.ppermute(shard, "ij", [(y, (y + step) % 8) for y in range(8)])
+def along_y(shard, hops):
+    pairs = [
+        (c * 8 + y, c * 8 + (y + hops * (1 - 2 * c)) % 8)
+        for c in range(2) for y in range(8)
+    ]
+    return lax.ppermute(shard, ("c", "ij"), pairs)
 
 
 def shifted(term, ahead):
@@ -27,13 +30,14 @@
 
 
 def first_kernel(*refs):
-    a_refs, v_refs, (a_all, v_all) = refs[:8], refs[8:12], refs[12:14]
+    a_refs, v_refs, (a_all, v_all, out, arrived) = refs[:8], refs[8:12], refs[12:]
     x, y, c = (lax.axis_index(name) for name in ("x", "ij", "c"))
-    near = 2 * c - 1
-    places = [0, -2, 2, 4]
-    places += [near + place for place in places]
-    for place, ref in zip(places, a_refs):
-        start = pl.multiple_of((y + place + 16) % 8 * 256, 256)
+    kept = pltpu.make_async_copy(
+        a_refs[0], a_all.at[:, pl.ds(pl.multiple_of(y * 256, 256), 256)], arrived
+    )
+    kept.start()
+    for place, ref in zip((2, 4, 6, 1, 3, 5, 7), a_refs[1:]):
+        start = pl.multiple_of((y + (2 * c - 1) * place + 8) % 8 * 256, 256)
         a_all[:, pl.ds(start, 256)] = ref[...]
     for s, t, ref in ((0, 0, v_refs[0]), (1, 0, v_refs[1]), (0, 1, v_refs[2]), (1, 1, v_refs[3])):
         offset = (x + s) % 2 * 128 + (c + t) % 2 * 64
@@ -43,10 +47,10 @@
 
     @pl.when(lax.axis_index("kl") == 3)
     def _():
-        v_all[pl.ds(1984, 64), :] = jnp.zeros((64, 1024), jnp.bfloat16)
+        v_all[PAIRS - 6144 :, :] = jnp.zeros((8192 - PAIRS, 1024), jnp.bfloat16)
 
-
-    place_product(2, a_all, v_all, refs[14])
+    kept.wait()
+    place_product(2, a_all, v_all, out)
 
 
 def place_product(ahead, a_all, v_all, out):
@@ -73,8 +77,9 @@
             jax.ShapeDtypeStruct((2048, 1024), jnp.bfloat16),
             TERM,
         ),
-        in_specs=[VMEM] * 12,
+        in_specs=[pl.BlockSpec(memory_space=pl.ANY)] + [VMEM] * 11,
         out_specs=[VMEM] * 3,
+        scratch_shapes=[pltpu.SemaphoreType.DMA],
         compiler_params=pltpu.CompilerParams(vmem_limit_bytes=16 << 20),
         cost_estimate=pl.CostEstimate(
             flops=2 * 512 * 2048 * 256, bytes_accessed=12 << 20, transcendentals=0
@@ -117,12 +122,13 @@
         tiled=True, axis_index_groups=X_PARITY,
     )
     blocks = [amplitudes]
-    for step in (2, -2, 4):
-        blocks.append(along_y(amplitudes, step))
+    for i in range(3):
+        blocks.append(along_y(blocks[i], 2))
     for i in range(4):
-        blocks.append(lax.ppermute(blocks[i], ("c", "ij"), Y_HOP))
+        block = along_y(blocks[i], 1)
         if i == 0:
-            blocks[4] = untouched(blocks[4])
+            block = untouched(block)
+        blocks.append(block)
     v10 = lax.ppermute(v00, ("x", "c"), X_HOP)
     v01 = lax.ppermute(v00, "c", SWAP)
     v11 = lax.ppermute(v10, "c", SWAP)

time: 166 us -> 150 us (0.904)
  starting transfers between devices: 92.2 us -> 78 us
  waiting for transfers between devices: 33.5 us -> 31 us
    ppermute x1, starting transfers between devices: 16.2 us -> 7.89 us  [staged(): v01 = lax.ppermute(v00, 'c', SWAP)]
    ppermute x3, starting transfers between devices: 36 us -> 31.2 us  [shifted(): lax.ppermute(term.astype(jnp.float16), 'kl', pairs).astype(jnp.float32)]
    ppermute x7, waiting for transfers between devices: 15 us -> 12.8 us  [along_y(): return lax.ppermute(shard, ('c', 'ij'), pairs)]
    ppermute x1, starting transfers between devices: 15.9 us -> 14 us  [staged(): v11 = lax.ppermute(v10, 'c', SWAP)]
where the time goes in v6:
time: 150 us; the launch traced here: 149 us
  starting transfers between devices  78 us (52%)
  blocking collectives  33.2 us (22%)
  waiting for transfers between devices  31 us (21%)
  Pallas kernels  3.17 us (2%)
  local copies, waits for them, and re-layouts  1.97 us (1%)
    all_to_all x1, blocking collectives, staged(): lax.all_to_all(jnp.broadcast_to(integrals[None], (8, 64, 1024)), ('zl', '...  33.2 us
    ppermute x3, starting transfers between devices, shifted(): lax.ppermute(term.astype(jnp.float16), 'kl', pairs).astype(jnp.float32)  31.2 us
    ppermute x7, starting transfers between devices, along_y(): return lax.ppermute(shard, ('c', 'ij'), pairs)  23 us
    ppermute x3, waiting for transfers between devices, shifted(): lax.ppermute(term.astype(jnp.float16), 'kl', pairs).astype(jnp.float32)  18.2 us
    ppermute x1, starting transfers between devices, staged(): v11 = lax.ppermute(v10, 'c', SWAP)  14 us
    ppermute x7, waiting for transfers between devices, along_y(): return lax.ppermute(shard, ('c', 'ij'), pairs)  12.8 us
    ppermute x1, starting transfers between devices, staged(): v01 = lax.ppermute(v00, 'c', SWAP)  7.89 us
  transfers between devices with their start and end apart: 13, of which 6 were waited for; matrix products, arithmetic and copies ran while one was open for 0% of the time, Pallas kernels for 0%

profile of v6, /device:TPU:1, one launch (start us, length us, event | category | flops | bytes accessed | tf_op | source)
XLA Modules:
  0.0 148.7 jit_solution(13159817060999156887)
XLA Ops:
  0.0 1.0 broadcast_in_dim.20
  1.0 33.2 %all_to_all.5.refs_8_ = bf16[8,64,1024]{2,1,0:T(8,128)(2,1)S(1)} all-to-all(bf16[8,64,1024]{2,1,0:T(8,128)(2,1)S(1)} %broadcast_in_dim.20), channel_id=1, replica_groups={{0,128,256,384,512,640,768,896},{64,192,320,448,576,704,832,960},{1,129..., dimensions={0} | all-to-all | bytes 2097152 | tf_op jit(solution)/shard_map/all_to_all | solution.py:120
  34.3 1.9 %collective-permute-start.7 = (bf16[8,64,1024]{2,1,0:T(8,128)(2,1)S(1)}, bf16[8,64,1024]{2,1,0:T(8,128)(2,1)S(1)}, u32[]{:S(2)}, u32[]{:S(2)}) collective-permute-start(bf16[8,64,1024]{2,1,0:T(8,128)(2,1)S(1)} %all_to_all.5.refs_8_), channel_id=1, source_target_pairs={{0,64},{64,128},{128,192},{192,256},{256,320},{320,384},{384,448},... | collective-permute-start | bytes 3145736 | tf_op jit(solution)/shard_map/ppermute | solution.py:132
  36.2 10.2 %collective-permute-start = (bf16[512,256]{1,0:T(8,128)(2,1)}, bf16[512,256]{1,0:T(8,128)(2,1)S(1)}, u32[]{:S(2)}, u32[]{:S(2)}) collective-permute-start(bf16[512,256]{1,0:T(8,128)(2,1)} %refs_0_.1), channel_id=1, source_target_pairs={{0,2},{1,3},{2,4},{3,5},{4,6},{5,7},{6,0},{7,1},{32,38},{33,39},{3... | collective-permute-start | bytes 786440 | tf_op jit(solution)/shard_map/ppermute | solution.py:24
  46.4 7.9 %collective-permute-start.8 = (bf16[8,64,1024]{2,1,0:T(8,128)(2,1)S(1)}, bf16[8,64,1024]{2,1,0:T(8,128)(2,1)S(1)}, u32[]{:S(2)}, u32[]{:S(2)}) collective-permute-start(bf16[8,64,1024]{2,1,0:T(8,128)(2,1)S(1)} %all_to_all.5.refs_8_), channel_id=1, source_target_pairs={{0,32},{32,0},{1,33},{33,1},{2,34},{34,2},{3,35},{35,3},{4,36},{36... | collective-permute-start | bytes 3145736 | tf_op jit(solution)/shard_map/ppermute | solution.py:133
  54.3 0.0 collective-permute-done.7.refs_9_
  54.3 14.0 %collective-permute-start.9 = (bf16[8,64,1024]{2,1,0:T(8,128)(2,1)S(1)}, bf16[8,64,1024]{2,1,0:T(8,128)(2,1)S(1)}, u32[]{:S(2)}, u32[]{:S(2)}) collective-permute-start(bf16[8,64,1024]{2,1,0:T(8,128)(2,1)S(1)} %collective-permute-done.7.refs_9_), channel_id=1, source_target_pairs={{0,32},{32,0},{1,33},{33,1},{2,34},{34,2},{3,35},{35,3},{4,36},{36... | collective-permute-start | bytes 3145736 | tf_op jit(solution)/shard_map/ppermute | solution.py:134
  68.4 0.0 collective-permute-done.refs_1_
  68.4 1.9 %collective-permute-start.1 = (bf16[512,256]{1,0:T(8,128)(2,1)S(1)}, bf16[512,256]{1,0:T(8,128)(2,1)S(1)}, u32[]{:S(2)}, u32[]{:S(2)}) collective-permute-start(bf16[512,256]{1,0:T(8,128)(2,1)S(1)} %collective-permute-done.refs_1_), channel_id=1, source_target_pairs={{0,2},{1,3},{2,4},{3,5},{4,6},{5,7},{6,0},{7,1},{32,38},{33,39},{3... | collective-permute-start | bytes 786440 | tf_op jit(solution)/shard_map/ppermute | solution.py:24
  70.3 1.9 %collective-permute-start.3 = (bf16[512,256]{1,0:T(8,128)(2,1)}, bf16[512,256]{1,0:T(8,128)(2,1)S(1)}, u32[]{:S(2)}, u32[]{:S(2)}) collective-permute-start(bf16[512,256]{1,0:T(8,128)(2,1)} %refs_0_.1), channel_id=1, source_target_pairs={{0,1},{1,2},{2,3},{3,4},{4,5},{5,6},{6,7},{7,0},{32,39},{33,32},{3... | collective-permute-start | bytes 786440 | tf_op jit(solution)/shard_map/ppermute | solution.py:24
  72.2 4.5 %collective-permute-done.1.refs_2_ = bf16[512,256]{1,0:T(8,128)(2,1)S(1)} collective-permute-done((bf16[512,256]{1,0:T(8,128)(2,1)S(1)}, bf16[512,256]{1,0:T(8,128)(2,1)S(1)}, u32[]{:S(2)}, u32[]{:S(2)}) %collective-permute-start.1) | collective-permute-done | bytes 262176 | tf_op jit(solution)/shard_map/ppermute | solution.py:24
  76.7 2.9 %collective-permute-start.2 = (bf16[512,256]{1,0:T(8,128)(2,1)S(1)}, bf16[512,256]{1,0:T(8,128)(2,1)S(1)}, u32[]{:S(2)}, u32[]{:S(2)}) collective-permute-start(bf16[512,256]{1,0:T(8,128)(2,1)S(1)} %collective-permute-done.1.refs_2_), channel_id=1, source_target_pairs={{0,2},{1,3},{2,4},{3,5},{4,6},{5,7},{6,0},{7,1},{32,38},{33,39},{3... | collective-permute-start | bytes 786440 | tf_op jit(solution)/shard_map/ppermute | solution.py:24
  79.6 1.9 %collective-permute-start.4 = (bf16[512,256]{1,0:T(8,128)(2,1)S(1)}, bf16[512,256]{1,0:T(8,128)(2,1)S(1)}, u32[]{:S(2)}, u32[]{:S(2)}) collective-permute-start(bf16[512,256]{1,0:T(8,128)(2,1)S(1)} %collective-permute-done.refs_1_), channel_id=1, source_target_pairs={{0,1},{1,2},{2,3},{3,4},{4,5},{5,6},{6,7},{7,0},{32,39},{33,32},{3... | collective-permute-start | bytes 786440 | tf_op jit(solution)/shard_map/ppermute | solution.py:24
  81.6 0.0 collective-permute-done.3.given
  81.6 2.2 %collective-permute-start.5 = (bf16[512,256]{1,0:T(8,128)(2,1)S(1)}, bf16[512,256]{1,0:T(8,128)(2,1)S(1)}, u32[]{:S(2)}, u32[]{:S(2)}) collective-permute-start(bf16[512,256]{1,0:T(8,128)(2,1)S(1)} %collective-permute-done.1.refs_2_), channel_id=1, source_target_pairs={{0,1},{1,2},{2,3},{3,4},{4,5},{5,6},{6,7},{7,0},{32,39},{33,32},{3... | collective-permute-start | bytes 786440 | tf_op jit(solution)/shard_map/ppermute | solution.py:24
  83.8 1.7 %collective-permute-done.2.refs_3_ = bf16[512,256]{1,0:T(8,128)(2,1)S(1)} collective-permute-done((bf16[512,256]{1,0:T(8,128)(2,1)S(1)}, bf16[512,256]{1,0:T(8,128)(2,1)S(1)}, u32[]{:S(2)}, u32[]{:S(2)}) %collective-permute-start.2) | collective-permute-done | bytes 262176 | tf_op jit(solution)/shard_map/ppermute | solution.py:24
  85.4 1.9 %collective-permute-start.6 = (bf16[512,256]{1,0:T(8,128)(2,1)S(1)}, bf16[512,256]{1,0:T(8,128)(2,1)S(1)}, u32[]{:S(2)}, u32[]{:S(2)}) collective-permute-start(bf16[512,256]{1,0:T(8,128)(2,1)S(1)} %collective-permute-done.2.refs_3_), channel_id=1, source_target_pairs={{0,1},{1,2},{2,3},{3,4},{4,5},{5,6},{6,7},{7,0},{32,39},{33,32},{3... | collective-permute-start | bytes 786440 | tf_op jit(solution)/shard_map/ppermute | solution.py:24
  87.4 1.1 collective-permute-done.4.refs_5_
  88.4 2.8 %collective-permute-done.5.refs_6_ = bf16[512,256]{1,0:T(8,128)(2,1)S(1)} collective-permute-done((bf16[512,256]{1,0:T(8,128)(2,1)S(1)}, bf16[512,256]{1,0:T(8,128)(2,1)S(1)}, u32[]{:S(2)}, u32[]{:S(2)}) %collective-permute-start.5) | collective-permute-done | bytes 262176 | tf_op jit(solution)/shard_map/ppermute | solution.py:24
  91.2 2.8 %collective-permute-done.6.refs_7_ = bf16[512,256]{1,0:T(8,128)(2,1)S(1)} collective-permute-done((bf16[512,256]{1,0:T(8,128)(2,1)S(1)}, bf16[512,256]{1,0:T(8,128)(2,1)S(1)}, u32[]{:S(2)}, u32[]{:S(2)}) %collective-permute-start.6) | collective-permute-done | bytes 262176 | tf_op jit(solution)/shard_map/ppermute | solution.py:24
  94.0 0.0 collective-permute-done.8.refs_10_
  94.0 0.0 collective-permute-done.9.refs_11_
  94.1 0.0 copy-start
  94.1 0.9 copy-done
  95.0 1.3 shard_map.29
  96.3 1.8 %shard_map.30 = (f32[512,256]{1,0:T(8,128)S(1)}, f32[512,256]{1,0:T(8,128)S(1)}, f32[512,256]{1,0:T(8,128)S(1)}) custom-call(bf16[512,2048]{1,0:T(8,128)(2,1)S(1)} %get-tuple-element.11.a_all, bf16[2048,1024]{1,0:T(8,128)(2,1)S(1)} %get-tuple-element.12.v_all), custom_call_target="tpu_custom_call" | custom-call | flops 1610612736 | bytes 8388608 | tf_op jit(solution)/shard_map/pallas_call | solution.py:91
  98.2 6.4 %collective-permute-start.10 = (f16[512,256]{1,0:T(8,128)(2,1)S(1)}, f16[512,256]{1,0:T(8,128)(2,1)S(1)}, u32[]{:S(2)}, u32[]{:S(2)}) collective-permute-start(f16[512,256]{1,0:T(8,128)(2,1)S(1)} %convert_element_type.18), channel_id=1, source_target_pairs={{0,8},{8,16},{16,24},{24,0},{1,9},{9,17},{17,25},{25,1},{2,10},{10... | collective-permute-start | bytes 786440 | tf_op jit(solution)/shard_map/ppermute | solution.py:29
  104.7 20.8 %collective-permute-start.11 = (f16[512,256]{1,0:T(8,128)(2,1)S(1)}, f16[512,256]{1,0:T(8,128)(2,1)S(1)}, u32[]{:S(2)}, u32[]{:S(2)}) collective-permute-start(f16[512,256]{1,0:T(8,128)(2,1)S(1)} %convert_element_type.20), channel_id=1, source_target_pairs={{0,24},{8,0},{16,8},{24,16},{1,25},{9,1},{17,9},{25,17},{2,26},{10... | collective-permute-start | bytes 786440 | tf_op jit(solution)/shard_map/ppermute | solution.py:29
  125.5 4.0 %collective-permute-start.12 = (f16[512,256]{1,0:T(8,128)(2,1)S(1)}, f16[512,256]{1,0:T(8,128)(2,1)S(1)}, u32[]{:S(2)}, u32[]{:S(2)}) collective-permute-start(f16[512,256]{1,0:T(8,128)(2,1)S(1)} %convert_element_type.22), channel_id=1, source_target_pairs={{0,16},{8,24},{16,0},{24,8},{1,17},{9,25},{17,1},{25,9},{2,18},{10... | collective-permute-start | bytes 786440 | tf_op jit(solution)/shard_map/ppermute | solution.py:29
  129.5 0.0 collective-permute-done.10
  129.6 18.2 %collective-permute-done.11 = f16[512,256]{1,0:T(8,128)(2,1)S(1)} collective-permute-done((f16[512,256]{1,0:T(8,128)(2,1)S(1)}, f16[512,256]{1,0:T(8,128)(2,1)S(1)}, u32[]{:S(2)}, u32[]{:S(2)}) %collective-permute-start.11) | collective-permute-done | bytes 262176 | tf_op jit(solution)/shard_map/ppermute | solution.py:29
  147.8 0.0 collective-permute-done.12
  147.8 0.9 multiply_select_fusion
  (5 shorter events, 0.1 us)
Async XLA Ops:
  34.3 20.1 %collective-permute-start.7 = (bf16[8,64,1024]{2,1,0:T(8,128)(2,1)S(1)}, bf16[8,64,1024]{2,1,0:T(8,128)(2,1)S(1)}, u32[]{:S(2)}, u32[]{:S(2)}) collective-permute-start(bf16[8,64,1024]{2,1,0:T(8,128)(2,1)S(1)} %all_to_all.5.refs_8_), channel_id=1, source_target_pairs={{0,64},{64,128},{128,192},{192,256},{256,320},{320,384},{384,448},... | collective-permute-start | bytes 3145736 | tf_op jit(solution)/shard_map/ppermute | solution.py:132
  36.2 32.2 %collective-permute-start = (bf16[512,256]{1,0:T(8,128)(2,1)}, bf16[512,256]{1,0:T(8,128)(2,1)S(1)}, u32[]{:S(2)}, u32[]{:S(2)}) collective-permute-start(bf16[512,256]{1,0:T(8,128)(2,1)} %refs_0_.1), channel_id=1, source_target_pairs={{0,2},{1,3},{2,4},{3,5},{4,6},{5,7},{6,0},{7,1},{32,38},{33,39},{3... | collective-permute-start | bytes 786440 | tf_op jit(solution)/shard_map/ppermute | solution.py:24
  46.4 47.6 %collective-permute-start.8 = (bf16[8,64,1024]{2,1,0:T(8,128)(2,1)S(1)}, bf16[8,64,1024]{2,1,0:T(8,128)(2,1)S(1)}, u32[]{:S(2)}, u32[]{:S(2)}) collective-permute-start(bf16[8,64,1024]{2,1,0:T(8,128)(2,1)S(1)} %all_to_all.5.refs_8_), channel_id=1, source_target_pairs={{0,32},{32,0},{1,33},{33,1},{2,34},{34,2},{3,35},{35,3},{4,36},{36... | collective-permute-start | bytes 3145736 | tf_op jit(solution)/shard_map/ppermute | solution.py:133
  54.3 39.7 %collective-permute-start.9 = (bf16[8,64,1024]{2,1,0:T(8,128)(2,1)S(1)}, bf16[8,64,1024]{2,1,0:T(8,128)(2,1)S(1)}, u32[]{:S(2)}, u32[]{:S(2)}) collective-permute-start(bf16[8,64,1024]{2,1,0:T(8,128)(2,1)S(1)} %collective-permute-done.7.refs_9_), channel_id=1, source_target_pairs={{0,32},{32,0},{1,33},{33,1},{2,34},{34,2},{3,35},{35,3},{4,36},{36... | collective-permute-start | bytes 3145736 | tf_op jit(solution)/shard_map/ppermute | solution.py:134
  68.4 8.3 %collective-permute-start.1 = (bf16[512,256]{1,0:T(8,128)(2,1)S(1)}, bf16[512,256]{1,0:T(8,128)(2,1)S(1)}, u32[]{:S(2)}, u32[]{:S(2)}) collective-permute-start(bf16[512,256]{1,0:T(8,128)(2,1)S(1)} %collective-permute-done.refs_1_), channel_id=1, source_target_pairs={{0,2},{1,3},{2,4},{3,5},{4,6},{5,7},{6,0},{7,1},{32,38},{33,39},{3... | collective-permute-start | bytes 786440 | tf_op jit(solution)/shard_map/ppermute | solution.py:24
  70.3 11.2 %collective-permute-start.3 = (bf16[512,256]{1,0:T(8,128)(2,1)}, bf16[512,256]{1,0:T(8,128)(2,1)S(1)}, u32[]{:S(2)}, u32[]{:S(2)}) collective-permute-start(bf16[512,256]{1,0:T(8,128)(2,1)} %refs_0_.1), channel_id=1, source_target_pairs={{0,1},{1,2},{2,3},{3,4},{4,5},{5,6},{6,7},{7,0},{32,39},{33,32},{3... | collective-permute-start | bytes 786440 | tf_op jit(solution)/shard_map/ppermute | solution.py:24
  76.7 8.7 %collective-permute-start.2 = (bf16[512,256]{1,0:T(8,128)(2,1)S(1)}, bf16[512,256]{1,0:T(8,128)(2,1)S(1)}, u32[]{:S(2)}, u32[]{:S(2)}) collective-permute-start(bf16[512,256]{1,0:T(8,128)(2,1)S(1)} %collective-permute-done.1.refs_2_), channel_id=1, source_target_pairs={{0,2},{1,3},{2,4},{3,5},{4,6},{5,7},{6,0},{7,1},{32,38},{33,39},{3... | collective-permute-start | bytes 786440 | tf_op jit(solution)/shard_map/ppermute | solution.py:24
  79.6 8.8 %collective-permute-start.4 = (bf16[512,256]{1,0:T(8,128)(2,1)S(1)}, bf16[512,256]{1,0:T(8,128)(2,1)S(1)}, u32[]{:S(2)}, u32[]{:S(2)}) collective-permute-start(bf16[512,256]{1,0:T(8,128)(2,1)S(1)} %collective-permute-done.refs_1_), channel_id=1, source_target_pairs={{0,1},{1,2},{2,3},{3,4},{4,5},{5,6},{6,7},{7,0},{32,39},{33,32},{3... | collective-permute-start | bytes 786440 | tf_op jit(solution)/shard_map/ppermute | solution.py:24
  81.6 9.7 %collective-permute-start.5 = (bf16[512,256]{1,0:T(8,128)(2,1)S(1)}, bf16[512,256]{1,0:T(8,128)(2,1)S(1)}, u32[]{:S(2)}, u32[]{:S(2)}) collective-permute-start(bf16[512,256]{1,0:T(8,128)(2,1)S(1)} %collective-permute-done.1.refs_2_), channel_id=1, source_target_pairs={{0,1},{1,2},{2,3},{3,4},{4,5},{5,6},{6,7},{7,0},{32,39},{33,32},{3... | collective-permute-start | bytes 786440 | tf_op jit(solution)/shard_map/ppermute | solution.py:24
  85.4 8.6 %collective-permute-start.6 = (bf16[512,256]{1,0:T(8,128)(2,1)S(1)}, bf16[512,256]{1,0:T(8,128)(2,1)S(1)}, u32[]{:S(2)}, u32[]{:S(2)}) collective-permute-start(bf16[512,256]{1,0:T(8,128)(2,1)S(1)} %collective-permute-done.2.refs_3_), channel_id=1, source_target_pairs={{0,1},{1,2},{2,3},{3,4},{4,5},{5,6},{6,7},{7,0},{32,39},{33,32},{3... | collective-permute-start | bytes 786440 | tf_op jit(solution)/shard_map/ppermute | solution.py:24
  94.1 1.0 copy-start
  98.2 31.3 %collective-permute-start.10 = (f16[512,256]{1,0:T(8,128)(2,1)S(1)}, f16[512,256]{1,0:T(8,128)(2,1)S(1)}, u32[]{:S(2)}, u32[]{:S(2)}) collective-permute-start(f16[512,256]{1,0:T(8,128)(2,1)S(1)} %convert_element_type.18), channel_id=1, source_target_pairs={{0,8},{8,16},{16,24},{24,0},{1,9},{9,17},{17,25},{25,1},{2,10},{10... | collective-permute-start | bytes 786440 | tf_op jit(solution)/shard_map/ppermute | solution.py:29
  104.7 43.1 %collective-permute-start.11 = (f16[512,256]{1,0:T(8,128)(2,1)S(1)}, f16[512,256]{1,0:T(8,128)(2,1)S(1)}, u32[]{:S(2)}, u32[]{:S(2)}) collective-permute-start(f16[512,256]{1,0:T(8,128)(2,1)S(1)} %convert_element_type.20), channel_id=1, source_target_pairs={{0,24},{8,0},{16,8},{24,16},{1,25},{9,1},{17,9},{25,17},{2,26},{10... | collective-permute-start | bytes 786440 | tf_op jit(solution)/shard_map/ppermute | solution.py:29
  125.5 22.2 %collective-permute-start.12 = (f16[512,256]{1,0:T(8,128)(2,1)S(1)}, f16[512,256]{1,0:T(8,128)(2,1)S(1)}, u32[]{:S(2)}, u32[]{:S(2)}) collective-permute-start(f16[512,256]{1,0:T(8,128)(2,1)S(1)} %convert_element_type.22), channel_id=1, source_target_pairs={{0,16},{8,24},{16,0},{24,8},{1,17},{9,25},{17,1},{25,9},{2,18},{10... | collective-permute-start | bytes 786440 | tf_op jit(solution)/shard_map/ppermute | solution.py:29

commit v7 on v6

--- a/solution.py
+++ b/solution.py
@@ -30,13 +30,9 @@
 
 
 def first_kernel(*refs):
-    a_refs, v_refs, (a_all, v_all, out, arrived) = refs[:8], refs[8:12], refs[12:]
+    a_refs, v_refs, (a_all, v_all, out) = refs[:8], refs[8:12], refs[12:]
     x, y, c = (lax.axis_index(name) for name in ("x", "ij", "c"))
-    kept = pltpu.make_async_copy(
-        a_refs[0], a_all.at[:, pl.ds(pl.multiple_of(y * 256, 256), 256)], arrived
-    )
-    kept.start()
-    for place, ref in zip((2, 4, 6, 1, 3, 5, 7), a_refs[1:]):
+    for place, ref in zip((0, 2, 4, 6, 1, 3, 5, 7), a_refs):
         start = pl.multiple_of((y + (2 * c - 1) * place + 8) % 8 * 256, 256)
         a_all[:, pl.ds(start, 256)] = ref[...]
     for s, t, ref in ((0, 0, v_refs[0]), (1, 0, v_refs[1]), (0, 1, v_refs[2]), (1, 1, v_refs[3])):
@@ -49,7 +45,6 @@
     def _():
         v_all[PAIRS - 6144 :, :] = jnp.zeros((8192 - PAIRS, 1024), jnp.bfloat16)
 
-    kept.wait()
     place_product(2, a_all, v_all, out)
 
 
@@ -77,9 +72,8 @@
             jax.ShapeDtypeStruct((2048, 1024), jnp.bfloat16),
             TERM,
         ),
-        in_specs=[pl.BlockSpec(memory_space=pl.ANY)] + [VMEM] * 11,
+        in_specs=[VMEM] * 12,
         out_specs=[VMEM] * 3,
-        scratch_shapes=[pltpu.SemaphoreType.DMA],
         compiler_params=pltpu.CompilerParams(vmem_limit_bytes=16 << 20),
         cost_estimate=pl.CostEstimate(
             flops=2 * 512 * 2048 * 256, bytes_accessed=12 << 20, transcendentals=0
@@ -100,25 +94,50 @@
     )(a_all, v_all)
 
 
-def untouched_kernel(given, out):
-    del given, out
+def copies_kernel(given, out, left):
+    sends = [pltpu.make_async_copy(given, out.at[i], left.at[i]) for i in range(8)]
+    for send in sends:
+        send.start()
+    for send in sends:
+        send.wait()
 
 
-def untouched(block):
+def copies(shard):
     return pl.pallas_call(
-        untouched_kernel,
-        out_shape=jax.ShapeDtypeStruct(block.shape, block.dtype),
-        in_specs=[pl.BlockSpec(memory_space=pl.ANY)],
+        copies_kernel,
+        out_shape=jax.ShapeDtypeStruct((8, *shard.shape), shard.dtype),
+        in_specs=[VMEM],
         out_specs=pl.BlockSpec(memory_space=pl.ANY),
+        scratch_shapes=[pltpu.SemaphoreType.DMA((8,))],
+        compiler_params=pltpu.CompilerParams(vmem_limit_bytes=2 << 20),
+        cost_estimate=pl.CostEstimate(
+            flops=1000, bytes_accessed=9 << 17, transcendentals=0
+        ),
+    )(shard)
+
+
+def kept_kernel(given, own, out, kept):
+    del given, out
+    kept[...] = own[...]
+
+
+def kept_beside(block, own):
+    shape = jax.ShapeDtypeStruct(block.shape, block.dtype)
+    anywhere = pl.BlockSpec(memory_space=pl.ANY)
+    return pl.pallas_call(
+        kept_kernel,
+        out_shape=(shape, shape),
+        in_specs=[anywhere, VMEM],
+        out_specs=[anywhere, VMEM],
         input_output_aliases={0: 0},
-        compiler_params=pltpu.CompilerParams(vmem_limit_bytes=1 << 20),
+        compiler_params=pltpu.CompilerParams(vmem_limit_bytes=2 << 20),
         cost_estimate=pl.CostEstimate(flops=1000, bytes_accessed=0, transcendentals=0),
-    )(block)
+    )(block, own)
 
 
 def staged(amplitudes, integrals):
     v00 = lax.all_to_all(
-        jnp.broadcast_to(integrals[None], (8, 64, 1024)), ("zl", "x"), 0, 0,
+        copies(integrals), ("zl", "x"), 0, 0,
         tiled=True, axis_index_groups=X_PARITY,
     )
     blocks = [amplitudes]
@@ -127,8 +146,9 @@
     for i in range(4):
         block = along_y(blocks[i], 1)
         if i == 0:
-            block = untouched(block)
+            block, kept = kept_beside(block, amplitudes)
         blocks.append(block)
+    blocks[0] = kept
     v10 = lax.ppermute(v00, ("x", "c"), X_HOP)
     v01 = lax.ppermute(v00, "c", SWAP)
     v11 = lax.ppermute(v10, "c", SWAP)

time: 150 us -> 138 us (0.920)
  the two profiles are of different devices: /device:TPU:1 before, /device:TPU:128 now
where the time goes in v7:
time: 138 us; the launch traced here: 137 us
  starting transfers between devices  57.6 us (42%)
  waiting for transfers between devices  37.2 us (27%)
  blocking collectives  34.7 us (25%)
  Pallas kernels  4.63 us (3%)
  local copies, waits for them, and re-layouts  1.85 us (1%)
    all_to_all x1, blocking collectives, staged(): lax.all_to_all(copies(integrals), ('zl', 'x'), 0, 0, tiled=True, axis_ind...  34.7 us
    ppermute x7, starting transfers between devices, along_y(): return lax.ppermute(shard, ('c', 'ij'), pairs)  29.2 us
    ppermute x3, starting transfers between devices, shifted(): lax.ppermute(term.astype(jnp.float16), 'kl', pairs).astype(jnp.float32)  22.2 us
    ppermute x3, waiting for transfers between devices, shifted(): lax.ppermute(term.astype(jnp.float16), 'kl', pairs).astype(jnp.float32)  18.7 us
    ppermute x7, waiting for transfers between devices, along_y(): return lax.ppermute(shard, ('c', 'ij'), pairs)  9.53 us
    ppermute x1, waiting for transfers between devices, staged(): v10 = lax.ppermute(v00, ('x', 'c'), X_HOP)  8.99 us
  transfers between devices with their start and end apart: 13, of which 7 were waited for; matrix products, arithmetic and copies ran while one was open for 0% of the time, Pallas kernels for 0%

profile of v7, /device:TPU:128, one launch (start us, length us, event | category | flops | bytes accessed | tf_op | source)
XLA Modules:
  0.0 137.2 jit_solution(14673465875477163119)
XLA Ops:
  0.0 0.0 copy-start.1
  0.0 0.9 copy-done.1
  0.9 1.4 %shard_map.29 = bf16[8,64,1024]{2,1,0:T(8,128)(2,1)S(1)} custom-call(bf16[64,1024]{1,0:T(8,128)(2,1)S(1)} %copy-done.1), custom_call_target="tpu_custom_call" | custom-call | flops 1000 | bytes 1179648 | tf_op jit(solution)/shard_map/pallas_call | solution.py:106
  2.3 34.7 %all_to_all.5.refs_8_ = bf16[8,64,1024]{2,1,0:T(8,128)(2,1)S(1)} all-to-all(bf16[8,64,1024]{2,1,0:T(8,128)(2,1)S(1)} %shard_map.29), channel_id=1, replica_groups={{0,128,256,384,512,640,768,896},{64,192,320,448,576,704,832,960},{1,129..., dimensions={0} | all-to-all | bytes 2097152 | tf_op jit(solution)/shard_map/all_to_all | solution.py:139
  37.0 1.9 %collective-permute-start.7 = (bf16[8,64,1024]{2,1,0:T(8,128)(2,1)S(1)}, bf16[8,64,1024]{2,1,0:T(8,128)(2,1)S(1)}, u32[]{:S(2)}, u32[]{:S(2)}) collective-permute-start(bf16[8,64,1024]{2,1,0:T(8,128)(2,1)S(1)} %all_to_all.5.refs_8_), channel_id=1, source_target_pairs={{0,64},{64,128},{128,192},{192,256},{256,320},{320,384},{384,448},... | collective-permute-start | bytes 3145736 | tf_op jit(solution)/shard_map/ppermute | solution.py:152
  38.9 4.5 %collective-permute-start.1 = (bf16[512,256]{1,0:T(8,128)(2,1)}, bf16[512,256]{1,0:T(8,128)(2,1)S(1)}, u32[]{:S(2)}, u32[]{:S(2)}) collective-permute-start(bf16[512,256]{1,0:T(8,128)(2,1)} %own.1), channel_id=1, source_target_pairs={{0,2},{1,3},{2,4},{3,5},{4,6},{5,7},{6,0},{7,1},{32,38},{33,39},{3... | collective-permute-start | bytes 786440 | tf_op jit(solution)/shard_map/ppermute | solution.py:24
  43.5 2.4 %collective-permute-start.8 = (bf16[8,64,1024]{2,1,0:T(8,128)(2,1)S(1)}, bf16[8,64,1024]{2,1,0:T(8,128)(2,1)S(1)}, u32[]{:S(2)}, u32[]{:S(2)}) collective-permute-start(bf16[8,64,1024]{2,1,0:T(8,128)(2,1)S(1)} %all_to_all.5.refs_8_), channel_id=1, source_target_pairs={{0,32},{32,0},{1,33},{33,1},{2,34},{34,2},{3,35},{35,3},{4,36},{36... | collective-permute-start | bytes 3145736 | tf_op jit(solution)/shard_map/ppermute | solution.py:153
  45.9 9.0 %collective-permute-done.7.refs_9_ = bf16[8,64,1024]{2,1,0:T(8,128)(2,1)S(1)} collective-permute-done((bf16[8,64,1024]{2,1,0:T(8,128)(2,1)S(1)}, bf16[8,64,1024]{2,1,0:T(8,128)(2,1)S(1)}, u32[]{:S(2)}, u32[]{:S(2)}) %collective-permute-start.7) | collective-permute-done | bytes 1048608 | tf_op jit(solution)/shard_map/ppermute | solution.py:152
  54.9 1.9 %collective-permute-start.9 = (bf16[8,64,1024]{2,1,0:T(8,128)(2,1)S(1)}, bf16[8,64,1024]{2,1,0:T(8,128)(2,1)S(1)}, u32[]{:S(2)}, u32[]{:S(2)}) collective-permute-start(bf16[8,64,1024]{2,1,0:T(8,128)(2,1)S(1)} %collective-permute-done.7.refs_9_), channel_id=1, source_target_pairs={{0,32},{32,0},{1,33},{33,1},{2,34},{34,2},{3,35},{35,3},{4,36},{36... | collective-permute-start | bytes 3145736 | tf_op jit(solution)/shard_map/ppermute | solution.py:154
  56.8 0.0 collective-permute-done.1.refs_1_
  56.8 4.5 %collective-permute-start.2 = (bf16[512,256]{1,0:T(8,128)(2,1)S(1)}, bf16[512,256]{1,0:T(8,128)(2,1)S(1)}, u32[]{:S(2)}, u32[]{:S(2)}) collective-permute-start(bf16[512,256]{1,0:T(8,128)(2,1)S(1)} %collective-permute-done.1.refs_1_), channel_id=1, source_target_pairs={{0,2},{1,3},{2,4},{3,5},{4,6},{5,7},{6,0},{7,1},{32,38},{33,39},{3... | collective-permute-start | bytes 786440 | tf_op jit(solution)/shard_map/ppermute | solution.py:24
  61.4 3.6 %collective-permute-start = (bf16[512,256]{1,0:T(8,128)(2,1)}, bf16[512,256]{1,0:T(8,128)(2,1)S(1)}, u32[]{:S(2)}, u32[]{:S(2)}) collective-permute-start(bf16[512,256]{1,0:T(8,128)(2,1)} %own.1), channel_id=1, source_target_pairs={{0,1},{1,2},{2,3},{3,4},{4,5},{5,6},{6,7},{7,0},{32,39},{33,32},{3... | collective-permute-start | bytes 786440 | tf_op jit(solution)/shard_map/ppermute | solution.py:24
  65.0 3.7 %collective-permute-done.2.refs_2_ = bf16[512,256]{1,0:T(8,128)(2,1)S(1)} collective-permute-done((bf16[512,256]{1,0:T(8,128)(2,1)S(1)}, bf16[512,256]{1,0:T(8,128)(2,1)S(1)}, u32[]{:S(2)}, u32[]{:S(2)}) %collective-permute-start.2) | collective-permute-done | bytes 262176 | tf_op jit(solution)/shard_map/ppermute | solution.py:24
  68.7 4.8 %collective-permute-start.3 = (bf16[512,256]{1,0:T(8,128)(2,1)S(1)}, bf16[512,256]{1,0:T(8,128)(2,1)S(1)}, u32[]{:S(2)}, u32[]{:S(2)}) collective-permute-start(bf16[512,256]{1,0:T(8,128)(2,1)S(1)} %collective-permute-done.2.refs_2_), channel_id=1, source_target_pairs={{0,2},{1,3},{2,4},{3,5},{4,6},{5,7},{6,0},{7,1},{32,38},{33,39},{3... | collective-permute-start | bytes 786440 | tf_op jit(solution)/shard_map/ppermute | solution.py:24
  73.5 3.3 %collective-permute-start.4 = (bf16[512,256]{1,0:T(8,128)(2,1)S(1)}, bf16[512,256]{1,0:T(8,128)(2,1)S(1)}, u32[]{:S(2)}, u32[]{:S(2)}) collective-permute-start(bf16[512,256]{1,0:T(8,128)(2,1)S(1)} %collective-permute-done.1.refs_1_), channel_id=1, source_target_pairs={{0,1},{1,2},{2,3},{3,4},{4,5},{5,6},{6,7},{7,0},{32,39},{33,32},{3... | collective-permute-start | bytes 786440 | tf_op jit(solution)/shard_map/ppermute | solution.py:24
  76.8 0.0 collective-permute-done.given
  76.8 5.7 %collective-permute-start.5 = (bf16[512,256]{1,0:T(8,128)(2,1)S(1)}, bf16[512,256]{1,0:T(8,128)(2,1)S(1)}, u32[]{:S(2)}, u32[]{:S(2)}) collective-permute-start(bf16[512,256]{1,0:T(8,128)(2,1)S(1)} %collective-permute-done.2.refs_2_), channel_id=1, source_target_pairs={{0,1},{1,2},{2,3},{3,4},{4,5},{5,6},{6,7},{7,0},{32,39},{33,32},{3... | collective-permute-start | bytes 786440 | tf_op jit(solution)/shard_map/ppermute | solution.py:24
  82.6 0.0 collective-permute-done.3.refs_3_
  82.6 2.6 %collective-permute-start.6 = (bf16[512,256]{1,0:T(8,128)(2,1)S(1)}, bf16[512,256]{1,0:T(8,128)(2,1)S(1)}, u32[]{:S(2)}, u32[]{:S(2)}) collective-permute-start(bf16[512,256]{1,0:T(8,128)(2,1)S(1)} %collective-permute-done.3.refs_3_), channel_id=1, source_target_pairs={{0,1},{1,2},{2,3},{3,4},{4,5},{5,6},{6,7},{7,0},{32,39},{33,32},{3... | collective-permute-start | bytes 786440 | tf_op jit(solution)/shard_map/ppermute | solution.py:24
  85.2 0.0 copy-start
  85.2 0.9 copy-done
  86.2 0.0 collective-permute-done.4.refs_5_
  86.2 1.3 collective-permute-done.5.refs_6_
  87.4 4.6 %collective-permute-done.6.refs_7_ = bf16[512,256]{1,0:T(8,128)(2,1)S(1)} collective-permute-done((bf16[512,256]{1,0:T(8,128)(2,1)S(1)}, bf16[512,256]{1,0:T(8,128)(2,1)S(1)}, u32[]{:S(2)}, u32[]{:S(2)}) %collective-permute-start.6) | collective-permute-done | bytes 262176 | tf_op jit(solution)/shard_map/ppermute | solution.py:24
  92.0 0.0 collective-permute-done.8.refs_10_
  92.0 0.0 collective-permute-done.9.refs_11_
  92.0 1.4 shard_map.30
  93.4 1.9 %shard_map.31 = (f32[512,256]{1,0:T(8,128)S(1)}, f32[512,256]{1,0:T(8,128)S(1)}, f32[512,256]{1,0:T(8,128)S(1)}) custom-call(bf16[512,2048]{1,0:T(8,128)(2,1)S(1)} %get-tuple-element.15.a_all, bf16[2048,1024]{1,0:T(8,128)(2,1)S(1)} %get-tuple-element.16.v_all), custom_call_target="tpu_custom_call" | custom-call | flops 1610612736 | bytes 8388608 | tf_op jit(solution)/shard_map/pallas_call | solution.py:85
  95.3 7.9 %collective-permute-start.10 = (f16[512,256]{1,0:T(8,128)(2,1)S(1)}, f16[512,256]{1,0:T(8,128)(2,1)S(1)}, u32[]{:S(2)}, u32[]{:S(2)}) collective-permute-start(f16[512,256]{1,0:T(8,128)(2,1)S(1)} %convert_element_type.18), channel_id=1, source_target_pairs={{0,8},{8,16},{16,24},{24,0},{1,9},{9,17},{17,25},{25,1},{2,10},{10... | collective-permute-start | bytes 786440 | tf_op jit(solution)/shard_map/ppermute | solution.py:29
  103.3 10.0 %collective-permute-start.11 = (f16[512,256]{1,0:T(8,128)(2,1)S(1)}, f16[512,256]{1,0:T(8,128)(2,1)S(1)}, u32[]{:S(2)}, u32[]{:S(2)}) collective-permute-start(f16[512,256]{1,0:T(8,128)(2,1)S(1)} %convert_element_type.20), channel_id=1, source_target_pairs={{0,24},{8,0},{16,8},{24,16},{1,25},{9,1},{17,9},{25,17},{2,26},{10... | collective-permute-start | bytes 786440 | tf_op jit(solution)/shard_map/ppermute | solution.py:29
  113.3 4.3 %collective-permute-start.12 = (f16[512,256]{1,0:T(8,128)(2,1)S(1)}, f16[512,256]{1,0:T(8,128)(2,1)S(1)}, u32[]{:S(2)}, u32[]{:S(2)}) collective-permute-start(f16[512,256]{1,0:T(8,128)(2,1)S(1)} %convert_element_type.22), channel_id=1, source_target_pairs={{0,16},{8,24},{16,0},{24,8},{1,17},{9,25},{17,1},{25,9},{2,18},{10... | collective-permute-start | bytes 786440 | tf_op jit(solution)/shard_map/ppermute | solution.py:29
  117.6 0.9 collective-permute-done.10
  118.5 11.9 %collective-permute-done.11 = f16[512,256]{1,0:T(8,128)(2,1)S(1)} collective-permute-done((f16[512,256]{1,0:T(8,128)(2,1)S(1)}, f16[512,256]{1,0:T(8,128)(2,1)S(1)}, u32[]{:S(2)}, u32[]{:S(2)}) %collective-permute-start.11) | collective-permute-done | bytes 262176 | tf_op jit(solution)/shard_map/ppermute | solution.py:29
  130.4 5.9 %collective-permute-done.12 = f16[512,256]{1,0:T(8,128)(2,1)S(1)} collective-permute-done((f16[512,256]{1,0:T(8,128)(2,1)S(1)}, f16[512,256]{1,0:T(8,128)(2,1)S(1)}, u32[]{:S(2)}, u32[]{:S(2)}) %collective-permute-start.12) | collective-permute-done | bytes 262176 | tf_op jit(solution)/shard_map/ppermute | solution.py:29
  136.3 0.9 multiply_select_fusion
  (5 shorter events, 0.1 us)
Async XLA Ops:
  0.0 0.9 copy-start.1
  37.0 17.9 %collective-permute-start.7 = (bf16[8,64,1024]{2,1,0:T(8,128)(2,1)S(1)}, bf16[8,64,1024]{2,1,0:T(8,128)(2,1)S(1)}, u32[]{:S(2)}, u32[]{:S(2)}) collective-permute-start(bf16[8,64,1024]{2,1,0:T(8,128)(2,1)S(1)} %all_to_all.5.refs_8_), channel_id=1, source_target_pairs={{0,64},{64,128},{128,192},{192,256},{256,320},{320,384},{384,448},... | collective-permute-start | bytes 3145736 | tf_op jit(solution)/shard_map/ppermute | solution.py:152
  38.9 17.9 %collective-permute-start.1 = (bf16[512,256]{1,0:T(8,128)(2,1)}, bf16[512,256]{1,0:T(8,128)(2,1)S(1)}, u32[]{:S(2)}, u32[]{:S(2)}) collective-permute-start(bf16[512,256]{1,0:T(8,128)(2,1)} %own.1), channel_id=1, source_target_pairs={{0,2},{1,3},{2,4},{3,5},{4,6},{5,7},{6,0},{7,1},{32,38},{33,39},{3... | collective-permute-start | bytes 786440 | tf_op jit(solution)/shard_map/ppermute | solution.py:24
  43.5 48.6 %collective-permute-start.8 = (bf16[8,64,1024]{2,1,0:T(8,128)(2,1)S(1)}, bf16[8,64,1024]{2,1,0:T(8,128)(2,1)S(1)}, u32[]{:S(2)}, u32[]{:S(2)}) collective-permute-start(bf16[8,64,1024]{2,1,0:T(8,128)(2,1)S(1)} %all_to_all.5.refs_8_), channel_id=1, source_target_pairs={{0,32},{32,0},{1,33},{33,1},{2,34},{34,2},{3,35},{35,3},{4,36},{36... | collective-permute-start | bytes 3145736 | tf_op jit(solution)/shard_map/ppermute | solution.py:153
  54.9 37.1 %collective-permute-start.9 = (bf16[8,64,1024]{2,1,0:T(8,128)(2,1)S(1)}, bf16[8,64,1024]{2,1,0:T(8,128)(2,1)S(1)}, u32[]{:S(2)}, u32[]{:S(2)}) collective-permute-start(bf16[8,64,1024]{2,1,0:T(8,128)(2,1)S(1)} %collective-permute-done.7.refs_9_), channel_id=1, source_target_pairs={{0,32},{32,0},{1,33},{33,1},{2,34},{34,2},{3,35},{35,3},{4,36},{36... | collective-permute-start | bytes 3145736 | tf_op jit(solution)/shard_map/ppermute | solution.py:154
  56.8 11.8 %collective-permute-start.2 = (bf16[512,256]{1,0:T(8,128)(2,1)S(1)}, bf16[512,256]{1,0:T(8,128)(2,1)S(1)}, u32[]{:S(2)}, u32[]{:S(2)}) collective-permute-start(bf16[512,256]{1,0:T(8,128)(2,1)S(1)} %collective-permute-done.1.refs_1_), channel_id=1, source_target_pairs={{0,2},{1,3},{2,4},{3,5},{4,6},{5,7},{6,0},{7,1},{32,38},{33,39},{3... | collective-permute-start | bytes 786440 | tf_op jit(solution)/shard_map/ppermute | solution.py:24
  61.4 15.4 %collective-permute-start = (bf16[512,256]{1,0:T(8,128)(2,1)}, bf16[512,256]{1,0:T(8,128)(2,1)S(1)}, u32[]{:S(2)}, u32[]{:S(2)}) collective-permute-start(bf16[512,256]{1,0:T(8,128)(2,1)} %own.1), channel_id=1, source_target_pairs={{0,1},{1,2},{2,3},{3,4},{4,5},{5,6},{6,7},{7,0},{32,39},{33,32},{3... | collective-permute-start | bytes 786440 | tf_op jit(solution)/shard_map/ppermute | solution.py:24
  68.7 13.9 %collective-permute-start.3 = (bf16[512,256]{1,0:T(8,128)(2,1)S(1)}, bf16[512,256]{1,0:T(8,128)(2,1)S(1)}, u32[]{:S(2)}, u32[]{:S(2)}) collective-permute-start(bf16[512,256]{1,0:T(8,128)(2,1)S(1)} %collective-permute-done.2.refs_2_), channel_id=1, source_target_pairs={{0,2},{1,3},{2,4},{3,5},{4,6},{5,7},{6,0},{7,1},{32,38},{33,39},{3... | collective-permute-start | bytes 786440 | tf_op jit(solution)/shard_map/ppermute | solution.py:24
  73.5 12.7 %collective-permute-start.4 = (bf16[512,256]{1,0:T(8,128)(2,1)S(1)}, bf16[512,256]{1,0:T(8,128)(2,1)S(1)}, u32[]{:S(2)}, u32[]{:S(2)}) collective-permute-start(bf16[512,256]{1,0:T(8,128)(2,1)S(1)} %collective-permute-done.1.refs_1_), channel_id=1, source_target_pairs={{0,1},{1,2},{2,3},{3,4},{4,5},{5,6},{6,7},{7,0},{32,39},{33,32},{3... | collective-permute-start | bytes 786440 | tf_op jit(solution)/shard_map/ppermute | solution.py:24
  76.8 10.6 %collective-permute-start.5 = (bf16[512,256]{1,0:T(8,128)(2,1)S(1)}, bf16[512,256]{1,0:T(8,128)(2,1)S(1)}, u32[]{:S(2)}, u32[]{:S(2)}) collective-permute-start(bf16[512,256]{1,0:T(8,128)(2,1)S(1)} %collective-permute-done.2.refs_2_), channel_id=1, source_target_pairs={{0,1},{1,2},{2,3},{3,4},{4,5},{5,6},{6,7},{7,0},{32,39},{33,32},{3... | collective-permute-start | bytes 786440 | tf_op jit(solution)/shard_map/ppermute | solution.py:24
  82.6 9.5 %collective-permute-start.6 = (bf16[512,256]{1,0:T(8,128)(2,1)S(1)}, bf16[512,256]{1,0:T(8,128)(2,1)S(1)}, u32[]{:S(2)}, u32[]{:S(2)}) collective-permute-start(bf16[512,256]{1,0:T(8,128)(2,1)S(1)} %collective-permute-done.3.refs_3_), channel_id=1, source_target_pairs={{0,1},{1,2},{2,3},{3,4},{4,5},{5,6},{6,7},{7,0},{32,39},{33,32},{3... | collective-permute-start | bytes 786440 | tf_op jit(solution)/shard_map/ppermute | solution.py:24
  85.2 1.0 copy-start
  95.3 23.2 %collective-permute-start.10 = (f16[512,256]{1,0:T(8,128)(2,1)S(1)}, f16[512,256]{1,0:T(8,128)(2,1)S(1)}, u32[]{:S(2)}, u32[]{:S(2)}) collective-permute-start(f16[512,256]{1,0:T(8,128)(2,1)S(1)} %convert_element_type.18), channel_id=1, source_target_pairs={{0,8},{8,16},{16,24},{24,0},{1,9},{9,17},{17,25},{25,1},{2,10},{10... | collective-permute-start | bytes 786440 | tf_op jit(solution)/shard_map/ppermute | solution.py:29
  103.3 27.1 %collective-permute-start.11 = (f16[512,256]{1,0:T(8,128)(2,1)S(1)}, f16[512,256]{1,0:T(8,128)(2,1)S(1)}, u32[]{:S(2)}, u32[]{:S(2)}) collective-permute-start(f16[512,256]{1,0:T(8,128)(2,1)S(1)} %convert_element_type.20), channel_id=1, source_target_pairs={{0,24},{8,0},{16,8},{24,16},{1,25},{9,1},{17,9},{25,17},{2,26},{10... | collective-permute-start | bytes 786440 | tf_op jit(solution)/shard_map/ppermute | solution.py:29
  113.3 23.0 %collective-permute-start.12 = (f16[512,256]{1,0:T(8,128)(2,1)S(1)}, f16[512,256]{1,0:T(8,128)(2,1)S(1)}, u32[]{:S(2)}, u32[]{:S(2)}) collective-permute-start(f16[512,256]{1,0:T(8,128)(2,1)S(1)} %convert_element_type.22), channel_id=1, source_target_pairs={{0,16},{8,24},{16,0},{24,8},{1,17},{9,25},{17,1},{25,9},{2,18},{10... | collective-permute-start | bytes 786440 | tf_op jit(solution)/shard_map/ppermute | solution.py:29

commit v8 on v7

--- a/solution.py
+++ b/solution.py
@@ -32,7 +32,7 @@
 def first_kernel(*refs):
     a_refs, v_refs, (a_all, v_all, out) = refs[:8], refs[8:12], refs[12:]
     x, y, c = (lax.axis_index(name) for name in ("x", "ij", "c"))
-    for place, ref in zip((0, 2, 4, 6, 1, 3, 5, 7), a_refs):
+    for place, ref in enumerate(a_refs):
         start = pl.multiple_of((y + (2 * c - 1) * place + 8) % 8 * 256, 256)
         a_all[:, pl.ds(start, 256)] = ref[...]
     for s, t, ref in ((0, 0, v_refs[0]), (1, 0, v_refs[1]), (0, 1, v_refs[2]), (1, 1, v_refs[3])):
@@ -140,15 +140,15 @@
         copies(integrals), ("zl", "x"), 0, 0,
         tiled=True, axis_index_groups=X_PARITY,
     )
-    blocks = [amplitudes]
-    for i in range(3):
-        blocks.append(along_y(blocks[i], 2))
-    for i in range(4):
-        block = along_y(blocks[i], 1)
-        if i == 0:
-            block, kept = kept_beside(block, amplitudes)
-        blocks.append(block)
-    blocks[0] = kept
+    two = along_y(amplitudes, 2)
+    one = along_y(amplitudes, 1)
+    one, kept = kept_beside(one, amplitudes)
+    seven = along_y(amplitudes, -1)
+    six = along_y(amplitudes, -2)
+    three = along_y(two, 1)
+    four = along_y(two, 2)
+    five = along_y(six, -1)
+    blocks = [kept, one, two, three, four, five, six, seven]
     v10 = lax.ppermute(v00, ("x", "c"), X_HOP)
     v01 = lax.ppermute(v00, "c", SWAP)
     v11 = lax.ppermute(v10, "c", SWAP)

time: 138 us -> 145 us (1.051)
  the two profiles are of different devices: /device:TPU:128 before, /device:TPU:145 now
where the time goes in v8:
time: 145 us; the launch traced here: 144 us
  starting transfers between devices  62.1 us (43%)
  waiting for transfers between devices  41.2 us (28%)
  blocking collectives  33.4 us (23%)
  Pallas kernels  4.63 us (3%)
  local copies, waits for them, and re-layouts  1.85 us (1%)
    all_to_all x1, blocking collectives, staged(): lax.all_to_all(copies(integrals), ('zl', 'x'), 0, 0, tiled=True, axis_ind...  33.4 us
    ppermute x7, starting transfers between devices, along_y(): return lax.ppermute(shard, ('c', 'ij'), pairs)  29.9 us
    ppermute x3, waiting for transfers between devices, shifted(): lax.ppermute(term.astype(jnp.float16), 'kl', pairs).astype(jnp.float32)  21.5 us
    ppermute x3, starting transfers between devices, shifted(): lax.ppermute(term.astype(jnp.float16), 'kl', pairs).astype(jnp.float32)  20.8 us
    ppermute x1, waiting for transfers between devices, staged(): v10 = lax.ppermute(v00, ('x', 'c'), X_HOP)  10.2 us
    ppermute x7, waiting for transfers between devices, along_y(): return lax.ppermute(shard, ('c', 'ij'), pairs)  9.58 us
    ppermute x1, starting transfers between devices, staged(): v11 = lax.ppermute(v10, 'c', SWAP)  5.8 us
    ppermute x1, starting transfers between devices, staged(): v01 = lax.ppermute(v00, 'c', SWAP)  3.74 us
  transfers between devices with their start and end apart: 13, of which 7 were waited for; matrix products, arithmetic and copies ran while one was open for 0% of the time, Pallas kernels for 0%

profile of v8, /device:TPU:145, one launch (start us, length us, event | category | flops | bytes accessed | tf_op | source)
XLA Modules:
  0.0 144.4 jit_solution(4043873408983127540)
XLA Ops:
  0.0 0.0 copy-start.1
  0.0 0.9 copy-done.1
  0.9 1.4 shard_map.29
  2.3 33.4 %all_to_all.5.refs_8_ = bf16[8,64,1024]{2,1,0:T(8,128)(2,1)S(1)} all-to-all(bf16[8,64,1024]{2,1,0:T(8,128)(2,1)S(1)} %shard_map.29), channel_id=1, replica_groups={{0,128,256,384,512,640,768,896},{64,192,320,448,576,704,832,960},{1,129..., dimensions={0} | all-to-all | bytes 2097152 | tf_op jit(solution)/shard_map/all_to_all | solution.py:139
  35.7 1.9 %collective-permute-start.7 = (bf16[8,64,1024]{2,1,0:T(8,128)(2,1)S(1)}, bf16[8,64,1024]{2,1,0:T(8,128)(2,1)S(1)}, u32[]{:S(2)}, u32[]{:S(2)}) collective-permute-start(bf16[8,64,1024]{2,1,0:T(8,128)(2,1)S(1)} %all_to_all.5.refs_8_), channel_id=1, source_target_pairs={{0,64},{64,128},{128,192},{192,256},{256,320},{320,384},{384,448},... | collective-permute-start | bytes 3145736 | tf_op jit(solution)/shard_map/ppermute | solution.py:152
  37.6 3.7 %collective-permute-start.8 = (bf16[8,64,1024]{2,1,0:T(8,128)(2,1)S(1)}, bf16[8,64,1024]{2,1,0:T(8,128)(2,1)S(1)}, u32[]{:S(2)}, u32[]{:S(2)}) collective-permute-start(bf16[8,64,1024]{2,1,0:T(8,128)(2,1)S(1)} %all_to_all.5.refs_8_), channel_id=1, source_target_pairs={{0,32},{32,0},{1,33},{33,1},{2,34},{34,2},{3,35},{35,3},{4,36},{36... | collective-permute-start | bytes 3145736 | tf_op jit(solution)/shard_map/ppermute | solution.py:153
  41.3 10.2 %collective-permute-done.7.refs_9_ = bf16[8,64,1024]{2,1,0:T(8,128)(2,1)S(1)} collective-permute-done((bf16[8,64,1024]{2,1,0:T(8,128)(2,1)S(1)}, bf16[8,64,1024]{2,1,0:T(8,128)(2,1)S(1)}, u32[]{:S(2)}, u32[]{:S(2)}) %collective-permute-start.7) | collective-permute-done | bytes 1048608 | tf_op jit(solution)/shard_map/ppermute | solution.py:152
  51.5 5.8 %collective-permute-start.9 = (bf16[8,64,1024]{2,1,0:T(8,128)(2,1)S(1)}, bf16[8,64,1024]{2,1,0:T(8,128)(2,1)S(1)}, u32[]{:S(2)}, u32[]{:S(2)}) collective-permute-start(bf16[8,64,1024]{2,1,0:T(8,128)(2,1)S(1)} %collective-permute-done.7.refs_9_), channel_id=1, source_target_pairs={{0,32},{32,0},{1,33},{33,1},{2,34},{34,2},{3,35},{35,3},{4,36},{36... | collective-permute-start | bytes 3145736 | tf_op jit(solution)/shard_map/ppermute | solution.py:154
  57.3 5.7 %collective-permute-start.1 = (bf16[512,256]{1,0:T(8,128)(2,1)}, bf16[512,256]{1,0:T(8,128)(2,1)S(1)}, u32[]{:S(2)}, u32[]{:S(2)}) collective-permute-start(bf16[512,256]{1,0:T(8,128)(2,1)} %own.1), channel_id=1, source_target_pairs={{0,2},{1,3},{2,4},{3,5},{4,6},{5,7},{6,0},{7,1},{32,38},{33,39},{3... | collective-permute-start | bytes 786440 | tf_op jit(solution)/shard_map/ppermute | solution.py:24
  63.0 2.9 %collective-permute-start = (bf16[512,256]{1,0:T(8,128)(2,1)}, bf16[512,256]{1,0:T(8,128)(2,1)S(1)}, u32[]{:S(2)}, u32[]{:S(2)}) collective-permute-start(bf16[512,256]{1,0:T(8,128)(2,1)} %own.1), channel_id=1, source_target_pairs={{0,1},{1,2},{2,3},{3,4},{4,5},{5,6},{6,7},{7,0},{32,39},{33,32},{3... | collective-permute-start | bytes 786440 | tf_op jit(solution)/shard_map/ppermute | solution.py:24
  65.8 1.9 %collective-permute-start.4 = (bf16[512,256]{1,0:T(8,128)(2,1)}, bf16[512,256]{1,0:T(8,128)(2,1)S(1)}, u32[]{:S(2)}, u32[]{:S(2)}) collective-permute-start(bf16[512,256]{1,0:T(8,128)(2,1)} %own.1), channel_id=1, source_target_pairs={{0,6},{1,7},{2,0},{3,1},{4,2},{5,3},{6,4},{7,5},{32,34},{33,35},{3... | collective-permute-start | bytes 786440 | tf_op jit(solution)/shard_map/ppermute | solution.py:24
  67.8 0.4 collective-permute-done.1.refs_2_
  68.2 4.8 %collective-permute-start.6 = (bf16[512,256]{1,0:T(8,128)(2,1)}, bf16[512,256]{1,0:T(8,128)(2,1)S(1)}, u32[]{:S(2)}, u32[]{:S(2)}) collective-permute-start(bf16[512,256]{1,0:T(8,128)(2,1)} %own.1), channel_id=1, source_target_pairs={{0,7},{1,0},{2,1},{3,2},{4,3},{5,4},{6,5},{7,6},{32,33},{33,34},{3... | collective-permute-start | bytes 786440 | tf_op jit(solution)/shard_map/ppermute | solution.py:24
  73.1 1.8 %collective-permute-done.given = bf16[512,256]{1,0:T(8,128)(2,1)S(1)} collective-permute-done((bf16[512,256]{1,0:T(8,128)(2,1)}, bf16[512,256]{1,0:T(8,128)(2,1)S(1)}, u32[]{:S(2)}, u32[]{:S(2)}) %collective-permute-start) | collective-permute-done | bytes 262176 | tf_op jit(solution)/shard_map/ppermute | solution.py:24
  74.8 6.1 %collective-permute-start.2 = (bf16[512,256]{1,0:T(8,128)(2,1)S(1)}, bf16[512,256]{1,0:T(8,128)(2,1)S(1)}, u32[]{:S(2)}, u32[]{:S(2)}) collective-permute-start(bf16[512,256]{1,0:T(8,128)(2,1)S(1)} %collective-permute-done.1.refs_2_), channel_id=1, source_target_pairs={{0,1},{1,2},{2,3},{3,4},{4,5},{5,6},{6,7},{7,0},{32,39},{33,32},{3... | collective-permute-start | bytes 786440 | tf_op jit(solution)/shard_map/ppermute | solution.py:24
  81.0 0.0 collective-permute-done.4.refs_6_
  81.0 5.1 %collective-permute-start.3 = (bf16[512,256]{1,0:T(8,128)(2,1)S(1)}, bf16[512,256]{1,0:T(8,128)(2,1)S(1)}, u32[]{:S(2)}, u32[]{:S(2)}) collective-permute-start(bf16[512,256]{1,0:T(8,128)(2,1)S(1)} %collective-permute-done.1.refs_2_), channel_id=1, source_target_pairs={{0,2},{1,3},{2,4},{3,5},{4,6},{5,7},{6,0},{7,1},{32,38},{33,39},{3... | collective-permute-start | bytes 786440 | tf_op jit(solution)/shard_map/ppermute | solution.py:24
  86.1 0.0 collective-permute-done.6.refs_7_
  86.1 3.4 %collective-permute-start.5 = (bf16[512,256]{1,0:T(8,128)(2,1)S(1)}, bf16[512,256]{1,0:T(8,128)(2,1)S(1)}, u32[]{:S(2)}, u32[]{:S(2)}) collective-permute-start(bf16[512,256]{1,0:T(8,128)(2,1)S(1)} %collective-permute-done.4.refs_6_), channel_id=1, source_target_pairs={{0,7},{1,0},{2,1},{3,2},{4,3},{5,4},{6,5},{7,6},{32,33},{33,34},{3... | collective-permute-start | bytes 786440 | tf_op jit(solution)/shard_map/ppermute | solution.py:24
  89.4 0.0 copy-start
  89.5 0.9 copy-done
  90.4 0.0 collective-permute-done.2.refs_3_
  90.4 1.6 %collective-permute-done.3.refs_4_ = bf16[512,256]{1,0:T(8,128)(2,1)S(1)} collective-permute-done((bf16[512,256]{1,0:T(8,128)(2,1)S(1)}, bf16[512,256]{1,0:T(8,128)(2,1)S(1)}, u32[]{:S(2)}, u32[]{:S(2)}) %collective-permute-start.3) | collective-permute-done | bytes 262176 | tf_op jit(solution)/shard_map/ppermute | solution.py:24
  92.1 5.8 %collective-permute-done.5.refs_5_ = bf16[512,256]{1,0:T(8,128)(2,1)S(1)} collective-permute-done((bf16[512,256]{1,0:T(8,128)(2,1)S(1)}, bf16[512,256]{1,0:T(8,128)(2,1)S(1)}, u32[]{:S(2)}, u32[]{:S(2)}) %collective-permute-start.5) | collective-permute-done | bytes 262176 | tf_op jit(solution)/shard_map/ppermute | solution.py:24
  97.8 0.0 collective-permute-done.8.refs_10_
  97.8 0.0 collective-permute-done.9.refs_11_
  97.8 1.4 shard_map.30
  99.2 1.8 %shard_map.31 = (f32[512,256]{1,0:T(8,128)S(1)}, f32[512,256]{1,0:T(8,128)S(1)}, f32[512,256]{1,0:T(8,128)S(1)}) custom-call(bf16[512,2048]{1,0:T(8,128)(2,1)S(1)} %get-tuple-element.15.a_all, bf16[2048,1024]{1,0:T(8,128)(2,1)S(1)} %get-tuple-element.16.v_all), custom_call_target="tpu_custom_call" | custom-call | flops 1610612736 | bytes 8388608 | tf_op jit(solution)/shard_map/pallas_call | solution.py:85
  101.1 7.6 %collective-permute-start.10 = (f16[512,256]{1,0:T(8,128)(2,1)S(1)}, f16[512,256]{1,0:T(8,128)(2,1)S(1)}, u32[]{:S(2)}, u32[]{:S(2)}) collective-permute-start(f16[512,256]{1,0:T(8,128)(2,1)S(1)} %convert_element_type.18), channel_id=1, source_target_pairs={{0,8},{8,16},{16,24},{24,0},{1,9},{9,17},{17,25},{25,1},{2,10},{10... | collective-permute-start | bytes 786440 | tf_op jit(solution)/shard_map/ppermute | solution.py:29
  108.8 7.9 %collective-permute-start.11 = (f16[512,256]{1,0:T(8,128)(2,1)S(1)}, f16[512,256]{1,0:T(8,128)(2,1)S(1)}, u32[]{:S(2)}, u32[]{:S(2)}) collective-permute-start(f16[512,256]{1,0:T(8,128)(2,1)S(1)} %convert_element_type.20), channel_id=1, source_target_pairs={{0,24},{8,0},{16,8},{24,16},{1,25},{9,1},{17,9},{25,17},{2,26},{10... | collective-permute-start | bytes 786440 | tf_op jit(solution)/shard_map/ppermute | solution.py:29
  116.7 5.3 %collective-permute-start.12 = (f16[512,256]{1,0:T(8,128)(2,1)S(1)}, f16[512,256]{1,0:T(8,128)(2,1)S(1)}, u32[]{:S(2)}, u32[]{:S(2)}) collective-permute-start(f16[512,256]{1,0:T(8,128)(2,1)S(1)} %convert_element_type.22), channel_id=1, source_target_pairs={{0,16},{8,24},{16,0},{24,8},{1,17},{9,25},{17,1},{25,9},{2,18},{10... | collective-permute-start | bytes 786440 | tf_op jit(solution)/shard_map/ppermute | solution.py:29
  122.0 2.3 %collective-permute-done.10 = f16[512,256]{1,0:T(8,128)(2,1)S(1)} collective-permute-done((f16[512,256]{1,0:T(8,128)(2,1)S(1)}, f16[512,256]{1,0:T(8,128)(2,1)S(1)}, u32[]{:S(2)}, u32[]{:S(2)}) %collective-permute-start.10) | collective-permute-done | bytes 262176 | tf_op jit(solution)/shard_map/ppermute | solution.py:29
  124.3 0.0 collective-permute-done.11
  124.3 19.1 %collective-permute-done.12 = f16[512,256]{1,0:T(8,128)(2,1)S(1)} collective-permute-done((f16[512,256]{1,0:T(8,128)(2,1)S(1)}, f16[512,256]{1,0:T(8,128)(2,1)S(1)}, u32[]{:S(2)}, u32[]{:S(2)}) %collective-permute-start.12) | collective-permute-done | bytes 262176 | tf_op jit(solution)/shard_map/ppermute | solution.py:29
  143.5 0.9 multiply_select_fusion
  (5 shorter events, 0.1 us)
Async XLA Ops:
  0.0 0.9 copy-start.1
  35.7 15.8 %collective-permute-start.7 = (bf16[8,64,1024]{2,1,0:T(8,128)(2,1)S(1)}, bf16[8,64,1024]{2,1,0:T(8,128)(2,1)S(1)}, u32[]{:S(2)}, u32[]{:S(2)}) collective-permute-start(bf16[8,64,1024]{2,1,0:T(8,128)(2,1)S(1)} %all_to_all.5.refs_8_), channel_id=1, source_target_pairs={{0,64},{64,128},{128,192},{192,256},{256,320},{320,384},{384,448},... | collective-permute-start | bytes 3145736 | tf_op jit(solution)/shard_map/ppermute | solution.py:152
  37.6 60.2 %collective-permute-start.8 = (bf16[8,64,1024]{2,1,0:T(8,128)(2,1)S(1)}, bf16[8,64,1024]{2,1,0:T(8,128)(2,1)S(1)}, u32[]{:S(2)}, u32[]{:S(2)}) collective-permute-start(bf16[8,64,1024]{2,1,0:T(8,128)(2,1)S(1)} %all_to_all.5.refs_8_), channel_id=1, source_target_pairs={{0,32},{32,0},{1,33},{33,1},{2,34},{34,2},{3,35},{35,3},{4,36},{36... | collective-permute-start | bytes 3145736 | tf_op jit(solution)/shard_map/ppermute | solution.py:153
  51.5 46.3 %collective-permute-start.9 = (bf16[8,64,1024]{2,1,0:T(8,128)(2,1)S(1)}, bf16[8,64,1024]{2,1,0:T(8,128)(2,1)S(1)}, u32[]{:S(2)}, u32[]{:S(2)}) collective-permute-start(bf16[8,64,1024]{2,1,0:T(8,128)(2,1)S(1)} %collective-permute-done.7.refs_9_), channel_id=1, source_target_pairs={{0,32},{32,0},{1,33},{33,1},{2,34},{34,2},{3,35},{35,3},{4,36},{36... | collective-permute-start | bytes 3145736 | tf_op jit(solution)/shard_map/ppermute | solution.py:154
  57.3 10.9 %collective-permute-start.1 = (bf16[512,256]{1,0:T(8,128)(2,1)}, bf16[512,256]{1,0:T(8,128)(2,1)S(1)}, u32[]{:S(2)}, u32[]{:S(2)}) collective-permute-start(bf16[512,256]{1,0:T(8,128)(2,1)} %own.1), channel_id=1, source_target_pairs={{0,2},{1,3},{2,4},{3,5},{4,6},{5,7},{6,0},{7,1},{32,38},{33,39},{3... | collective-permute-start | bytes 786440 | tf_op jit(solution)/shard_map/ppermute | solution.py:24
  63.0 11.8 %collective-permute-start = (bf16[512,256]{1,0:T(8,128)(2,1)}, bf16[512,256]{1,0:T(8,128)(2,1)S(1)}, u32[]{:S(2)}, u32[]{:S(2)}) collective-permute-start(bf16[512,256]{1,0:T(8,128)(2,1)} %own.1), channel_id=1, source_target_pairs={{0,1},{1,2},{2,3},{3,4},{4,5},{5,6},{6,7},{7,0},{32,39},{33,32},{3... | collective-permute-start | bytes 786440 | tf_op jit(solution)/shard_map/ppermute | solution.py:24
  65.8 15.1 %collective-permute-start.4 = (bf16[512,256]{1,0:T(8,128)(2,1)}, bf16[512,256]{1,0:T(8,128)(2,1)S(1)}, u32[]{:S(2)}, u32[]{:S(2)}) collective-permute-start(bf16[512,256]{1,0:T(8,128)(2,1)} %own.1), channel_id=1, source_target_pairs={{0,6},{1,7},{2,0},{3,1},{4,2},{5,3},{6,4},{7,5},{32,34},{33,35},{3... | collective-permute-start | bytes 786440 | tf_op jit(solution)/shard_map/ppermute | solution.py:24
  68.2 17.9 %collective-permute-start.6 = (bf16[512,256]{1,0:T(8,128)(2,1)}, bf16[512,256]{1,0:T(8,128)(2,1)S(1)}, u32[]{:S(2)}, u32[]{:S(2)}) collective-permute-start(bf16[512,256]{1,0:T(8,128)(2,1)} %own.1), channel_id=1, source_target_pairs={{0,7},{1,0},{2,1},{3,2},{4,3},{5,4},{6,5},{7,6},{32,33},{33,34},{3... | collective-permute-start | bytes 786440 | tf_op jit(solution)/shard_map/ppermute | solution.py:24
  74.8 15.6 %collective-permute-start.2 = (bf16[512,256]{1,0:T(8,128)(2,1)S(1)}, bf16[512,256]{1,0:T(8,128)(2,1)S(1)}, u32[]{:S(2)}, u32[]{:S(2)}) collective-permute-start(bf16[512,256]{1,0:T(8,128)(2,1)S(1)} %collective-permute-done.1.refs_2_), channel_id=1, source_target_pairs={{0,1},{1,2},{2,3},{3,4},{4,5},{5,6},{6,7},{7,0},{32,39},{33,32},{3... | collective-permute-start | bytes 786440 | tf_op jit(solution)/shard_map/ppermute | solution.py:24
  81.0 11.1 %collective-permute-start.3 = (bf16[512,256]{1,0:T(8,128)(2,1)S(1)}, bf16[512,256]{1,0:T(8,128)(2,1)S(1)}, u32[]{:S(2)}, u32[]{:S(2)}) collective-permute-start(bf16[512,256]{1,0:T(8,128)(2,1)S(1)} %collective-permute-done.1.refs_2_), channel_id=1, source_target_pairs={{0,2},{1,3},{2,4},{3,5},{4,6},{5,7},{6,0},{7,1},{32,38},{33,39},{3... | collective-permute-start | bytes 786440 | tf_op jit(solution)/shard_map/ppermute | solution.py:24
  86.1 11.7 %collective-permute-start.5 = (bf16[512,256]{1,0:T(8,128)(2,1)S(1)}, bf16[512,256]{1,0:T(8,128)(2,1)S(1)}, u32[]{:S(2)}, u32[]{:S(2)}) collective-permute-start(bf16[512,256]{1,0:T(8,128)(2,1)S(1)} %collective-permute-done.4.refs_6_), channel_id=1, source_target_pairs={{0,7},{1,0},{2,1},{3,2},{4,3},{5,4},{6,5},{7,6},{32,33},{33,34},{3... | collective-permute-start | bytes 786440 | tf_op jit(solution)/shard_map/ppermute | solution.py:24
  89.4 1.0 copy-start
  101.1 23.2 %collective-permute-start.10 = (f16[512,256]{1,0:T(8,128)(2,1)S(1)}, f16[512,256]{1,0:T(8,128)(2,1)S(1)}, u32[]{:S(2)}, u32[]{:S(2)}) collective-permute-start(f16[512,256]{1,0:T(8,128)(2,1)S(1)} %convert_element_type.18), channel_id=1, source_target_pairs={{0,8},{8,16},{16,24},{24,0},{1,9},{9,17},{17,25},{25,1},{2,10},{10... | collective-permute-start | bytes 786440 | tf_op jit(solution)/shard_map/ppermute | solution.py:29
  108.8 15.6 %collective-permute-start.11 = (f16[512,256]{1,0:T(8,128)(2,1)S(1)}, f16[512,256]{1,0:T(8,128)(2,1)S(1)}, u32[]{:S(2)}, u32[]{:S(2)}) collective-permute-start(f16[512,256]{1,0:T(8,128)(2,1)S(1)} %convert_element_type.20), channel_id=1, source_target_pairs={{0,24},{8,0},{16,8},{24,16},{1,25},{9,1},{17,9},{25,17},{2,26},{10... | collective-permute-start | bytes 786440 | tf_op jit(solution)/shard_map/ppermute | solution.py:29
  116.7 26.8 %collective-permute-start.12 = (f16[512,256]{1,0:T(8,128)(2,1)S(1)}, f16[512,256]{1,0:T(8,128)(2,1)S(1)}, u32[]{:S(2)}, u32[]{:S(2)}) collective-permute-start(f16[512,256]{1,0:T(8,128)(2,1)S(1)} %convert_element_type.22), channel_id=1, source_target_pairs={{0,16},{8,24},{16,0},{24,8},{1,17},{9,25},{17,1},{25,9},{2,18},{10... | collective-permute-start | bytes 786440 | tf_op jit(solution)/shard_map/ppermute | solution.py:29

commit v9 on v8

--- a/solution.py
+++ b/solution.py
@@ -30,7 +30,7 @@
 
 
 def first_kernel(*refs):
-    a_refs, v_refs, (a_all, v_all, out) = refs[:8], refs[8:12], refs[12:]
+    a_refs, v_refs, (a_all, v_all, out_2, out_1) = refs[:8], refs[8:12], refs[12:]
     x, y, c = (lax.axis_index(name) for name in ("x", "ij", "c"))
     for place, ref in enumerate(a_refs):
         start = pl.multiple_of((y + (2 * c - 1) * place + 8) % 8 * 256, 256)
@@ -45,7 +45,8 @@
     def _():
         v_all[PAIRS - 6144 :, :] = jnp.zeros((8192 - PAIRS, 1024), jnp.bfloat16)
 
-    place_product(2, a_all, v_all, out)
+    place_product(2, a_all, v_all, out_2)
+    place_product(1, a_all, v_all, out_1)
 
 
 def place_product(ahead, a_all, v_all, out):
@@ -56,7 +57,7 @@
 
 
 def later_kernel(a_all, v_all, *outs):
-    for ahead, out in zip((1, 3, 0), outs):
+    for ahead, out in zip((3, 0), outs):
         place_product(ahead, a_all, v_all, out)
 
 
@@ -71,12 +72,13 @@
             jax.ShapeDtypeStruct((512, 2048), jnp.bfloat16),
             jax.ShapeDtypeStruct((2048, 1024), jnp.bfloat16),
             TERM,
+            TERM,
         ),
         in_specs=[VMEM] * 12,
-        out_specs=[VMEM] * 3,
+        out_specs=[VMEM] * 4,
         compiler_params=pltpu.CompilerParams(vmem_limit_bytes=16 << 20),
         cost_estimate=pl.CostEstimate(
-            flops=2 * 512 * 2048 * 256, bytes_accessed=12 << 20, transcendentals=0
+            flops=4 * 512 * 2048 * 256, bytes_accessed=12 << 20, transcendentals=0
         ),
     )(*pieces)
 
@@ -84,12 +86,12 @@
 def later_products(a_all, v_all):
     return pl.pallas_call(
         later_kernel,
-        out_shape=(TERM,) * 3,
+        out_shape=(TERM,) * 2,
         in_specs=[VMEM] * 2,
-        out_specs=[VMEM] * 3,
+        out_specs=[VMEM] * 2,
         compiler_params=pltpu.CompilerParams(vmem_limit_bytes=16 << 20),
         cost_estimate=pl.CostEstimate(
-            flops=6 * 512 * 2048 * 256, bytes_accessed=8 << 20, transcendentals=0
+            flops=4 * 512 * 2048 * 256, bytes_accessed=8 << 20, transcendentals=0
         ),
     )(a_all, v_all)
 
@@ -152,10 +154,10 @@
     v10 = lax.ppermute(v00, ("x", "c"), X_HOP)
     v01 = lax.ppermute(v00, "c", SWAP)
     v11 = lax.ppermute(v10, "c", SWAP)
-    a_all, v_all, term = first_product(*blocks, v00, v10, v01, v11)
+    a_all, v_all, term, term_1 = first_product(*blocks, v00, v10, v01, v11)
     total = [shifted(term, 2)]
-    term_1, term_3, own = later_products(a_all, v_all)
     total.append(shifted(term_1, 1))
+    term_3, own = later_products(a_all, v_all)
     total.append(shifted(term_3, 3))
     total = own + (total[1] + total[2]) + total[0]
     kl = lax.axis_index("kl")

time: 145 us -> 146 us (level)
  the two profiles are of different devices: /device:TPU:145 before, /device:TPU:1 now
where the time goes in v9:
time: 146 us
  starting transfers between devices  56.8 us (39%)
  waiting for transfers between devices  44.3 us (30%)
  blocking collectives  36.8 us (25%)
  Pallas kernels  4.61 us (3%)
  local copies, waits for them, and re-layouts  1.85 us (1%)
    all_to_all x1, blocking collectives, staged(): lax.all_to_all(copies(integrals), ('zl', 'x'), 0, 0, tiled=True, axis_ind...  36.8 us
    ppermute x7, starting transfers between devices, along_y(): return lax.ppermute(shard, ('c', 'ij'), pairs)  24.5 us
    ppermute x3, starting transfers between devices, shifted(): lax.ppermute(term.astype(jnp.float16), 'kl', pairs).astype(jnp.float32)  20.7 us
    ppermute x3, waiting for transfers between devices, shifted(): lax.ppermute(term.astype(jnp.float16), 'kl', pairs).astype(jnp.float32)  19.6 us
    ppermute x7, waiting for transfers between devices, along_y(): return lax.ppermute(shard, ('c', 'ij'), pairs)  14.6 us
    ppermute x1, waiting for transfers between devices, staged(): v10 = lax.ppermute(v00, ('x', 'c'), X_HOP)  10.1 us
    ppermute x1, starting transfers between devices, staged(): v11 = lax.ppermute(v10, 'c', SWAP)  5.87 us
    ppermute x1, starting transfers between devices, staged(): v01 = lax.ppermute(v00, 'c', SWAP)  3.82 us
  transfers between devices with their start and end apart: 13, of which 7 were waited for; matrix products, arithmetic and copies ran while one was open for 0% of the time, Pallas kernels for 0%

profile of v9, /device:TPU:1, one launch (start us, length us, event | category | flops | bytes accessed | tf_op | source)
XLA Modules:
  0.0 145.6 jit_solution(8647745804918603722)
XLA Ops:
  0.0 0.0 copy-start.1
  0.0 0.9 copy-done.1
  0.9 1.4 shard_map.29
  2.3 36.8 %all_to_all.5.refs_8_ = bf16[8,64,1024]{2,1,0:T(8,128)(2,1)S(1)} all-to-all(bf16[8,64,1024]{2,1,0:T(8,128)(2,1)S(1)} %shard_map.29), channel_id=1, replica_groups={{0,128,256,384,512,640,768,896},{64,192,320,448,576,704,832,960},{1,129..., dimensions={0} | all-to-all | bytes 2097152 | tf_op jit(solution)/shard_map/all_to_all | solution.py:141
  39.1 1.9 %collective-permute-start.7 = (bf16[8,64,1024]{2,1,0:T(8,128)(2,1)S(1)}, bf16[8,64,1024]{2,1,0:T(8,128)(2,1)S(1)}, u32[]{:S(2)}, u32[]{:S(2)}) collective-permute-start(bf16[8,64,1024]{2,1,0:T(8,128)(2,1)S(1)} %all_to_all.5.refs_8_), channel_id=1, source_target_pairs={{0,64},{64,128},{128,192},{192,256},{256,320},{320,384},{384,448},... | collective-permute-start | bytes 3145736 | tf_op jit(solution)/shard_map/ppermute | solution.py:154
  41.0 3.8 %collective-permute-start.8 = (bf16[8,64,1024]{2,1,0:T(8,128)(2,1)S(1)}, bf16[8,64,1024]{2,1,0:T(8,128)(2,1)S(1)}, u32[]{:S(2)}, u32[]{:S(2)}) collective-permute-start(bf16[8,64,1024]{2,1,0:T(8,128)(2,1)S(1)} %all_to_all.5.refs_8_), channel_id=1, source_target_pairs={{0,32},{32,0},{1,33},{33,1},{2,34},{34,2},{3,35},{35,3},{4,36},{36... | collective-permute-start | bytes 3145736 | tf_op jit(solution)/shard_map/ppermute | solution.py:155
  44.8 10.1 %collective-permute-done.7.refs_9_ = bf16[8,64,1024]{2,1,0:T(8,128)(2,1)S(1)} collective-permute-done((bf16[8,64,1024]{2,1,0:T(8,128)(2,1)S(1)}, bf16[8,64,1024]{2,1,0:T(8,128)(2,1)S(1)}, u32[]{:S(2)}, u32[]{:S(2)}) %collective-permute-start.7) | collective-permute-done | bytes 1048608 | tf_op jit(solution)/shard_map/ppermute | solution.py:154
  54.9 5.9 %collective-permute-start.9 = (bf16[8,64,1024]{2,1,0:T(8,128)(2,1)S(1)}, bf16[8,64,1024]{2,1,0:T(8,128)(2,1)S(1)}, u32[]{:S(2)}, u32[]{:S(2)}) collective-permute-start(bf16[8,64,1024]{2,1,0:T(8,128)(2,1)S(1)} %collective-permute-done.7.refs_9_), channel_id=1, source_target_pairs={{0,32},{32,0},{1,33},{33,1},{2,34},{34,2},{3,35},{35,3},{4,36},{36... | collective-permute-start | bytes 3145736 | tf_op jit(solution)/shard_map/ppermute | solution.py:156
  60.8 6.8 %collective-permute-start.1 = (bf16[512,256]{1,0:T(8,128)(2,1)}, bf16[512,256]{1,0:T(8,128)(2,1)S(1)}, u32[]{:S(2)}, u32[]{:S(2)}) collective-permute-start(bf16[512,256]{1,0:T(8,128)(2,1)} %own.1), channel_id=1, source_target_pairs={{0,2},{1,3},{2,4},{3,5},{4,6},{5,7},{6,0},{7,1},{32,38},{33,39},{3... | collective-permute-start | bytes 786440 | tf_op jit(solution)/shard_map/ppermute | solution.py:24
  67.6 2.9 %collective-permute-start = (bf16[512,256]{1,0:T(8,128)(2,1)}, bf16[512,256]{1,0:T(8,128)(2,1)S(1)}, u32[]{:S(2)}, u32[]{:S(2)}) collective-permute-start(bf16[512,256]{1,0:T(8,128)(2,1)} %own.1), channel_id=1, source_target_pairs={{0,1},{1,2},{2,3},{3,4},{4,5},{5,6},{6,7},{7,0},{32,39},{33,32},{3... | collective-permute-start | bytes 786440 | tf_op jit(solution)/shard_map/ppermute | solution.py:24
  70.4 2.6 %collective-permute-start.4 = (bf16[512,256]{1,0:T(8,128)(2,1)}, bf16[512,256]{1,0:T(8,128)(2,1)S(1)}, u32[]{:S(2)}, u32[]{:S(2)}) collective-permute-start(bf16[512,256]{1,0:T(8,128)(2,1)} %own.1), channel_id=1, source_target_pairs={{0,6},{1,7},{2,0},{3,1},{4,2},{5,3},{6,4},{7,5},{32,34},{33,35},{3... | collective-permute-start | bytes 786440 | tf_op jit(solution)/shard_map/ppermute | solution.py:24
  73.1 1.2 collective-permute-done.1.refs_2_
  74.2 1.9 %collective-permute-start.6 = (bf16[512,256]{1,0:T(8,128)(2,1)}, bf16[512,256]{1,0:T(8,128)(2,1)S(1)}, u32[]{:S(2)}, u32[]{:S(2)}) collective-permute-start(bf16[512,256]{1,0:T(8,128)(2,1)} %own.1), channel_id=1, source_target_pairs={{0,7},{1,0},{2,1},{3,2},{4,3},{5,4},{6,5},{7,6},{32,33},{33,34},{3... | collective-permute-start | bytes 786440 | tf_op jit(solution)/shard_map/ppermute | solution.py:24
  76.2 6.5 %collective-permute-done.given = bf16[512,256]{1,0:T(8,128)(2,1)S(1)} collective-permute-done((bf16[512,256]{1,0:T(8,128)(2,1)}, bf16[512,256]{1,0:T(8,128)(2,1)S(1)}, u32[]{:S(2)}, u32[]{:S(2)}) %collective-permute-start) | collective-permute-done | bytes 262176 | tf_op jit(solution)/shard_map/ppermute | solution.py:24
  82.7 5.3 %collective-permute-start.2 = (bf16[512,256]{1,0:T(8,128)(2,1)S(1)}, bf16[512,256]{1,0:T(8,128)(2,1)S(1)}, u32[]{:S(2)}, u32[]{:S(2)}) collective-permute-start(bf16[512,256]{1,0:T(8,128)(2,1)S(1)} %collective-permute-done.1.refs_2_), channel_id=1, source_target_pairs={{0,1},{1,2},{2,3},{3,4},{4,5},{5,6},{6,7},{7,0},{32,39},{33,32},{3... | collective-permute-start | bytes 786440 | tf_op jit(solution)/shard_map/ppermute | solution.py:24
  88.0 0.0 collective-permute-done.4.refs_6_
  88.0 1.9 %collective-permute-start.3 = (bf16[512,256]{1,0:T(8,128)(2,1)S(1)}, bf16[512,256]{1,0:T(8,128)(2,1)S(1)}, u32[]{:S(2)}, u32[]{:S(2)}) collective-permute-start(bf16[512,256]{1,0:T(8,128)(2,1)S(1)} %collective-permute-done.1.refs_2_), channel_id=1, source_target_pairs={{0,2},{1,3},{2,4},{3,5},{4,6},{5,7},{6,0},{7,1},{32,38},{33,39},{3... | collective-permute-start | bytes 786440 | tf_op jit(solution)/shard_map/ppermute | solution.py:24
  90.0 0.0 collective-permute-done.6.refs_7_
  90.0 3.1 %collective-permute-start.5 = (bf16[512,256]{1,0:T(8,128)(2,1)S(1)}, bf16[512,256]{1,0:T(8,128)(2,1)S(1)}, u32[]{:S(2)}, u32[]{:S(2)}) collective-permute-start(bf16[512,256]{1,0:T(8,128)(2,1)S(1)} %collective-permute-done.4.refs_6_), channel_id=1, source_target_pairs={{0,7},{1,0},{2,1},{3,2},{4,3},{5,4},{6,5},{7,6},{32,33},{33,34},{3... | collective-permute-start | bytes 786440 | tf_op jit(solution)/shard_map/ppermute | solution.py:24
  93.1 0.0 copy-start
  93.1 0.9 copy-done
  94.1 0.0 collective-permute-done.2.refs_3_
  94.1 5.4 %collective-permute-done.3.refs_4_ = bf16[512,256]{1,0:T(8,128)(2,1)S(1)} collective-permute-done((bf16[512,256]{1,0:T(8,128)(2,1)S(1)}, bf16[512,256]{1,0:T(8,128)(2,1)S(1)}, u32[]{:S(2)}, u32[]{:S(2)}) %collective-permute-start.3) | collective-permute-done | bytes 262176 | tf_op jit(solution)/shard_map/ppermute | solution.py:24
  99.4 1.6 %collective-permute-done.5.refs_5_ = bf16[512,256]{1,0:T(8,128)(2,1)S(1)} collective-permute-done((bf16[512,256]{1,0:T(8,128)(2,1)S(1)}, bf16[512,256]{1,0:T(8,128)(2,1)S(1)}, u32[]{:S(2)}, u32[]{:S(2)}) %collective-permute-start.5) | collective-permute-done | bytes 262176 | tf_op jit(solution)/shard_map/ppermute | solution.py:24
  101.0 0.0 collective-permute-done.8.refs_10_
  101.0 0.0 collective-permute-done.9.refs_11_
  101.0 1.9 %shard_map.30 = (bf16[512,2048]{1,0:T(8,128)(2,1)S(1)}, bf16[2048,1024]{1,0:T(8,128)(2,1)S(1)}, f32[512,256]{1,0:T(8,128)S(1)}, f32[512,256]{1,0:T(8,128)S(1)}) custom-call(bf16[512,256]{1,0:T(8,128)(2,1)S(1)} %get-tuple-element.13.refs_0_, bf16[512,256]{1,0:T(8,128)(2,1)S(1)} %get-tuple-element.14.refs_1_, ...), custom_call_target="tpu_custom_call" | custom-call | flops 1073741824 | bytes 12582912 | tf_op jit(solution)/shard_map/pallas_call | solution.py:69
  102.9 1.3 shard_map.31
  104.3 14.7 %collective-permute-start.11 = (f16[512,256]{1,0:T(8,128)(2,1)S(1)}, f16[512,256]{1,0:T(8,128)(2,1)S(1)}, u32[]{:S(2)}, u32[]{:S(2)}) collective-permute-start(f16[512,256]{1,0:T(8,128)(2,1)S(1)} %convert_element_type.20), channel_id=1, source_target_pairs={{0,24},{8,0},{16,8},{24,16},{1,25},{9,1},{17,9},{25,17},{2,26},{10... | collective-permute-start | bytes 786440 | tf_op jit(solution)/shard_map/ppermute | solution.py:29
  119.1 1.9 %collective-permute-start.10 = (f16[512,256]{1,0:T(8,128)(2,1)S(1)}, f16[512,256]{1,0:T(8,128)(2,1)S(1)}, u32[]{:S(2)}, u32[]{:S(2)}) collective-permute-start(f16[512,256]{1,0:T(8,128)(2,1)S(1)} %convert_element_type.18), channel_id=1, source_target_pairs={{0,8},{8,16},{16,24},{24,0},{1,9},{9,17},{17,25},{25,1},{2,10},{10... | collective-permute-start | bytes 786440 | tf_op jit(solution)/shard_map/ppermute | solution.py:29
  121.0 4.0 %collective-permute-start.12 = (f16[512,256]{1,0:T(8,128)(2,1)S(1)}, f16[512,256]{1,0:T(8,128)(2,1)S(1)}, u32[]{:S(2)}, u32[]{:S(2)}) collective-permute-start(f16[512,256]{1,0:T(8,128)(2,1)S(1)} %convert_element_type.22), channel_id=1, source_target_pairs={{0,16},{8,24},{16,0},{24,8},{1,17},{9,25},{17,1},{25,9},{2,18},{10... | collective-permute-start | bytes 786440 | tf_op jit(solution)/shard_map/ppermute | solution.py:29
  125.1 16.7 %collective-permute-done.11 = f16[512,256]{1,0:T(8,128)(2,1)S(1)} collective-permute-done((f16[512,256]{1,0:T(8,128)(2,1)S(1)}, f16[512,256]{1,0:T(8,128)(2,1)S(1)}, u32[]{:S(2)}, u32[]{:S(2)}) %collective-permute-start.11) | collective-permute-done | bytes 262176 | tf_op jit(solution)/shard_map/ppermute | solution.py:29
  141.8 0.0 collective-permute-done.10
  141.8 2.8 %collective-permute-done.12 = f16[512,256]{1,0:T(8,128)(2,1)S(1)} collective-permute-done((f16[512,256]{1,0:T(8,128)(2,1)S(1)}, f16[512,256]{1,0:T(8,128)(2,1)S(1)}, u32[]{:S(2)}, u32[]{:S(2)}) %collective-permute-start.12) | collective-permute-done | bytes 262176 | tf_op jit(solution)/shard_map/ppermute | solution.py:29
  144.6 0.9 multiply_select_fusion
  (5 shorter events, 0.1 us)
Async XLA Ops:
  0.0 0.9 copy-start.1
  39.1 15.8 %collective-permute-start.7 = (bf16[8,64,1024]{2,1,0:T(8,128)(2,1)S(1)}, bf16[8,64,1024]{2,1,0:T(8,128)(2,1)S(1)}, u32[]{:S(2)}, u32[]{:S(2)}) collective-permute-start(bf16[8,64,1024]{2,1,0:T(8,128)(2,1)S(1)} %all_to_all.5.refs_8_), channel_id=1, source_target_pairs={{0,64},{64,128},{128,192},{192,256},{256,320},{320,384},{384,448},... | collective-permute-start | bytes 3145736 | tf_op jit(solution)/shard_map/ppermute | solution.py:154
  41.0 60.0 %collective-permute-start.8 = (bf16[8,64,1024]{2,1,0:T(8,128)(2,1)S(1)}, bf16[8,64,1024]{2,1,0:T(8,128)(2,1)S(1)}, u32[]{:S(2)}, u32[]{:S(2)}) collective-permute-start(bf16[8,64,1024]{2,1,0:T(8,128)(2,1)S(1)} %all_to_all.5.refs_8_), channel_id=1, source_target_pairs={{0,32},{32,0},{1,33},{33,1},{2,34},{34,2},{3,35},{35,3},{4,36},{36... | collective-permute-start | bytes 3145736 | tf_op jit(solution)/shard_map/ppermute | solution.py:155
  54.9 46.1 %collective-permute-start.9 = (bf16[8,64,1024]{2,1,0:T(8,128)(2,1)S(1)}, bf16[8,64,1024]{2,1,0:T(8,128)(2,1)S(1)}, u32[]{:S(2)}, u32[]{:S(2)}) collective-permute-start(bf16[8,64,1024]{2,1,0:T(8,128)(2,1)S(1)} %collective-permute-done.7.refs_9_), channel_id=1, source_target_pairs={{0,32},{32,0},{1,33},{33,1},{2,34},{34,2},{3,35},{35,3},{4,36},{36... | collective-permute-start | bytes 3145736 | tf_op jit(solution)/shard_map/ppermute | solution.py:156
  60.8 13.5 %collective-permute-start.1 = (bf16[512,256]{1,0:T(8,128)(2,1)}, bf16[512,256]{1,0:T(8,128)(2,1)S(1)}, u32[]{:S(2)}, u32[]{:S(2)}) collective-permute-start(bf16[512,256]{1,0:T(8,128)(2,1)} %own.1), channel_id=1, source_target_pairs={{0,2},{1,3},{2,4},{3,5},{4,6},{5,7},{6,0},{7,1},{32,38},{33,39},{3... | collective-permute-start | bytes 786440 | tf_op jit(solution)/shard_map/ppermute | solution.py:24
  67.6 15.1 %collective-permute-start = (bf16[512,256]{1,0:T(8,128)(2,1)}, bf16[512,256]{1,0:T(8,128)(2,1)S(1)}, u32[]{:S(2)}, u32[]{:S(2)}) collective-permute-start(bf16[512,256]{1,0:T(8,128)(2,1)} %own.1), channel_id=1, source_target_pairs={{0,1},{1,2},{2,3},{3,4},{4,5},{5,6},{6,7},{7,0},{32,39},{33,32},{3... | collective-permute-start | bytes 786440 | tf_op jit(solution)/shard_map/ppermute | solution.py:24
  70.4 17.6 %collective-permute-start.4 = (bf16[512,256]{1,0:T(8,128)(2,1)}, bf16[512,256]{1,0:T(8,128)(2,1)S(1)}, u32[]{:S(2)}, u32[]{:S(2)}) collective-permute-start(bf16[512,256]{1,0:T(8,128)(2,1)} %own.1), channel_id=1, source_target_pairs={{0,6},{1,7},{2,0},{3,1},{4,2},{5,3},{6,4},{7,5},{32,34},{33,35},{3... | collective-permute-start | bytes 786440 | tf_op jit(solution)/shard_map/ppermute | solution.py:24
  74.2 15.7 %collective-permute-start.6 = (bf16[512,256]{1,0:T(8,128)(2,1)}, bf16[512,256]{1,0:T(8,128)(2,1)S(1)}, u32[]{:S(2)}, u32[]{:S(2)}) collective-permute-start(bf16[512,256]{1,0:T(8,128)(2,1)} %own.1), channel_id=1, source_target_pairs={{0,7},{1,0},{2,1},{3,2},{4,3},{5,4},{6,5},{7,6},{32,33},{33,34},{3... | collective-permute-start | bytes 786440 | tf_op jit(solution)/shard_map/ppermute | solution.py:24
  82.7 11.4 %collective-permute-start.2 = (bf16[512,256]{1,0:T(8,128)(2,1)S(1)}, bf16[512,256]{1,0:T(8,128)(2,1)S(1)}, u32[]{:S(2)}, u32[]{:S(2)}) collective-permute-start(bf16[512,256]{1,0:T(8,128)(2,1)S(1)} %collective-permute-done.1.refs_2_), channel_id=1, source_target_pairs={{0,1},{1,2},{2,3},{3,4},{4,5},{5,6},{6,7},{7,0},{32,39},{33,32},{3... | collective-permute-start | bytes 786440 | tf_op jit(solution)/shard_map/ppermute | solution.py:24
  88.0 11.4 %collective-permute-start.3 = (bf16[512,256]{1,0:T(8,128)(2,1)S(1)}, bf16[512,256]{1,0:T(8,128)(2,1)S(1)}, u32[]{:S(2)}, u32[]{:S(2)}) collective-permute-start(bf16[512,256]{1,0:T(8,128)(2,1)S(1)} %collective-permute-done.1.refs_2_), channel_id=1, source_target_pairs={{0,2},{1,3},{2,4},{3,5},{4,6},{5,7},{6,0},{7,1},{32,38},{33,39},{3... | collective-permute-start | bytes 786440 | tf_op jit(solution)/shard_map/ppermute | solution.py:24
  90.0 11.0 %collective-permute-start.5 = (bf16[512,256]{1,0:T(8,128)(2,1)S(1)}, bf16[512,256]{1,0:T(8,128)(2,1)S(1)}, u32[]{:S(2)}, u32[]{:S(2)}) collective-permute-start(bf16[512,256]{1,0:T(8,128)(2,1)S(1)} %collective-permute-done.4.refs_6_), channel_id=1, source_target_pairs={{0,7},{1,0},{2,1},{3,2},{4,3},{5,4},{6,5},{7,6},{32,33},{33,34},{3... | collective-permute-start | bytes 786440 | tf_op jit(solution)/shard_map/ppermute | solution.py:24
  93.1 1.0 copy-start
  104.3 37.5 %collective-permute-start.11 = (f16[512,256]{1,0:T(8,128)(2,1)S(1)}, f16[512,256]{1,0:T(8,128)(2,1)S(1)}, u32[]{:S(2)}, u32[]{:S(2)}) collective-permute-start(f16[512,256]{1,0:T(8,128)(2,1)S(1)} %convert_element_type.20), channel_id=1, source_target_pairs={{0,24},{8,0},{16,8},{24,16},{1,25},{9,1},{17,9},{25,17},{2,26},{10... | collective-permute-start | bytes 786440 | tf_op jit(solution)/shard_map/ppermute | solution.py:29
  119.1 22.7 %collective-permute-start.10 = (f16[512,256]{1,0:T(8,128)(2,1)S(1)}, f16[512,256]{1,0:T(8,128)(2,1)S(1)}, u32[]{:S(2)}, u32[]{:S(2)}) collective-permute-start(f16[512,256]{1,0:T(8,128)(2,1)S(1)} %convert_element_type.18), channel_id=1, source_target_pairs={{0,8},{8,16},{16,24},{24,0},{1,9},{9,17},{17,25},{25,1},{2,10},{10... | collective-permute-start | bytes 786440 | tf_op jit(solution)/shard_map/ppermute | solution.py:29
  121.0 23.6 %collective-permute-start.12 = (f16[512,256]{1,0:T(8,128)(2,1)S(1)}, f16[512,256]{1,0:T(8,128)(2,1)S(1)}, u32[]{:S(2)}, u32[]{:S(2)}) collective-permute-start(f16[512,256]{1,0:T(8,128)(2,1)S(1)} %convert_element_type.22), channel_id=1, source_target_pairs={{0,16},{8,24},{16,0},{24,8},{1,17},{9,25},{17,1},{25,9},{2,18},{10... | collective-permute-start | bytes 786440 | tf_op jit(solution)/shard_map/ppermute | solution.py:29
